TPU v7x, 8 devices: a whole 2x2x1 slice. The times are simulated.
8 devices in a mesh: data: 1 (over z), store: 2 (over y), model: 4 (over x, core).
Axes of the slice: x: 2, y: 2, z: 1, core: 2. Of those that a mesh axis runs over, the one named last changes fastest.
Arguments:
- queries: bfloat16 [128, 2560], P('data')
- w_head: bfloat16 [2560, 51200], P(None, 'model')
- store_keys: bfloat16 [131072, 2560], P(('store', 'model'))
- store_tok: int32 [131072], P(('store', 'model'))
- temperature: float32 [], replicated
- mix_weight: float32 [], replicated
Outputs:
- output: float32 [128, 51200], P(('data', 'store'), 'model')
All inputs are finite; a program needn't handle non-finite values.
Results may differ from a plain program's by a relative error of at most 0.001.
Values are sent between devices in bfloat16 or wider.
A program may use at most 1 GiB of HBM per device.

v0:
```python
import jax
import jax.numpy as jnp
from jax import lax
from jax.sharding import PartitionSpec as P


def solution(mesh):
    store_devs = mesh.shape["store"]
    model_devs = mesh.shape["model"]
    group_axes = ("store", "model")

    def local_step(queries, w_head, store_keys, store_tok, value_a11, mix_weight):
        vocab_loc = w_head.shape[1]
        rows_loc = queries.shape[0] // store_devs
        key_dots = lax.dot_general(store_keys, queries, (((1,), (1,)), ((), ())), preferred_element_type=jnp.float32)
        key_norms = jnp.sum(jnp.square(store_keys.astype(jnp.float32)), axis=1)
        scores = (2.0 * key_dots - key_norms[:, None]) / value_a11
        row_top = lax.pmax(jnp.max(scores, axis=0), group_axes)
        weights = jnp.exp(scores - row_top)
        row_total = lax.psum(jnp.sum(weights, axis=0), group_axes)
        histogram = jax.ops.segment_sum(weights, store_tok, num_segments=vocab_loc * model_devs)
        histogram = lax.psum_scatter(histogram, "model", scatter_dimension=0, tiled=True)
        histogram = lax.psum_scatter(histogram, "store", scatter_dimension=1, tiled=True)
        row_start = lax.axis_index("store") * rows_loc
        my_rows = lax.dynamic_slice_in_dim(queries, row_start, rows_loc, axis=0)
        my_total = lax.dynamic_slice_in_dim(row_total, row_start, rows_loc)
        logits = lax.dot_general(w_head, my_rows, (((0,), (1,)), ((), ())), preferred_element_type=jnp.float32)
        lm_top = lax.pmax(jnp.max(logits, axis=0), "model")
        lm_exp = jnp.exp(logits - lm_top)
        lm_total = lax.psum(jnp.sum(lm_exp, axis=0), "model")
        mixed = mix_weight * (histogram / my_total) + (1.0 - mix_weight) * (lm_exp / lm_total)
        return jnp.log(mixed).T

    return jax.shard_map(local_step, mesh=mesh, in_specs=(P("data", None), P(None, "model"), P(group_axes, None), P(group_axes), P(), P()), out_specs=P(("data", "store"), "model"), check_vma=False)
```

profile of v0, /device:TPU:0, one launch (start us, length us, event | category | flops | bytes accessed | tf_op | source)
XLA Modules:
  0.0 488.4 jit_solution(7140987401974197279)
XLA Ops:
  6.5 0.0 copy-start
  6.5 0.0 reduce-scatter.3.cloned.1.call-start
  6.5 26.4 %multiply_reduce_fusion = f32[16384]{0:T(1024)S(1)} fusion(bf16[16384,2560]{1,0:T(8,128)(2,1)} %param.8), kind=kLoop, calls=%fused_computation.1 | loop fusion | flops 125812736 | bytes 83951616 | tf_op jit(solution)/shard_map/reduce_sum | solution.py:16
  33.6 0.0 copy-done
  33.6 34.3 %fusion.12 = (f32[128]{0:T(128)S(1)}, f32[16384,128]{1,0:T(8,128)}) fusion(f32[]{:T(128)S(6)} %copy.8, f32[16384]{0:T(1024)S(1)} %multiply_reduce_fusion, bf16[16384,2560]{1,0:T(8,128)(2,1)} %param.8, bf16[128,2560]{1,0:T(8,128)(2,1)S(1)} %copy-done), kind=kOutput, calls=%fused_computation.18 | convolution fusion | flops 10745806848 | bytes 92996096 | tf_op jit(solution)/shard_map/dot_general | solution.py:15
  67.9 25.0 %pmax.14 = f32[128]{0:T(128)S(1)} all-reduce(f32[128]{0:T(128)S(1)} %get-tuple-element.5), channel_id=1, replica_groups=mesh['data'=1,'store'=2,'model'=4] {'store','model'}, use_global_device_ids=true, to_apply=%region_2.0 | all-reduce | flops 128 | bytes 1024 | tf_op jit(solution)/shard_map/pmax | solution.py:18
  92.9 99.2 %scatter_custom_fusion = f32[51200,128]{1,0:T(8,128)} fusion(s32[16384]{0:T(1024)} %param.9, f32[]{:T(128)} %constant.9.clone.1, f32[16384,128]{1,0:T(8,128)} %get-tuple-element.6, f32[128]{0:T(128)S(1)} %pmax.14), kind=kCustom, calls=%fused_computation.5 | custom fusion | flops 4194304 | bytes 34604032 | tf_op jit(solution)/shard_map/scatter-add | solution.py:21
  192.1 26.5 %copy.7 = f32[51200,128]{0,1:T(8,128)} copy(f32[51200,128]{1,0:T(8,128)} %scatter_custom_fusion) | data formatting | bytes 52428800 | tf_op jit(solution)/shard_map/scatter-add | solution.py:21
  218.6 0.0 reduce-scatter.3.cloned.1.call-update
  218.7 0.2 reduce-scatter.5.cloned.1.call-start
  218.9 176.1 %reduce-scatter.3.cloned.1.call-done = f32[12800,128]{0,1:T(8,128)} async-done(((f32[51200,128]{0,1:T(8,128)}), f32[12800,128]{0,1:T(8,128)}) %reduce-scatter.3.cloned.1.call-update) | async-done | bytes 6553616 | tf_op jit(solution)/shard_map/reduce_scatter | solution.py:22
  395.0 0.0 reduce-scatter.5.cloned.1.call-update
  395.7 4.6 fusion.4
  400.3 22.9 %psum.14 = f32[128]{0:T(128)S(1)} all-reduce(f32[128]{0:T(128)S(1)} %fusion.4), channel_id=1, replica_groups=mesh['data'=1,'store'=2,'model'=4] {'store','model'}, use_global_device_ids=true, to_apply=%region_7.0 | all-reduce | flops 128 | bytes 1024 | tf_op jit(solution)/shard_map/psum | solution.py:20
  423.2 0.1 dynamic_slice.6
  423.2 24.9 %fusion.13 = (f32[64]{0:T(128)S(1)}, f32[64,12800]{1,0:T(8,128)}) fusion(bf16[2560,12800]{1,0:T(8,128)(2,1)} %param.7, bf16[128,2560]{1,0:T(8,128)(2,1)S(1)} %copy-done, s32[]{:T(128)S(6)} %select_n.4), kind=kOutput, calls=%fused_computation.19 | convolution fusion | flops 4195123200 | bytes 69140736 | tf_op jit(solution)/shard_map/dot_general | solution.py:27
  448.1 7.0 %pmax.15 = f32[64]{0:T(128)S(1)} all-reduce(f32[64]{0:T(128)S(1)} %get-tuple-element.7), channel_id=1, replica_groups=mesh['data'=1,'store'=2,'model'=4] {'model'}, use_global_device_ids=true, to_apply=%region_9.0 | all-reduce | flops 64 | bytes 512 | tf_op jit(solution)/shard_map/pmax | solution.py:28
  455.2 2.5 fusion.8
  457.7 6.4 %psum.15 = f32[64]{0:T(128)S(1)} all-reduce(f32[64]{0:T(128)S(1)} %fusion.8), channel_id=1, replica_groups=mesh['data'=1,'store'=2,'model'=4] {'model'}, use_global_device_ids=true, to_apply=%region_11.0 | all-reduce | flops 64 | bytes 512 | tf_op jit(solution)/shard_map/psum | solution.py:30
  464.1 11.7 %reduce-scatter.5.cloned.1.call-done = f32[12800,64]{0,1:T(8,128)} async-done(((f32[12800,128]{0,1:T(8,128)}), f32[12800,64]{0,1:T(8,128)}) %reduce-scatter.5.cloned.1.call-update) | async-done | bytes 3276816 | tf_op jit(solution)/shard_map/reduce_scatter | solution.py:23
  475.8 5.8 %fusion.7 = f32[64,12800]{1,0:T(8,128)} fusion(f32[12800,64]{0,1:T(8,128)} %reduce-scatter.5.cloned.1.call-done, f32[64,12800]{1,0:T(8,128)} %get-tuple-element.8, f32[64]{0:T(128)S(1)} %psum.15, f32[64]{0:T(128)S(1)} %pmax.15, f32[]{:T(128)S(6)} %sub.32, f32[64]{0:T(128)S(1)} %dynamic_slice.6, f32[]{:T(128)S(6)} %copy.9), kind=kLoop, calls=%fused_computation.12 | loop fusion | flops 4915200 | bytes 9831176 | tf_op jit(solution)/shard_map/transpose | solution.py:32
Async XLA Ops:
  6.5 27.0 %copy-start = (bf16[128,2560]{1,0:T(8,128)(2,1)S(1)}, bf16[128,2560]{1,0:T(8,128)(2,1)}, u32[]{:S(2)}) copy-start(bf16[128,2560]{1,0:T(8,128)(2,1)} %param.6) | copy-start | bytes 1966084
  6.5 388.5 %reduce-scatter.3.cloned.1.call-start = ((), (), s32[]{:S(2)}) async-start(), calls=%async_computation.2 | async-start | bytes 32768000 | tf_op jit(solution)/shard_map/reduce_scatter | solution.py:22
  218.7 257.1 %reduce-scatter.5.cloned.1.call-start = ((), (), s32[]{:S(2)}) async-start(), calls=%async_computation.3 | async-start | bytes 9830400 | tf_op jit(solution)/shard_map/reduce_scatter | solution.py:23
Sparse Core Ops, SparseCore 0:
  218.8 176.1 reduce-scatter.2
  397.3 78.4 reduce-scatter.4
where the time goes:
time: 489 us; the launch traced here: 488 us
  waiting for transfers between devices  188 us (38%)
  other arithmetic  138 us (28%)
  blocking collectives  61.4 us (13%)
  matrix products  59.2 us (12%)
  local copies, waits for them, and re-layouts  26.6 us (5%)
  between operations  14.7 us (3%)
    reduce_scatter x1, waiting for transfers between devices, local_step(): lax.psum_scatter(histogram, 'model', scatter_dimension=0, tiled=True)  176 us
    scatter-add x1, other arithmetic, local_step(): jax.ops.segment_sum(weights, store_tok, num_segments=vocab_loc * model_devs)  99.2 us
    dot_general x1, matrix products, local_step(): lax.dot_general(store_keys, queries, (((1,), (1,)), ((), ())), preferred_...  34.3 us
    scatter-add x1, local copies, waits for them, and re-layouts, local_step(): jax.ops.segment_sum(weights, store_tok, num_segments=vocab_loc * model_devs)  26.5 us
    reduce_sum x1, other arithmetic, local_step(): key_norms = jnp.sum(jnp.square(store_keys.astype(jnp.float32)), axis=1)  26.4 us
    pmax x1, blocking collectives, local_step(): row_top = lax.pmax(jnp.max(scores, axis=0), group_axes)  25 us
    dot_general x1, matrix products, local_step(): lax.dot_general(w_head, my_rows, (((0,), (1,)), ((), ())), preferred_elem...  24.9 us
    psum x1, blocking collectives, local_step(): row_total = lax.psum(jnp.sum(weights, axis=0), group_axes)  22.9 us
  transfers between devices with their start and end apart: 2, of which 2 were waited for; matrix products, arithmetic and copies ran while one was open for 7% of the time, Pallas kernels for 0%

commit v1 on v0

v1 whole, which is shorter than its diff:
```python
import functools

import jax
import jax.numpy as jnp
from jax import lax
from jax.experimental import pallas as pl
from jax.experimental.pallas import tpu as pltpu
from jax.sharding import PartitionSpec as P

F32 = jnp.float32
ANY = pl.ANY
VMEM = pltpu.VMEM
SMEM = pltpu.SMEM
KEY_BLOCK = 512
BATCH_KEYS = 16
FLAG_KEYS = 64
PACK = 4
TOK_BLOCK = 128
STAGE_BLOCKS = 5
HEAD = 8


def lane_group(width):
    return lax.broadcasted_iota(jnp.int32, (1, 128), 1) // width


def pick(group, parts):
    out = parts[-1]
    for index in range(len(parts) - 2, -1, -1):
        out = jnp.where(group == index, parts[index], out)
    return out


def roll(value, shift):
    return pltpu.roll(value, shift % 128, 1)


def score_kernel(tau_ref, q_ref, k_ref, own_ref, first_ref, second_ref):
    tau = tau_ref[0]
    dots = jnp.dot(k_ref[...], q_ref[...], preferred_element_type=F32)
    step = 128
    norms = []
    for row in range(0, KEY_BLOCK, step):
        acc = jnp.zeros((step, 128), F32)
        for col in range(0, k_ref.shape[1], 128):
            part = k_ref[row : row + step, col : col + 128].astype(F32)
            acc += part * part
        norms.append(jnp.sum(acc, axis=1, keepdims=True))
    group = lane_group(32)
    scores = [(2.0 * dots[i * step : (i + 1) * step] - norms[i]) / tau for i in range(KEY_BLOCK // step)]
    for i in range(KEY_BLOCK // step // 2):
        own_ref[i * step : (i + 1) * step, :] = jnp.where(group < 2, scores[2 * i], roll(scores[2 * i + 1], 64))
    for i in range(KEY_BLOCK // step // 4):
        four = scores[4 * i : 4 * i + 4]
        rows = slice(i * step, (i + 1) * step)
        first_ref[rows, :] = pick(group, [roll(four[0], 64), roll(four[1], 96), four[2], roll(four[3], 32)])
        second_ref[rows, :] = pick(group, [roll(four[0], 32), roll(four[1], 64), roll(four[2], 96), four[3]])


def score_call(tau, q_cols, keys, start, count):
    width = keys.shape[1]
    base = start // KEY_BLOCK
    steps = count // KEY_BLOCK
    half, quarter = KEY_BLOCK // 2, KEY_BLOCK // 4
    return pl.pallas_call(
        score_kernel,
        grid=(steps,),
        out_shape=(
            jax.ShapeDtypeStruct((count // 2, 128), F32),
            jax.ShapeDtypeStruct((count // 4, 128), F32),
            jax.ShapeDtypeStruct((count // 4, 128), F32),
        ),
        in_specs=[
            pl.BlockSpec(memory_space=SMEM),
            pl.BlockSpec((width, 128), lambda i: (0, 0)),
            pl.BlockSpec((KEY_BLOCK, width), lambda i: (i + base, 0)),
        ],
        out_specs=(
            pl.BlockSpec((half, 128), lambda i: (i, 0)),
            pl.BlockSpec((quarter, 128), lambda i: (i, 0)),
            pl.BlockSpec((quarter, 128), lambda i: (i, 0)),
        ),
        compiler_params=pltpu.CompilerParams(vmem_limit_bytes=24 * 2**20),
        cost_estimate=pl.CostEstimate(flops=2 * count * width * 128, bytes_accessed=2 * count * width, transcendentals=0),
        name="scores",
    )(tau, q_cols, keys)


def histogram_kernel(hists, n_parts, n_prev, line_ref, flag_ref, pos_ref, group_ref, *refs):
    parts, refs = refs[:n_parts], refs[n_parts:]
    prevs, refs = refs[:n_prev], refs[n_prev:]
    outs, refs = refs[: 4 * hists], refs[4 * hists :]
    scores, weights, hist, heads, in_sem, prev_sem, out_sem, head_sem = refs
    rows = scores.shape[0]
    lines = hist.shape[1]
    piece = lines // 4
    width = 128 // PACK * hists
    group = lane_group(128 // PACK)
    x, core = pos_ref[0], pos_ref[1]

    def piece_at(k):
        x_of = x if k >= 2 else 1 - x
        core_of = core if k % 2 else 1 - core
        return pl.ds(pl.multiple_of((2 * x_of + core_of) * piece, 8), piece)

    copies = []
    start = 0
    for i, part in enumerate(parts):
        copies.append(pltpu.make_async_copy(part, scores.at[pl.ds(start, part.shape[0])], in_sem.at[i]))
        copies[-1].start()
        start += part.shape[0]
    fetches = []
    for k in range(n_prev):
        fetches.append(pltpu.make_async_copy(prevs[k].at[pl.ds(0, piece)], hist.at[0, piece_at(k)], prev_sem.at[k]))
    if n_prev:
        fetches.append(pltpu.make_async_copy(prevs[0].at[pl.ds(piece, HEAD)], heads.at[1], prev_sem.at[n_prev]))
    for fetch in fetches:
        fetch.start()

    if not n_prev:
        clear_rows = 512

        def clear(i, carry):
            at = pl.ds(pl.multiple_of(i * clear_rows, clear_rows), clear_rows)
            hist[:, at, :] = jnp.zeros((hists, clear_rows, 128), F32)
            return carry

        lax.fori_loop(0, lines // clear_rows, clear, 0)
    for copy in copies:
        copy.wait()

    chunk = 256

    def top_of(i, best):
        block = scores[pl.ds(pl.multiple_of(i * chunk, chunk), chunk), :]
        return jnp.maximum(best, jnp.max(block.reshape(chunk // 8, 8, 128), axis=0))

    best = lax.fori_loop(0, rows // chunk, top_of, jnp.full((8, 128), -jnp.inf, F32))
    top = jnp.max(best, axis=0, keepdims=True)
    span = width
    while span < 128:
        top = jnp.maximum(top, roll(top, span))
        span *= 2

    if n_prev:
        for fetch in fetches:
            fetch.wait()
        old_top, old_total = heads[1, 0:1, :], heads[1, 1:2, :]
        top = jnp.maximum(top, old_top)
        old_scale = jnp.exp(old_top - top)
        scale_rows = 512

        def rescale(i, carry):
            at = pl.ds(pl.multiple_of(i * scale_rows, scale_rows), scale_rows)
            hist[0, at, :] = hist[0, at, :] * old_scale
            return carry

        lax.fori_loop(0, lines // scale_rows, rescale, 0)

    spread_lane = lax.broadcasted_iota(jnp.int32, (128, 128), 1) // width
    spread_row = lax.broadcasted_iota(jnp.int32, (128, 128), 0)
    keys_per_row = PACK // hists
    together = 2

    def spread(i, total):
        for u in range(together):
            block = i * together + u
            select = (spread_row == block * keys_per_row + spread_lane).astype(F32).astype(jnp.bfloat16)
            target = jnp.dot(group_ref[...], select, preferred_element_type=F32).astype(jnp.int32)
            shift = (target - group) & (PACK - 1)
            value = jnp.exp(scores[pl.ds(pl.multiple_of(block * 128, 128), 128), :] - top)
            total = total + jnp.sum(value.reshape(16, 8, 128), axis=0)
            turned = [jnp.where(shift == d, value, 0.0) for d in range(PACK)]
            turned = [turned[0]] + [roll(turned[d], 32 * d) for d in range(1, PACK)]
            for source in range(PACK):
                line = pick(group, [turned[(g - source) % PACK] for g in range(PACK)])
                at = pl.multiple_of((block * keys_per_row + source // hists) * 128, 128)
                weights[source % hists, pl.ds(at, 128), :] = line
        return total

    total = lax.fori_loop(0, rows // 128 // together, spread, jnp.zeros((8, 128), F32))
    total = jnp.sum(total, axis=0, keepdims=True)
    span = width
    while span < 128:
        total = total + roll(total, span)
        span *= 2

    def add(key, count):
        at = [line_ref[key + k] for k in range(count)]
        sums = [
            hist[h, pl.ds(at[k], 1), :] + weights[h, pl.ds(key + k, 1), :] for k in range(count) for h in range(hists)
        ]
        for k in range(count):
            for h in range(hists):
                hist[h, pl.ds(at[k], 1), :] = sums[k * hists + h]

    def add_keys(i, carry):
        key = i * FLAG_KEYS

        def apart():
            for b in range(FLAG_KEYS // BATCH_KEYS):
                add(key + b * BATCH_KEYS, BATCH_KEYS)

        def one_by_one():
            def step(k, carry):
                add(key + k, 1)
                return carry

            lax.fori_loop(0, FLAG_KEYS, step, 0)

        lax.cond(flag_ref[i] == 0, apart, one_by_one)
        return carry

    lax.fori_loop(0, weights.shape[1] // FLAG_KEYS, add_keys, 0)

    row = lax.broadcasted_iota(jnp.int32, (HEAD, 128), 0)
    if n_prev:
        tops, totals = [top], [total + old_total * old_scale]
    else:
        even = (group % 2) == 0
        tops, totals = [[jnp.where(even, v, roll(v, 32)), jnp.where(even, roll(v, 32), v)] for v in (top, total)]
    sends = []
    for h in range(hists):
        heads[h] = jnp.where(row == 0, tops[h], jnp.where(row == 1, totals[h], 0.0))
        for k in range(4):
            out = outs[k * hists + h]
            sends.append(pltpu.make_async_copy(hist.at[h, piece_at(k)], out.at[pl.ds(0, piece)], out_sem.at[h, k]))
            sends.append(pltpu.make_async_copy(heads.at[h], out.at[pl.ds(piece, HEAD)], head_sem.at[h, k]))
    for send in sends:
        send.start()
    for send in sends:
        send.wait()


def histogram_call(line, flags, pos, group, parts, prevs, vocab):
    hists = 1 if prevs else 2
    rows = sum(part.shape[0] for part in parts)
    lines = vocab // PACK
    out = jax.ShapeDtypeStruct((lines // 4 + HEAD, 128), F32)
    return pl.pallas_call(
        functools.partial(histogram_kernel, hists, len(parts), len(prevs)),
        out_shape=(out,) * (4 * hists),
        in_specs=[pl.BlockSpec(memory_space=SMEM)] * 3
        + [pl.BlockSpec(memory_space=VMEM)]
        + [pl.BlockSpec(memory_space=ANY)] * (len(parts) + len(prevs)),
        out_specs=(pl.BlockSpec(memory_space=ANY),) * (4 * hists),
        scratch_shapes=[
            VMEM((rows, 128), F32),
            VMEM((hists, line.shape[0], 128), F32),
            VMEM((hists, lines, 128), F32),
            VMEM((2, HEAD, 128), F32),
            pltpu.SemaphoreType.DMA((len(parts),)),
            pltpu.SemaphoreType.DMA((5,)),
            pltpu.SemaphoreType.DMA((hists, 4)),
            pltpu.SemaphoreType.DMA((hists, 4)),
        ],
        compiler_params=pltpu.CompilerParams(vmem_limit_bytes=(20 + 18 * hists) * 2**20),
        cost_estimate=pl.CostEstimate(flops=4 * 10**9, bytes_accessed=2 * 10**7, transcendentals=0),
        name="histogram",
    )(line, flags, pos, group, *parts, *prevs)


def place_ids(tok, vocab):
    piece = vocab // 4
    block = PACK * TOK_BLOCK
    part, within = tok // piece, tok % piece
    line = part * (piece // PACK) + (within // block) * TOK_BLOCK + within % TOK_BLOCK
    group = (within % block) // TOK_BLOCK
    batch = line.reshape(-1, BATCH_KEYS)
    meet = jnp.zeros(batch.shape[0], jnp.bool_)
    for shift in range(1, BATCH_KEYS):
        meet = meet | jnp.any(batch[:, shift:] == batch[:, :-shift], axis=1)
    flags = jnp.any(meet.reshape(-1, FLAG_KEYS // BATCH_KEYS), axis=1).astype(jnp.int32)
    return line, flags, group.reshape(-1, 128).T.astype(jnp.bfloat16)


def merge_kernel(a_ref, b_ref, out_ref):
    lines = a_ref.shape[0] - HEAD
    a_top, b_top = a_ref[lines : lines + 1, :], b_ref[lines : lines + 1, :]
    top = jnp.maximum(a_top, b_top)
    a_scale, b_scale = jnp.exp(a_top - top), jnp.exp(b_top - top)
    total = a_ref[lines + 1 : lines + 2, :] * a_scale + b_ref[lines + 1 : lines + 2, :] * b_scale
    chunk = 128

    def add(i, carry):
        at = pl.ds(pl.multiple_of(i * chunk, chunk), chunk)
        out_ref[at, :] = a_ref[at, :] * a_scale + b_ref[at, :] * b_scale
        return carry

    lax.fori_loop(0, lines // chunk, add, 0)
    row = lax.broadcasted_iota(jnp.int32, (HEAD, 128), 0)
    out_ref[lines : lines + HEAD, :] = jnp.where(row == 0, top, jnp.where(row == 1, total, 0.0))


def merge_call(a, b):
    return pl.pallas_call(
        merge_kernel,
        out_shape=jax.ShapeDtypeStruct(a.shape, F32),
        compiler_params=pltpu.CompilerParams(vmem_limit_bytes=16 * 2**20),
        cost_estimate=pl.CostEstimate(flops=10**8, bytes_accessed=3 * a.size * 4, transcendentals=0),
        name="merge",
    )(a, b)


def head_kernel(q_ref, w_ref, after_ref, logits_ref, stat_ref, top_ref, sum_ref):
    del after_ref
    i = pl.program_id(0)

    @pl.when(i == 0)
    def _():
        top_ref[...] = jnp.full(top_ref.shape, -jnp.inf, F32)
        sum_ref[...] = jnp.zeros(sum_ref.shape, F32)

    logits = jnp.dot(q_ref[...], w_ref[...], preferred_element_type=F32)
    logits_ref[...] = logits
    old = top_ref[...]
    new = jnp.maximum(old, jnp.max(logits, axis=1, keepdims=True))
    part = jnp.sum(jnp.exp(logits - new[:, 0:1]), axis=1, keepdims=True)
    sum_ref[...] = sum_ref[...] * jnp.exp(old - new) + part
    top_ref[...] = new
    stat_ref[0] = top_ref[...]
    stat_ref[1] = sum_ref[...]


def head_call(rows, w_head, after):
    count, width = rows.shape
    cols = w_head.shape[1]
    block = cols // 10
    return pl.pallas_call(
        head_kernel,
        grid=(cols // block,),
        out_shape=(jax.ShapeDtypeStruct((count, cols), F32), jax.ShapeDtypeStruct((2, count, 128), F32)),
        in_specs=[
            pl.BlockSpec((count, width), lambda i: (0, 0)),
            pl.BlockSpec((width, block), lambda i: (0, i)),
            pl.BlockSpec(memory_space=ANY),
        ],
        out_specs=(pl.BlockSpec((count, block), lambda i: (0, i)), pl.BlockSpec((2, count, 128), lambda i: (0, 0, 0))),
        scratch_shapes=[VMEM((count, 128), F32), VMEM((count, 128), F32)],
        compiler_params=pltpu.CompilerParams(vmem_limit_bytes=24 * 2**20),
        cost_estimate=pl.CostEstimate(flops=2 * count * width * cols, bytes_accessed=2 * width * cols, transcendentals=0),
        name="head",
    )(rows, w_head, after)


def mix_kernel(n_prev, mix_ref, *refs):
    ins, heads, logits_ref, stat_ref = refs[:3], refs[3:6], refs[6], refs[7]
    out_ref = refs[8 + n_prev]
    mix = mix_ref[0]
    tops = [head[0:1, :] for head in heads]
    top = jnp.maximum(jnp.maximum(tops[0], tops[1]), tops[2])
    scales = [jnp.exp(value - top) for value in tops]
    total = sum(head[1:2, :] * scale for head, scale in zip(heads, scales))
    scales = [scale * mix / total for scale in scales]
    lm_top = stat_ref[0]
    lm_scale = (1.0 - mix) / stat_ref[1]
    for b in range(STAGE_BLOCKS):
        rows = slice(b * TOK_BLOCK, (b + 1) * TOK_BLOCK)
        value = ins[0][rows, :] * scales[0] + ins[1][rows, :] * scales[1] + ins[2][rows, :] * scales[2]
        turned = value.T
        for g in range(PACK):
            cols = slice((b * PACK + g) * TOK_BLOCK, (b * PACK + g + 1) * TOK_BLOCK)
            lm = jnp.exp(logits_ref[:, cols] - lm_top) * lm_scale
            out_ref[:, cols] = jnp.log(turned[g * 32 : (g + 1) * 32, :] + lm)


def mix_call(mix, pieces, logits, stat, index, prev):
    lines = pieces[0].shape[0] - HEAD
    block = STAGE_BLOCKS * TOK_BLOCK
    count, cols = logits.shape
    n_prev = 0 if prev is None else 1
    wide = block * PACK
    return pl.pallas_call(
        functools.partial(mix_kernel, n_prev),
        grid=(lines // block,),
        out_shape=jax.ShapeDtypeStruct((count, cols), F32),
        in_specs=[pl.BlockSpec(memory_space=SMEM)]
        + [pl.BlockSpec((block, 128), lambda i: (i, 0))] * 3
        + [pl.BlockSpec((HEAD, 128), lambda i: (lines // HEAD, 0))] * 3
        + [pl.BlockSpec((32, wide), lambda i: (index, i)), pl.BlockSpec((2, 32, 128), lambda i: (0, index, 0))]
        + [pl.BlockSpec(memory_space=ANY)] * n_prev,
        out_specs=pl.BlockSpec((32, wide), lambda i: (index, i)),
        input_output_aliases={9: 0} if n_prev else {},
        compiler_params=pltpu.CompilerParams(vmem_limit_bytes=16 * 2**20),
        cost_estimate=pl.CostEstimate(flops=10**8, bytes_accessed=8 * 10**6, transcendentals=0),
        name="mix",
    )(mix, *pieces, *pieces, logits, stat, *([prev] if n_prev else []))


CHUNKS = (2048, 4096, 4096, 6144)


def solution(mesh):
    store_devs = mesh.shape["store"]
    model_devs = mesh.shape["model"]
    assert store_devs == 2 and model_devs == 4
    group_axes = ("store", "model")
    across_y = [(0, 1), (1, 0)]
    across_core = [(0, 1), (1, 0), (2, 3), (3, 2)]
    across_x = [(0, 2), (2, 0), (1, 3), (3, 1)]

    def swap_y(value):
        return lax.ppermute(value, "store", across_y)

    def swap_core(value):
        return lax.ppermute(value, "model", across_core)

    def swap_x(value):
        return lax.ppermute(value, "model", across_x)

    def local_step(queries, w_head, store_keys, store_tok, temperature, mix_weight):
        vocab = w_head.shape[1] * model_devs
        rows = queries.shape[0] // store_devs
        y = lax.axis_index("store")
        m = lax.axis_index("model")
        pos = jnp.stack([m // 2, m % 2]).astype(jnp.int32)
        mine = lax.dynamic_slice_in_dim(queries, y * rows, rows, axis=0)
        theirs = lax.dynamic_slice_in_dim(queries, (1 - y) * rows, rows, axis=0)
        q_cols = jnp.concatenate([mine, theirs], axis=0).T
        tau = temperature.reshape(1)
        mix = mix_weight.reshape(1)

        their_tok = swap_y(store_tok)
        own, first, second = [], [], []
        start = 0
        for count in CHUNKS:
            a, b, c = score_call(tau, q_cols, store_keys, start, count)
            own.append(a)
            first.append(swap_y(b))
            second.append(c)
            start += count
        second = [swap_y(part) for part in second]

        own_line, own_flags, own_group = place_ids(store_tok, vocab)
        line, flags, group = place_ids(their_tok, vocab)
        kept = histogram_call(own_line, own_flags, pos, own_group, own, [], vocab)
        sums = []
        for index, parts in enumerate((first, second)):
            out = histogram_call(line, flags, pos, group, parts, kept[index::2], vocab)
            far = swap_x(merge_call(out[1], swap_core(out[0])))
            sums.append((out[3], swap_core(out[2]), far))
            last = out[3]
        logits, stat = head_call(mine, w_head, last)
        for swap in (swap_core, swap_x):
            other = swap(stat)
            top = jnp.maximum(stat[0], other[0])
            stat = jnp.stack([top, stat[1] * jnp.exp(stat[0] - top) + other[1] * jnp.exp(other[0] - top)])
        result = mix_call(mix, sums[0], logits, stat, 0, None)
        return mix_call(mix, sums[1], logits, stat, 1, result)

    return jax.shard_map(
        local_step,
        mesh=mesh,
        in_specs=(P("data", None), P(None, "model"), P(group_axes, None), P(group_axes), P(), P()),
        out_specs=P(("data", "store"), "model"),
        check_vma=False,
    )
```

time: 489 us -> 335 us (0.69)
  Pallas kernels: 0 us -> 232 us
  waiting for transfers between devices: 188 us -> 43.5 us
  other arithmetic: 138 us -> 14.4 us
  blocking collectives: 61.4 us -> 0 us
  matrix products: 59.2 us -> 0 us
  starting transfers between devices: 0.22 us -> 15.3 us
  between operations: 14.7 us -> 1.71 us
    pallas_call x0 -> x12, Pallas kernels: none -> 232 us  [the longest x3 138 us: histogram_call(): pl.pallas_call(functools.partial(histogram_kernel, hists, len(parts), len...]
    reduce_scatter x2 -> x0, waiting for transfers between devices: 188 us -> none  [the longest x1 176 us: local_step(): lax.psum_scatter(histogram, 'model', scatter_dimension=0, tiled=True)]
    scatter-add x1 -> x0, other arithmetic: 99.2 us -> none  [local_step(): jax.ops.segment_sum(weights, store_tok, num_segments=vocab_loc * model_devs)]
    dot_general x2 -> x0, matrix products: 59.2 us -> none  [the longest x1 34.3 us: local_step(): lax.dot_general(store_keys, queries, (((1,), (1,)), ((), ())), preferred_...]
    ppermute x0 -> x17, waiting for transfers between devices: none -> 43.5 us  [the longest x3 41.1 us: swap_x(): return lax.ppermute(value, 'model', across_x)]
    reduce_sum x3 -> x0, other arithmetic: 33.5 us -> none  [the longest x1 26.4 us: local_step(): key_norms = jnp.sum(jnp.square(store_keys.astype(jnp.float32)), axis=1)]
    pmax x2 -> x0, blocking collectives: 32 us -> none  [the longest x1 25 us: local_step(): row_top = lax.pmax(jnp.max(scores, axis=0), group_axes)]
    psum x2 -> x0, blocking collectives: 29.4 us -> none  [the longest x1 22.9 us: local_step(): row_total = lax.psum(jnp.sum(weights, axis=0), group_axes)]
  transfers between devices with their start and end apart: 2 -> 17, of which waited for: 2 -> 3; matrix products, arithmetic and copies ran while one was open for 7% -> 5% of each run, Pallas kernels for 0% -> 69%
where the time goes in v1:
time: 335 us; the launch traced here: 330 us
  Pallas kernels  232 us (69%)
  waiting for transfers between devices  43.5 us (13%)
  local copies, waits for them, and re-layouts  23.2 us (7%)
  starting transfers between devices  15.3 us (5%)
  other arithmetic  14.4 us (4%)
    pallas_call x3, Pallas kernels, histogram_call(): pl.pallas_call(functools.partial(histogram_kernel, hists, len(parts), len...  138 us
    pallas_call x4, Pallas kernels, score_call(): pl.pallas_call(score_kernel, grid=(steps,), out_shape=(jax.ShapeDtypeStru...  56.5 us
    ppermute x3, waiting for transfers between devices, swap_x(): return lax.ppermute(value, 'model', across_x)  41.1 us
    pallas_call x1, Pallas kernels, head_call(): pl.pallas_call(head_kernel, grid=(cols // block,), out_shape=(jax.ShapeDt...  24.9 us
    unnamed x54, local copies, waits for them, and re-layouts  19.9 us
    reduce_or x28, other arithmetic, place_ids(): meet = meet | jnp.any(batch[:, shift:] == batch[:, :-shift], axis=1)  11.7 us
    ppermute x9, starting transfers between devices, swap_y(): return lax.ppermute(value, 'store', across_y)  11.5 us
    pallas_call x2, Pallas kernels, mix_call(): pl.pallas_call(functools.partial(mix_kernel, n_prev), grid=(lines // bloc...  10 us
  transfers between devices with their start and end apart: 17, of which 3 were waited for; matrix products, arithmetic and copies ran while one was open for 5% of the time, Pallas kernels for 69%

profile of v1, /device:TPU:0, one launch (start us, length us, event | category | flops | bytes accessed | tf_op | source)
XLA Modules:
  0.0 330.5 jit_solution(9457518505890407303)
XLA Ops:
  0.0 3.4 %collective-permute-start = (s32[16384]{0:T(1024)}, s32[16384]{0:T(1024)S(1)}, u32[]{:S(2)}, u32[]{:S(2)}) collective-permute-start(s32[16384]{0:T(1024)} %param.9), channel_id=1, source_target_pairs={{0,4},{4,0},{1,5},{5,1},{2,6},{6,2},{3,7},{7,3}} | collective-permute-start | bytes 196616 | tf_op jit(solution)/shard_map/ppermute | solution.py:403
  3.4 1.1 constant_dynamic-slice_fusion.1
  4.6 0.7 copy-done.2
  6.3 19.7 %scores.7 = (f32[3072,128]{1,0:T(8,128)S(1)}, f32[1536,128]{1,0:T(8,128)S(1)}, f32[1536,128]{1,0:T(8,128)S(1)}) custom-call(f32[1]{0:T(128)} %bitcast.15.tau_ref, bf16[2560,128]{1,0:T(8,128)(2,1)S(1)} %copy.13.q_ref, bf16[16384,2560]{1,0:T(8,128)(2,1)} %k_ref.7), custom_call_target="tpu_custom_call" | custom-call | flops 4026531840 | bytes 31457280 | tf_op jit(solution)/shard_map/scores/pallas_call | solution.py:65
  26.0 1.2 copy-done.4
  27.2 14.3 %scores.5 = (f32[2048,128]{1,0:T(8,128)S(1)}, f32[1024,128]{1,0:T(8,128)}, f32[1024,128]{1,0:T(8,128)S(1)}) custom-call(f32[1]{0:T(128)} %bitcast.13.tau_ref, bf16[2560,128]{1,0:T(8,128)(2,1)S(1)} %copy.13.q_ref, bf16[16384,2560]{1,0:T(8,128)(2,1)} %k_ref.7), custom_call_target="tpu_custom_call" | custom-call | flops 2684354560 | bytes 20971520 | tf_op jit(solution)/shard_map/scores/pallas_call | solution.py:65
  41.4 1.0 copy-done.5
  42.5 2.0 collective-permute-start.11
  44.5 14.4 %scores.6 = (f32[2048,128]{1,0:T(8,128)S(1)}, f32[1024,128]{1,0:T(8,128)}, f32[1024,128]{1,0:T(8,128)}) custom-call(f32[1]{0:T(128)} %bitcast.14.tau_ref, bf16[2560,128]{1,0:T(8,128)(2,1)S(1)} %copy.13.q_ref, bf16[16384,2560]{1,0:T(8,128)(2,1)} %k_ref.7), custom_call_target="tpu_custom_call" | custom-call | flops 2684354560 | bytes 20971520 | tf_op jit(solution)/shard_map/scores/pallas_call | solution.py:65
  58.9 1.0 copy-done.6
  60.1 8.1 %scores.4 = (f32[1024,128]{1,0:T(8,128)S(1)}, f32[512,128]{1,0:T(8,128)}, f32[512,128]{1,0:T(8,128)}) custom-call(f32[1]{0:T(128)} %bitcast.12.tau_ref, bf16[2560,128]{1,0:T(8,128)(2,1)S(1)} %copy.13.q_ref, bf16[16384,2560]{1,0:T(8,128)(2,1)} %k_ref.7), custom_call_target="tpu_custom_call" | custom-call | flops 1342177280 | bytes 10485760 | tf_op jit(solution)/shard_map/scores/pallas_call | solution.py:65
  68.2 0.8 copy-done.11
  69.0 1.8 collective-permute-start.10
  77.3 0.5 convert_element_type.24.flag_ref
  77.8 0.7 copy.17
  78.6 0.6 pad_add_fusion.pos_ref
  79.2 57.6 %histogram.3 = (f32[3208,128]{1,0:T(8,128)}, f32[3208,128]{1,0:T(8,128)}, f32[3208,128]{1,0:T(8,128)}, f32[3208,128]{1,0:T(8,128)}, f32[3208,128]{1,0:T(8,128)},...) custom-call(s32[16384]{0:T(1024)} %copy-done.25, s32[256]{0:T(256)} %convert_element_type.24.flag_ref, ...), custom_call_target="tpu_custom_call" | custom-call | flops 4000000000 | bytes 20000000 | tf_op jit(solution)/shard_map/histogram/pallas_call | solution.py:240
  136.8 0.5 collective-permute-start.4
  141.9 1.7 fusion.7
  143.9 0.4 fusion.9
  144.3 1.5 collective-permute-start.2
  145.9 0.5 collective-permute-start.3
  147.3 1.5 collective-permute-start.1
  148.9 0.9 copy-done.7
  149.8 1.1 copy-done.8
  150.9 0.9 copy-done.13
  151.9 1.4 copy-done.19
  153.3 1.4 copy-done.20
  154.7 1.4 copy-done.21
  156.2 1.4 copy-done.22
  157.6 40.0 %histogram.5 = (f32[3208,128]{1,0:T(8,128)S(1)}, f32[3208,128]{1,0:T(8,128)S(1)}, f32[3208,128]{1,0:T(8,128)}, f32[3208,128]{1,0:T(8,128)S(1)}) custom-call(s32[16384]{0:T(1024)S(1)} %get-tuple-element.74.line_ref, s32[256]{0:T(256)S(1)} %convert_element_type.20.flag_ref, s32[2]{0:T(128)S(1)} %copy-done.14, bf16[128,128]{1,0:T(8,128)(2,1)S(1)} %bitcast.18, ...), custom_call_target="tpu_custom_call" | custom-call | flops 4000000000 | bytes 20000000 | tf_op jit(solution)/shard_map/histogram/pallas_call | solution.py:240
  197.7 1.4 copy-done.17
  199.2 1.4 copy-done.18
  200.6 40.3 %histogram.4 = (f32[3208,128]{1,0:T(8,128)S(1)}, f32[3208,128]{1,0:T(8,128)S(1)}, f32[3208,128]{1,0:T(8,128)}, f32[3208,128]{1,0:T(8,128)S(1)}) custom-call(s32[16384]{0:T(1024)S(1)} %get-tuple-element.74.line_ref, s32[256]{0:T(256)S(1)} %convert_element_type.20.flag_ref, s32[2]{0:T(128)S(1)} %copy-done.14, bf16[128,128]{1,0:T(8,128)(2,1)S(1)} %bitcast.19, ...), custom_call_target="tpu_custom_call" | custom-call | flops 4000000000 | bytes 20000000 | tf_op jit(solution)/shard_map/histogram/pallas_call | solution.py:240
  240.9 1.1 collective-permute-start.6
  242.1 1.5 merge.3
  243.6 0.5 collective-permute-start.5
  244.1 1.1 collective-permute-done.6.b_ref
  245.2 1.6 merge.2
  246.7 0.6 collective-permute-start.7
  247.4 24.9 %head.1 = (f32[64,12800]{1,0:T(8,128)S(1)}, f32[2,64,128]{2,1,0:T(8,128)S(1)}) custom-call(bf16[64,2560]{1,0:T(8,128)(2,1)S(1)} %copy-done.3, bf16[2560,12800]{1,0:T(8,128)(2,1)} %w_ref.1, f32[3208,128]{1,0:T(8,128)S(1)} %get-tuple-element.47.after_ref.refs_0_.refs_3_), custom_call_target="tpu_custom_call" | custom-call | flops 4194304000 | bytes 65536000 | tf_op jit(solution)/shard_map/head/pallas_call | solution.py:329
  272.2 1.7 copy-done
  274.0 1.2 collective-permute-done.8
  275.2 1.4 collective-permute-start.9
  277.3 41.1 %collective-permute-done.9 = f32[2,64,128]{2,1,0:T(8,128)S(1)} collective-permute-done((f32[2,64,128]{2,1,0:T(8,128)S(1)}, f32[2,64,128]{2,1,0:T(8,128)S(1)}, u32[]{:S(2)}, u32[]{:S(2)}) %collective-permute-start.9) | collective-permute-done | bytes 65568 | tf_op jit(solution)/shard_map/ppermute | solution.py:409
  318.5 1.9 copy-done.1
  320.4 5.0 %mix.2.refs_8_ = f32[64,12800]{1,0:T(8,128)} custom-call(f32[1]{0:T(128)} %bitcast.16.mix_ref, f32[3208,128]{1,0:T(8,128)S(1)} %get-tuple-element.61.refs_0_.refs_3_, f32[3208,128]{1,0:T(8,128)} %collective-permute-done.14.refs_1_.refs_4_, f32[3208,128]{1,0:T(8,128)} %collective-permute-done.16.refs_2_.refs_5_, ...), custom_call_target="tpu_custom_call" | custom-call | flops 100000000 | bytes 8000000 | tf_op jit(solution)/shard_map/mix/pallas_call | solution.py:373
  325.4 5.0 %mix.3 = f32[64,12800]{1,0:T(8,128)} custom-call(f32[1]{0:T(128)} %bitcast.17.mix_ref, f32[3208,128]{1,0:T(8,128)S(1)} %get-tuple-element.47.after_ref.refs_0_.refs_3_, f32[3208,128]{1,0:T(8,128)} %collective-permute-done.5.refs_1_.refs_4_, f32[3208,128]{1,0:T(8,128)} %collective-permute-done.7.refs_2_.refs_5_, ...), custom_call_target="tpu_custom_call", output_to_operand_aliasing={{}: (9, {})} | custom-call | flops 100000000 | bytes 8000000 | tf_op jit(solution)/shard_map/mix/pallas_call | solution.py:373
  (106 shorter events, 13.1 us)
Async XLA Ops:
  0.0 136.8 %collective-permute-start = (s32[16384]{0:T(1024)}, s32[16384]{0:T(1024)S(1)}, u32[]{:S(2)}, u32[]{:S(2)}) collective-permute-start(s32[16384]{0:T(1024)} %param.9), channel_id=1, source_target_pairs={{0,4},{4,0},{1,5},{5,1},{2,6},{6,2},{3,7},{7,3}} | collective-permute-start | bytes 196616 | tf_op jit(solution)/shard_map/ppermute | solution.py:403
  4.5 0.7 copy-start.2
  26.0 1.2 copy-start.4
  27.2 121.7 %collective-permute-start.13 = (f32[1536,128]{1,0:T(8,128)S(1)}, f32[1536,128]{1,0:T(8,128)S(1)}, u32[]{:S(2)}, u32[]{:S(2)}) collective-permute-start(f32[1536,128]{1,0:T(8,128)S(1)} %get-tuple-element.56), channel_id=1, source_target_pairs={{0,4},{4,0},{1,5},{5,1},{2,6},{6,2},{3,7},{7,3}} | collective-permute-start | bytes 2359304 | tf_op jit(solution)/shard_map/ppermute | solution.py:403
  41.4 1.0 copy-start.5
  42.4 16.4 %copy-start.9 = (f32[1024,128]{1,0:T(8,128)}, f32[1024,128]{1,0:T(8,128)S(1)}, u32[]{:S(2)}) copy-start(f32[1024,128]{1,0:T(8,128)S(1)} %get-tuple-element.36) | copy-start | bytes 1572868
  42.5 103.4 %collective-permute-start.11 = (f32[1024,128]{1,0:T(8,128)}, f32[1024,128]{1,0:T(8,128)}, u32[]{:S(2)}, u32[]{:S(2)}) collective-permute-start(f32[1024,128]{1,0:T(8,128)} %get-tuple-element.54), channel_id=1, source_target_pairs={{0,4},{4,0},{1,5},{5,1},{2,6},{6,2},{3,7},{7,3}} | collective-permute-start | bytes 1572872 | tf_op jit(solution)/shard_map/ppermute | solution.py:403
  58.9 1.0 copy-start.6
  59.9 87.5 %collective-permute-start.12 = (f32[1024,128]{1,0:T(8,128)}, f32[1024,128]{1,0:T(8,128)}, u32[]{:S(2)}, u32[]{:S(2)}) collective-permute-start(f32[1024,128]{1,0:T(8,128)} %get-tuple-element.55), channel_id=1, source_target_pairs={{0,4},{4,0},{1,5},{5,1},{2,6},{6,2},{3,7},{7,3}} | collective-permute-start | bytes 1572872 | tf_op jit(solution)/shard_map/ppermute | solution.py:403
  60.1 10.8 %copy-start.26 = (s32[16384]{0:T(1024)S(1)}, s32[16384]{0:T(1024)}, u32[]{:S(2)}) copy-start(s32[16384]{0:T(1024)} %param.9) | copy-start | bytes 196612
  68.2 0.8 copy-start.11
  69.0 75.3 %collective-permute-start.10 = (f32[512,128]{1,0:T(8,128)}, f32[512,128]{1,0:T(8,128)S(1)}, u32[]{:S(2)}, u32[]{:S(2)}) collective-permute-start(f32[512,128]{1,0:T(8,128)} %get-tuple-element.53), channel_id=1, source_target_pairs={{0,4},{4,0},{1,5},{5,1},{2,6},{6,2},{3,7},{7,3}} | collective-permute-start | bytes 786440 | tf_op jit(solution)/shard_map/ppermute | solution.py:403
  71.0 1.3 copy-start.25
  136.8 60.9 %collective-permute-start.4 = (f32[1536,128]{1,0:T(8,128)S(1)}, f32[1536,128]{1,0:T(8,128)}, u32[]{:S(2)}, u32[]{:S(2)}) collective-permute-start(f32[1536,128]{1,0:T(8,128)S(1)} %get-tuple-element.38), channel_id=1, source_target_pairs={{0,4},{4,0},{1,5},{5,1},{2,6},{6,2},{3,7},{7,3}} | collective-permute-start | bytes 2359304 | tf_op jit(solution)/shard_map/ppermute | solution.py:403
  137.7 3.8 %copy-start.23 = (s32[1024,16]{1,0:T(8,128)}, s32[1024,16]{1,0:T(8,128)S(1)}, u32[]{:S(2)}) copy-start(s32[1024,16]{1,0:T(8,128)S(1)} %reshape.171) | copy-start | bytes 196612
  141.9 1.7 copy-start.24
  141.9 2.5 copy-start.10
  143.5 6.2 %copy-start.14 = (s32[2]{0:T(128)S(1)}, s32[2]{0:T(128)}, u32[]{:S(2)}) copy-start(s32[2]{0:T(128)} %pad_add_fusion.pos_ref) | copy-start | bytes 28
  144.3 5.5 %copy-start.12 = (f32[512,128]{1,0:T(8,128)}, f32[512,128]{1,0:T(8,128)S(1)}, u32[]{:S(2)}) copy-start(f32[512,128]{1,0:T(8,128)S(1)} %collective-permute-done.10.refs_0_) | copy-start | bytes 786436
  144.3 53.3 %collective-permute-start.2 = (f32[1024,128]{1,0:T(8,128)S(1)}, f32[1024,128]{1,0:T(8,128)}, u32[]{:S(2)}, u32[]{:S(2)}) collective-permute-start(f32[1024,128]{1,0:T(8,128)S(1)} %copy-done.10), channel_id=1, source_target_pairs={{0,4},{4,0},{1,5},{5,1},{2,6},{6,2},{3,7},{7,3}} | collective-permute-start | bytes 1572872 | tf_op jit(solution)/shard_map/ppermute | solution.py:403
  145.9 51.8 %collective-permute-start.3 = (f32[1024,128]{1,0:T(8,128)}, f32[1024,128]{1,0:T(8,128)}, u32[]{:S(2)}, u32[]{:S(2)}) collective-permute-start(f32[1024,128]{1,0:T(8,128)} %get-tuple-element.37), channel_id=1, source_target_pairs={{0,4},{4,0},{1,5},{5,1},{2,6},{6,2},{3,7},{7,3}} | collective-permute-start | bytes 1572872 | tf_op jit(solution)/shard_map/ppermute | solution.py:403
  147.3 50.3 %collective-permute-start.1 = (f32[512,128]{1,0:T(8,128)}, f32[512,128]{1,0:T(8,128)S(1)}, u32[]{:S(2)}, u32[]{:S(2)}) collective-permute-start(f32[512,128]{1,0:T(8,128)} %get-tuple-element.35), channel_id=1, source_target_pairs={{0,4},{4,0},{1,5},{5,1},{2,6},{6,2},{3,7},{7,3}} | collective-permute-start | bytes 786440 | tf_op jit(solution)/shard_map/ppermute | solution.py:403
  148.9 0.9 copy-start.7
  149.8 1.1 copy-start.8
  150.9 0.9 copy-start.13
  151.9 1.4 copy-start.19
  153.3 1.4 copy-start.20
  154.7 1.4 copy-start.21
  156.2 1.4 copy-start.22
  157.6 40.1 %copy-start.15 = (f32[3208,128]{1,0:T(8,128)S(1)}, f32[3208,128]{1,0:T(8,128)}, u32[]{:S(2)}) copy-start(f32[3208,128]{1,0:T(8,128)} %get-tuple-element.43.refs_4_) | copy-start | bytes 4927492
  157.6 40.1 %copy-start.16 = (f32[3208,128]{1,0:T(8,128)S(1)}, f32[3208,128]{1,0:T(8,128)}, u32[]{:S(2)}) copy-start(f32[3208,128]{1,0:T(8,128)} %get-tuple-element.44.refs_5_) | copy-start | bytes 4927492
  197.6 44.4 %collective-permute-start.15 = (f32[3208,128]{1,0:T(8,128)S(1)}, f32[3208,128]{1,0:T(8,128)S(1)}, u32[]{:S(2)}, u32[]{:S(2)}) collective-permute-start(f32[3208,128]{1,0:T(8,128)S(1)} %get-tuple-element.64), channel_id=1, source_target_pairs={{0,1},{1,0},{2,3},{3,2},{4,5},{5,4},{6,7},{7,6}} | collective-permute-start | bytes 4927496 | tf_op jit(solution)/shard_map/ppermute | solution.py:406
  197.7 1.4 copy-start.17
  199.2 1.4 copy-start.18
  240.9 4.3 %collective-permute-start.6 = (f32[3208,128]{1,0:T(8,128)S(1)}, f32[3208,128]{1,0:T(8,128)S(1)}, u32[]{:S(2)}, u32[]{:S(2)}) collective-permute-start(f32[3208,128]{1,0:T(8,128)S(1)} %get-tuple-element.50), channel_id=1, source_target_pairs={{0,1},{1,0},{2,3},{3,2},{4,5},{5,4},{6,7},{7,6}} | collective-permute-start | bytes 4927496 | tf_op jit(solution)/shard_map/ppermute | solution.py:406
  242.0 76.4 %collective-permute-start.14 = (f32[3208,128]{1,0:T(8,128)}, f32[3208,128]{1,0:T(8,128)}, u32[]{:S(2)}, u32[]{:S(2)}) collective-permute-start(f32[3208,128]{1,0:T(8,128)} %get-tuple-element.62), channel_id=1, source_target_pairs={{0,1},{1,0},{2,3},{3,2},{4,5},{5,4},{6,7},{7,6}} | collective-permute-start | bytes 4927496 | tf_op jit(solution)/shard_map/ppermute | solution.py:406
  243.6 74.9 %collective-permute-start.16 = (f32[3208,128]{1,0:T(8,128)}, f32[3208,128]{1,0:T(8,128)}, u32[]{:S(2)}, u32[]{:S(2)}) collective-permute-start(f32[3208,128]{1,0:T(8,128)} %merge.3), channel_id=1, source_target_pairs={{0,2},{2,0},{1,3},{3,1},{4,6},{6,4},{5,7},{7,5}} | collective-permute-start | bytes 4927496 | tf_op jit(solution)/shard_map/ppermute | solution.py:409
  243.6 81.9 %collective-permute-start.5 = (f32[3208,128]{1,0:T(8,128)}, f32[3208,128]{1,0:T(8,128)}, u32[]{:S(2)}, u32[]{:S(2)}) collective-permute-start(f32[3208,128]{1,0:T(8,128)} %get-tuple-element.48), channel_id=1, source_target_pairs={{0,1},{1,0},{2,3},{3,2},{4,5},{5,4},{6,7},{7,6}} | collective-permute-start | bytes 4927496 | tf_op jit(solution)/shard_map/ppermute | solution.py:406
  245.2 2.2 copy-start.3
  246.7 78.7 %collective-permute-start.7 = (f32[3208,128]{1,0:T(8,128)}, f32[3208,128]{1,0:T(8,128)}, u32[]{:S(2)}, u32[]{:S(2)}) collective-permute-start(f32[3208,128]{1,0:T(8,128)} %merge.2), channel_id=1, source_target_pairs={{0,2},{2,0},{1,3},{3,1},{4,6},{6,4},{5,7},{7,5}} | collective-permute-start | bytes 4927496 | tf_op jit(solution)/shard_map/ppermute | solution.py:409
  272.2 1.7 copy-start
  273.9 1.3 collective-permute-start.8
  275.2 43.2 %collective-permute-start.9 = (f32[2,64,128]{2,1,0:T(8,128)S(1)}, f32[2,64,128]{2,1,0:T(8,128)S(1)}, u32[]{:S(2)}, u32[]{:S(2)}) collective-permute-start(f32[2,64,128]{2,1,0:T(8,128)S(1)} %pad_maximum_fusion), channel_id=1, source_target_pairs={{0,2},{2,0},{1,3},{3,1},{4,6},{6,4},{5,7},{7,5}} | collective-permute-start | bytes 196616 | tf_op jit(solution)/shard_map/ppermute | solution.py:409
  318.5 1.9 copy-start.1

commit v2 on v1

v2 whole, which is shorter than its diff:
```python
import functools

import jax
import jax.numpy as jnp
from jax import lax
from jax.experimental import pallas as pl
from jax.experimental.pallas import tpu as pltpu
from jax.sharding import PartitionSpec as P


F32 = jnp.float32
ANY = pl.ANY
VMEM = pltpu.VMEM
SMEM = pltpu.SMEM
KEY_BLOCK = 1024
VMEM_BYTES = 63 * 2**20
BATCH_KEYS = 8
FLAG_KEYS = 128
PACK = 4
TOK_BLOCK = 128
ORDERS = ((0, 2, 1, 3), (3, 0, 2, 1))
STAGE_BLOCKS = 5
HEAD = 8


def lane_group(width):
    return lax.broadcasted_iota(jnp.int32, (1, 128), 1) // width


def pick(group, parts):
    out = parts[-1]
    for index in range(len(parts) - 2, -1, -1):
        out = jnp.where(group == index, parts[index], out)
    return out


def roll(value, shift):
    return pltpu.roll(value, shift % 128, 1)


def score_kernel(tau_ref, q_ref, k_ref, own_ref, first_ref, second_ref):
    tau = tau_ref[0]
    dots = jnp.dot(k_ref[...], q_ref[...], preferred_element_type=F32)
    step = 128
    norms = []
    for row in range(0, KEY_BLOCK, step):
        acc = jnp.zeros((step, 128), F32)
        for col in range(0, k_ref.shape[1], 128):
            part = k_ref[row : row + step, col : col + 128].astype(F32)
            acc += part * part
        norms.append(jnp.sum(acc, axis=1, keepdims=True))
    group = lane_group(32)
    scores = [(2.0 * dots[i * step : (i + 1) * step] - norms[i]) / tau for i in range(KEY_BLOCK // step)]
    for i in range(KEY_BLOCK // step // 2):
        own_ref[i * step : (i + 1) * step, :] = jnp.where(group < 2, scores[2 * i], roll(scores[2 * i + 1], 64))
    for i in range(KEY_BLOCK // step // 4):
        four = scores[4 * i : 4 * i + 4]
        rows = slice(i * step, (i + 1) * step)
        first_ref[rows, :] = pick(group, [roll(four[0], 64), roll(four[1], 96), four[2], roll(four[3], 32)])
        second_ref[rows, :] = pick(group, [roll(four[0], 32), roll(four[1], 64), roll(four[2], 96), four[3]])


def score_call(tau, q_cols, keys, start, count):
    width = keys.shape[1]
    base = start // KEY_BLOCK
    steps = count // KEY_BLOCK
    half, quarter = KEY_BLOCK // 2, KEY_BLOCK // 4
    return pl.pallas_call(
        score_kernel,
        grid=(steps,),
        out_shape=(
            jax.ShapeDtypeStruct((count // 2, 128), F32),
            jax.ShapeDtypeStruct((count // 4, 128), F32),
            jax.ShapeDtypeStruct((count // 4, 128), F32),
        ),
        in_specs=[
            pl.BlockSpec(memory_space=SMEM),
            pl.BlockSpec((width, 128), lambda i: (0, 0)),
            pl.BlockSpec((KEY_BLOCK, width), lambda i: (i + base, 0)),
        ],
        out_specs=(
            pl.BlockSpec((half, 128), lambda i: (i, 0)),
            pl.BlockSpec((quarter, 128), lambda i: (i, 0)),
            pl.BlockSpec((quarter, 128), lambda i: (i, 0)),
        ),
        compiler_params=pltpu.CompilerParams(vmem_limit_bytes=VMEM_BYTES),
        cost_estimate=pl.CostEstimate(flops=2 * count * width * 128, bytes_accessed=2 * count * width, transcendentals=0),
        name="scores",
    )(tau, q_cols, keys)


def place_ids(tok_ref, order, group_ref, ids_ref, line_ref, flag_ref, sem):
    assert PACK == 4 and TOK_BLOCK == 128
    tok = tok_ref[...]
    block, run, within = tok >> 9, (tok >> 7) & 3, tok & 127
    if order is None:
        line = block * 256 + (run >> 1) * 128 + within
        group = run & 1
    else:
        line = block * 128 + within
        group = sum(jnp.where(run == order[g], g, 0) for g in range(PACK))
    lane = lax.broadcasted_iota(jnp.int32, (1, 128), 1)
    meet = jnp.zeros(tok.shape, F32)
    for shift in range(1, BATCH_KEYS):
        same = (line == roll(line, shift)) & (lane % BATCH_KEYS >= shift)
        meet = jnp.where(same, 1.0, meet)
    rows = lax.broadcasted_iota(jnp.int32, (128, 128), 0) // FLAG_KEYS
    shared = (rows == lax.broadcasted_iota(jnp.int32, (128, 128), 1) // FLAG_KEYS).astype(F32)
    ids_ref[0] = line
    ids_ref[1] = jnp.dot(meet, shared, preferred_element_type=F32).astype(jnp.int32)
    group_ref[...] = group.astype(F32).T.astype(jnp.bfloat16)
    return [
        pltpu.make_async_copy(ids_ref.at[0], line_ref, sem.at[0]),
        pltpu.make_async_copy(ids_ref.at[1], flag_ref, sem.at[1]),
    ]


def load_parts(parts, scores, sem):
    copies = []
    start = 0
    for i, part in enumerate(parts):
        copies.append(pltpu.make_async_copy(part, scores.at[pl.ds(start, part.shape[0])], sem.at[i]))
        copies[-1].start()
        start += part.shape[0]
    return copies


def clear(hist):
    step = 512

    def body(i, carry):
        hist[pl.ds(pl.multiple_of(i * step, step), step), :] = jnp.zeros((step, 128), F32)
        return carry

    lax.fori_loop(0, hist.shape[0] // step, body, 0)


def across(value, width, combine):
    while width < 128:
        value = combine(value, roll(value, width))
        width *= 2
    return value


def top_of(scores, width):
    step = 512

    def body(i, best):
        block = scores[pl.ds(pl.multiple_of(i * step, step), step), :]
        return jnp.maximum(best, jnp.max(block.reshape(step // 8, 8, 128), axis=0))

    best = lax.fori_loop(0, scores.shape[0] // step, body, jnp.full((8, 128), -jnp.inf, F32))
    return across(jnp.max(best, axis=0, keepdims=True), width, jnp.maximum)


def spread_weights(scores, weights, group_ref, top, width):
    count = 128 // width
    group = lane_group(width)
    spread_lane = lax.broadcasted_iota(jnp.int32, (128, 128), 1) // width
    spread_row = lax.broadcasted_iota(jnp.int32, (128, 128), 0)
    together = 4

    def body(i, total):
        for u in range(together):
            block = i * together + u
            select = (spread_row == block * count + spread_lane).astype(F32).astype(jnp.bfloat16)
            target = jnp.dot(group_ref[...], select, preferred_element_type=F32).astype(jnp.int32)
            shift = (target - group) & (count - 1)
            value = jnp.exp(scores[pl.ds(pl.multiple_of(block * 128, 128), 128), :] - top)
            total = total + jnp.sum(value.reshape(16, 8, 128), axis=0)
            turned = [jnp.where(shift == d, value, 0.0) for d in range(count)]
            turned = [turned[0]] + [roll(turned[d], width * d) for d in range(1, count)]
            for source in range(count):
                line = pick(group, [turned[(g - source) % count] for g in range(count)])
                at = pl.multiple_of((block * count + source) * 128, 128)
                weights[pl.ds(at, 128), :] = line
        return total

    total = lax.fori_loop(0, scores.shape[0] // 128 // together, body, jnp.zeros((8, 128), F32))
    return across(jnp.sum(total, axis=0, keepdims=True), width, jnp.add)


def add_weights(line_ref, flag_ref, weights, hists):
    assert FLAG_KEYS == 128

    def add(hist, row, lane, key, count):
        at = [line_ref[row, lane + k] for k in range(count)]
        sums = [hist[pl.ds(at[k], 1), :] + weights[pl.ds(key + k, 1), :] for k in range(count)]
        for k in range(count):
            hist[pl.ds(at[k], 1), :] = sums[k]

    def body(i, carry):
        key = i * FLAG_KEYS

        def apart():
            for b in range(FLAG_KEYS // BATCH_KEYS):
                add(hists[b % 2], i, b * BATCH_KEYS, key + b * BATCH_KEYS, BATCH_KEYS)

        def one_by_one():
            def step(k, carry):
                for which in range(2):
                    add(hists[which], i, 2 * k + which, key + 2 * k + which, 1)
                return carry

            lax.fori_loop(0, FLAG_KEYS // 2, step, 0)

        lax.cond(flag_ref[i, 0] == 0, apart, one_by_one)
        return carry

    lax.fori_loop(0, weights.shape[0] // FLAG_KEYS, body, 0)


def piece_at(pos_ref, k, size):
    x, core = pos_ref[0], pos_ref[1]
    x_of = x if k >= 2 else 1 - x
    core_of = core if k % 2 else 1 - core
    return pl.ds(pl.multiple_of((2 * x_of + core_of) * size, 8), size)


def head_block(top, total):
    row = lax.broadcasted_iota(jnp.int32, (HEAD, 128), 0)
    return jnp.where(row == 0, top, jnp.where(row == 1, total, 0.0))


def own_kernel(order, n_parts, pos_ref, tok_ref, *refs):
    parts, refs = refs[:n_parts], refs[n_parts:]
    outs, refs = refs[:8], refs[8:]
    group_ref, ids_ref, line_ref, flag_ref, id_sem, scores, weights, even, odd, heads, in_sem, out_sem, head_sem = refs
    lines = even.shape[0]
    piece = lines // 8
    copies = load_parts(parts, scores, in_sem)
    copies += place_ids(tok_ref, order, group_ref, ids_ref, line_ref, flag_ref, id_sem)
    for copy in copies[-2:]:
        copy.start()
    clear(even)
    clear(odd)
    for copy in copies:
        copy.wait()
    top = top_of(scores, 64)
    total = spread_weights(scores, weights, group_ref, top, 64)
    add_weights(line_ref, flag_ref, weights, (even, odd))

    quad = lane_group(32) % 2 == 0
    tops = [jnp.where(quad, top, roll(top, 32)), jnp.where(quad, roll(top, 32), top)]
    totals = [jnp.where(quad, total, roll(total, 32)), jnp.where(quad, roll(total, 32), total)]
    for c in range(2):
        heads[c] = head_block(tops[c], totals[c])
    together = 4

    def split(i, carry):
        values = []
        for u in range(together):
            block = i * together + u
            near = pl.ds(pl.multiple_of(block * 256, 256), 128)
            far = pl.ds(pl.multiple_of(block * 256 + 128, 128), 128)
            low = even[near, :] + odd[near, :]
            high = roll(even[far, :] + odd[far, :], 32)
            values.append((block, low, high))
        for block, low, high in values:
            at = pl.ds(pl.multiple_of(block * 128, 128), 128)
            weights[at, :] = jnp.where(quad, low, high)
            even[at, :] = jnp.where(quad, high, low)
        return carry

    lax.fori_loop(0, lines // 256 // together, split, 0)
    sends = []
    for c, source in enumerate((weights, even)):
        for k in range(4):
            out = outs[k * 2 + c]
            at = piece_at(pos_ref, k, piece)
            sends.append(pltpu.make_async_copy(source.at[at], out.at[pl.ds(0, piece)], out_sem.at[c, k]))
            sends.append(pltpu.make_async_copy(heads.at[c], out.at[pl.ds(piece, HEAD)], head_sem.at[c, k]))
    for send in sends:
        send.start()
    for send in sends:
        send.wait()


def chunk_kernel(order, n_parts, pos_ref, tok_ref, *refs):
    parts, refs = refs[:n_parts], refs[n_parts:]
    prevs, refs = refs[:4], refs[5:]
    outs, refs = refs[:4], refs[4:]
    group_ref, ids_ref, line_ref, flag_ref, id_sem, scores, weights, even, odd, heads, in_sem, prev_sem, out_sem, head_sem = refs
    lines = even.shape[0]
    piece = lines // 4
    copies = load_parts(parts, scores, in_sem)
    fetches = [
        pltpu.make_async_copy(prevs[k].at[pl.ds(0, piece)], even.at[piece_at(pos_ref, k, piece)], prev_sem.at[k])
        for k in range(4)
    ]
    fetches.append(pltpu.make_async_copy(prevs[0].at[pl.ds(piece, HEAD)], heads.at[1], prev_sem.at[4]))
    for fetch in fetches:
        fetch.start()
    copies += place_ids(tok_ref, order, group_ref, ids_ref, line_ref, flag_ref, id_sem)
    for copy in copies[-2:]:
        copy.start()
    clear(odd)
    for copy in copies:
        copy.wait()
    top = top_of(scores, 32)
    for fetch in fetches:
        fetch.wait()
    old_top, old_total = heads[1, 0:1, :], heads[1, 1:2, :]
    top = jnp.maximum(top, old_top)
    old_scale = jnp.exp(old_top - top)
    total = spread_weights(scores, weights, group_ref, top, 32)
    step = 256

    def rescale(i, carry):
        at = pl.ds(pl.multiple_of(i * step, step), step)
        even[at, :] = even[at, :] * old_scale
        return carry

    lax.fori_loop(0, lines // step, rescale, 0)
    add_weights(line_ref, flag_ref, weights, (even, odd))

    def join(i, carry):
        at = pl.ds(pl.multiple_of(i * step, step), step)
        even[at, :] = even[at, :] + odd[at, :]
        return carry

    lax.fori_loop(0, lines // step, join, 0)
    heads[0] = head_block(top, total + old_total * old_scale)
    sends = []
    for k in range(4):
        at = piece_at(pos_ref, k, piece)
        sends.append(pltpu.make_async_copy(even.at[at], outs[k].at[pl.ds(0, piece)], out_sem.at[k]))
        sends.append(pltpu.make_async_copy(heads.at[0], outs[k].at[pl.ds(piece, HEAD)], head_sem.at[k]))
    for send in sends:
        send.start()
    for send in sends:
        send.wait()


def histogram_call(tok, order, pos, parts, prevs, after, vocab):
    own = not prevs
    rows = sum(part.shape[0] for part in parts)
    lines = vocab // (2 if own else PACK)
    out = jax.ShapeDtypeStruct((vocab // PACK // 4 + HEAD, 128), F32)
    keys = tok.shape[0]
    tok = tok.reshape(128, 128)
    assert keys == 128 * 128
    count = 8 if own else 4
    dma = pltpu.SemaphoreType.DMA
    extra = [] if own else [*prevs, after]
    return pl.pallas_call(
        functools.partial(own_kernel if own else chunk_kernel, order, len(parts)),
        out_shape=(out,) * count,
        in_specs=[pl.BlockSpec(memory_space=SMEM), pl.BlockSpec(memory_space=VMEM)]
        + [pl.BlockSpec(memory_space=ANY)] * (len(parts) + len(extra)),
        out_specs=(pl.BlockSpec(memory_space=ANY),) * count,
        scratch_shapes=[VMEM((128, 128), jnp.bfloat16), VMEM((2, 128, 128), jnp.int32)]
        + [SMEM((128, 128), jnp.int32), SMEM((128, 128), jnp.int32), dma((2,))]
        + [VMEM((rows, 128), F32), VMEM((keys, 128), F32), VMEM((lines, 128), F32), VMEM((lines, 128), F32)]
        + [VMEM((2, HEAD, 128), F32), dma((len(parts),))]
        + ([dma((2, 4)), dma((2, 4))] if own else [dma((5,)), dma((4,)), dma((4,))]),
        compiler_params=pltpu.CompilerParams(vmem_limit_bytes=VMEM_BYTES),
        cost_estimate=pl.CostEstimate(flops=10**6, bytes_accessed=2 * 10**7, transcendentals=0),
        name="own_histogram" if own else "chunk_histogram",
    )(pos, tok, *parts, *extra)


def merge_kernel(a_ref, b_ref, out_ref):
    lines = a_ref.shape[0] - HEAD
    a_top, b_top = a_ref[lines : lines + 1, :], b_ref[lines : lines + 1, :]
    top = jnp.maximum(a_top, b_top)
    a_scale, b_scale = jnp.exp(a_top - top), jnp.exp(b_top - top)
    total = a_ref[lines + 1 : lines + 2, :] * a_scale + b_ref[lines + 1 : lines + 2, :] * b_scale
    chunk = 128

    def add(i, carry):
        at = pl.ds(pl.multiple_of(i * chunk, chunk), chunk)
        out_ref[at, :] = a_ref[at, :] * a_scale + b_ref[at, :] * b_scale
        return carry

    lax.fori_loop(0, lines // chunk, add, 0)
    row = lax.broadcasted_iota(jnp.int32, (HEAD, 128), 0)
    out_ref[lines : lines + HEAD, :] = jnp.where(row == 0, top, jnp.where(row == 1, total, 0.0))


def merge_call(a, b):
    return pl.pallas_call(
        merge_kernel,
        out_shape=jax.ShapeDtypeStruct(a.shape, F32),
        compiler_params=pltpu.CompilerParams(vmem_limit_bytes=VMEM_BYTES),
        cost_estimate=pl.CostEstimate(flops=10**5, bytes_accessed=3 * a.size * 4, transcendentals=0),
        name="merge",
    )(a, b)


def head_kernel(q_ref, w_ref, after_ref, logits_ref, stat_ref, top_ref, sum_ref):
    del after_ref
    i = pl.program_id(0)

    @pl.when(i == 0)
    def _():
        top_ref[...] = jnp.full(top_ref.shape, -jnp.inf, F32)
        sum_ref[...] = jnp.zeros(sum_ref.shape, F32)

    logits = jnp.dot(q_ref[...], w_ref[...], preferred_element_type=F32)
    logits_ref[...] = logits
    old = top_ref[...]
    new = jnp.maximum(old, jnp.max(logits, axis=1, keepdims=True))
    part = jnp.sum(jnp.exp(logits - new[:, 0:1]), axis=1, keepdims=True)
    sum_ref[...] = sum_ref[...] * jnp.exp(old - new) + part
    top_ref[...] = new
    stat_ref[0] = top_ref[...]
    stat_ref[1] = sum_ref[...]


def head_call(rows, w_head, after):
    count, width = rows.shape
    cols = w_head.shape[1]
    block = cols // 10
    return pl.pallas_call(
        head_kernel,
        grid=(cols // block,),
        out_shape=(jax.ShapeDtypeStruct((count, cols), F32), jax.ShapeDtypeStruct((2, count, 128), F32)),
        in_specs=[
            pl.BlockSpec((count, width), lambda i: (0, 0)),
            pl.BlockSpec((width, block), lambda i: (0, i)),
            pl.BlockSpec(memory_space=ANY),
        ],
        out_specs=(pl.BlockSpec((count, block), lambda i: (0, i)), pl.BlockSpec((2, count, 128), lambda i: (0, 0, 0))),
        scratch_shapes=[VMEM((count, 128), F32), VMEM((count, 128), F32)],
        compiler_params=pltpu.CompilerParams(vmem_limit_bytes=VMEM_BYTES),
        cost_estimate=pl.CostEstimate(flops=2 * count * width * cols, bytes_accessed=2 * width * cols, transcendentals=0),
        name="head",
    )(rows, w_head, after)


def mix_kernel(order, n_prev, mix_ref, *refs):
    ins, heads, logits_ref, stat_ref = refs[:3], refs[3:6], refs[6], refs[7]
    out_ref = refs[8 + n_prev]
    mix = mix_ref[0]
    tops = [head[0:1, :] for head in heads]
    top = jnp.maximum(jnp.maximum(tops[0], tops[1]), tops[2])
    scales = [jnp.exp(value - top) for value in tops]
    total = sum(head[1:2, :] * scale for head, scale in zip(heads, scales))
    scales = [scale * mix / total for scale in scales]
    lm_top = stat_ref[0]
    lm_scale = (1.0 - mix) / stat_ref[1]
    for b in range(STAGE_BLOCKS):
        rows = slice(b * TOK_BLOCK, (b + 1) * TOK_BLOCK)
        value = ins[0][rows, :] * scales[0] + ins[1][rows, :] * scales[1] + ins[2][rows, :] * scales[2]
        turned = value.T
        for g in range(PACK):
            run = order[g]
            cols = slice((b * PACK + run) * TOK_BLOCK, (b * PACK + run + 1) * TOK_BLOCK)
            lm = jnp.exp(logits_ref[:, cols] - lm_top) * lm_scale
            out_ref[:, cols] = jnp.log(turned[g * 32 : (g + 1) * 32, :] + lm)


def mix_call(mix, pieces, logits, stat, index, prev):
    lines = pieces[0].shape[0] - HEAD
    block = STAGE_BLOCKS * TOK_BLOCK
    count, cols = logits.shape
    n_prev = 0 if prev is None else 1
    wide = block * PACK
    return pl.pallas_call(
        functools.partial(mix_kernel, ORDERS[index], n_prev),
        grid=(lines // block,),
        out_shape=jax.ShapeDtypeStruct((count, cols), F32),
        in_specs=[pl.BlockSpec(memory_space=SMEM)]
        + [pl.BlockSpec((block, 128), lambda i: (i, 0))] * 3
        + [pl.BlockSpec((HEAD, 128), lambda i: (lines // HEAD, 0))] * 3
        + [pl.BlockSpec((32, wide), lambda i: (index, i)), pl.BlockSpec((2, 32, 128), lambda i: (0, index, 0))]
        + [pl.BlockSpec(memory_space=ANY)] * n_prev,
        out_specs=pl.BlockSpec((32, wide), lambda i: (index, i)),
        input_output_aliases={9: 0} if n_prev else {},
        compiler_params=pltpu.CompilerParams(vmem_limit_bytes=VMEM_BYTES),
        cost_estimate=pl.CostEstimate(flops=10**5, bytes_accessed=8 * 10**6, transcendentals=0),
        name="mix",
    )(mix, *pieces, *pieces, logits, stat, *([prev] if n_prev else []))


CHUNKS = (2048, 6144, 8192)


def solution(mesh):
    store_devs = mesh.shape["store"]
    model_devs = mesh.shape["model"]
    assert store_devs == 2 and model_devs == 4
    group_axes = ("store", "model")
    across_y = [(0, 1), (1, 0)]
    across_core = [(0, 1), (1, 0), (2, 3), (3, 2)]
    across_x = [(0, 2), (2, 0), (1, 3), (3, 1)]

    def swap_y(value):
        return lax.ppermute(value, "store", across_y)

    def swap_core(value):
        return lax.ppermute(value, "model", across_core)

    def swap_x(value):
        return lax.ppermute(value, "model", across_x)

    def local_step(queries, w_head, store_keys, store_tok, temperature, mix_weight):
        vocab = w_head.shape[1] * model_devs
        rows = queries.shape[0] // store_devs
        y = lax.axis_index("store")
        m = lax.axis_index("model")
        pos = jnp.stack([m // 2, m % 2]).astype(jnp.int32)
        mine = lax.dynamic_slice_in_dim(queries, y * rows, rows, axis=0)
        theirs = lax.dynamic_slice_in_dim(queries, (1 - y) * rows, rows, axis=0)
        q_cols = jnp.concatenate([mine, theirs], axis=0).T
        tau = temperature.reshape(1)
        mix = mix_weight.reshape(1)

        their_tok = swap_y(store_tok)
        own, first, second = [], [], []
        start = 0
        for count in CHUNKS:
            a, b, c = score_call(tau, q_cols, store_keys, start, count)
            own.append(a)
            first.append(swap_y(b))
            second.append(swap_y(c))
            start += count

        kept = histogram_call(store_tok, None, pos, own, [], None, vocab)
        sums = []
        after = kept[0]
        for index, parts in enumerate((first, second)):
            out = histogram_call(their_tok, ORDERS[index], pos, parts, kept[index::2], after, vocab)
            far = swap_core(out[0])
            near = swap_core(out[2])
            after = merge_call(out[1], far)
            sums.append((out[3], near, swap_x(after)))
            last = out[3]
        logits, stat = head_call(mine, w_head, last)
        for swap in (swap_core, swap_x):
            other = swap(stat)
            top = jnp.maximum(stat[0], other[0])
            stat = jnp.stack([top, stat[1] * jnp.exp(stat[0] - top) + other[1] * jnp.exp(other[0] - top)])
        result = mix_call(mix, sums[0], logits, stat, 0, None)
        return mix_call(mix, sums[1], logits, stat, 1, result)

    return jax.shard_map(
        local_step,
        mesh=mesh,
        in_specs=(P("data", None), P(None, "model"), P(group_axes, None), P(group_axes), P(), P()),
        out_specs=P(("data", "store"), "model"),
        check_vma=False,
    )
```

time: 335 us -> 301 us (0.90)
  Pallas kernels: 232 us -> 190 us
  waiting for transfers between devices: 43.5 us -> 80.5 us
  local copies, waits for them, and re-layouts: 23.2 us -> 3.97 us
  other arithmetic: 14.4 us -> 2.06 us
  starting transfers between devices: 15.3 us -> 21.9 us
    ppermute x9 -> x7, waiting for transfers between devices: 0.02 us -> 41.2 us  [swap_y(): return lax.ppermute(value, 'store', across_y)]
    pallas_call x5, Pallas kernels: 148 us -> 107 us  [the longest x3 95.9 us: histogram_call(): pl.pallas_call(functools.partial(own_kernel if own else chunk_kernel, ord...]
    unnamed x54 -> x10, local copies, waits for them, and re-layouts: 19.9 us -> 1.78 us
    reduce_or x30 -> x0, other arithmetic: 12 us -> none  [the longest x28 11.7 us: place_ids(): meet = meet | jnp.any(batch[:, shift:] == batch[:, :-shift], axis=1)]
    ppermute x3, starting transfers between devices: 2.05 us -> 9.49 us  [swap_x(): return lax.ppermute(value, 'model', across_x)]
    pallas_call x4 -> x3, Pallas kernels: 56.5 us -> 50 us  [score_call(): pl.pallas_call(score_kernel, grid=(steps,), out_shape=(jax.ShapeDtypeStru...]
    pallas_call x2, Pallas kernels: 3.06 us -> 6.8 us  [merge_call(): pl.pallas_call(merge_kernel, out_shape=jax.ShapeDtypeStruct(a.shape, F32)...]
    ppermute x9 -> x7, starting transfers between devices: 11.5 us -> 9.44 us  [swap_y(): return lax.ppermute(value, 'store', across_y)]
  transfers between devices with their start and end apart: 17 -> 15, of which waited for: 3 -> 3; matrix products, arithmetic and copies ran while one was open for 5% -> 1% of each run, Pallas kernels for 69% -> 34%
where the time goes in v2:
time: 301 us; the launch traced here: 299 us
  Pallas kernels  190 us (63%)
  waiting for transfers between devices  80.5 us (27%)
  starting transfers between devices  21.9 us (7%)
  local copies, waits for them, and re-layouts  3.97 us (1%)
    pallas_call x3, Pallas kernels, histogram_call(): pl.pallas_call(functools.partial(own_kernel if own else chunk_kernel, ord...  95.9 us
    pallas_call x3, Pallas kernels, score_call(): pl.pallas_call(score_kernel, grid=(steps,), out_shape=(jax.ShapeDtypeStru...  50 us
    ppermute x7, waiting for transfers between devices, swap_y(): return lax.ppermute(value, 'store', across_y)  41.2 us
    ppermute x3, waiting for transfers between devices, swap_x(): return lax.ppermute(value, 'model', across_x)  37.9 us
    pallas_call x1, Pallas kernels, head_call(): pl.pallas_call(head_kernel, grid=(cols // block,), out_shape=(jax.ShapeDt...  25.6 us
    pallas_call x2, Pallas kernels, mix_call(): pl.pallas_call(functools.partial(mix_kernel, ORDERS[index], n_prev), grid...  11.3 us
    ppermute x3, starting transfers between devices, swap_x(): return lax.ppermute(value, 'model', across_x)  9.49 us
    ppermute x7, starting transfers between devices, swap_y(): return lax.ppermute(value, 'store', across_y)  9.44 us
  transfers between devices with their start and end apart: 15, of which 3 were waited for; matrix products, arithmetic and copies ran while one was open for 1% of the time, Pallas kernels for 34%

profile of v2, /device:TPU:0, one launch (start us, length us, event | category | flops | bytes accessed | tf_op | source)
XLA Modules:
  0.0 299.4 jit_solution(13878501886149081440)
XLA Ops:
  0.0 1.1 constant_dynamic-slice_fusion.1
  1.2 1.1 copy.8.q_ref
  2.9 23.4 %scores.5 = (f32[4096,128]{1,0:T(8,128)}, f32[2048,128]{1,0:T(8,128)}, f32[2048,128]{1,0:T(8,128)}) custom-call(f32[1]{0:T(128)} %bitcast.10.tau_ref, bf16[2560,128]{1,0:T(8,128)(2,1)} %copy.8.q_ref, bf16[16384,2560]{1,0:T(8,128)(2,1)} %k_ref.5), custom_call_target="tpu_custom_call" | custom-call | flops 5368709120 | bytes 41943040 | tf_op jit(solution)/shard_map/scores/pallas_call | solution.py:68
  26.3 3.3 %collective-permute-start.6 = (f32[2048,128]{1,0:T(8,128)}, f32[2048,128]{1,0:T(8,128)}, u32[]{:S(2)}, u32[]{:S(2)}) collective-permute-start(f32[2048,128]{1,0:T(8,128)} %get-tuple-element.44), channel_id=1, source_target_pairs={{0,4},{4,0},{1,5},{5,1},{2,6},{6,2},{3,7},{7,3}} | collective-permute-start | bytes 3145736 | tf_op jit(solution)/shard_map/ppermute | solution.py:490
  29.7 18.3 %scores.4 = (f32[3072,128]{1,0:T(8,128)}, f32[1536,128]{1,0:T(8,128)}, f32[1536,128]{1,0:T(8,128)}) custom-call(f32[1]{0:T(128)} %bitcast.9.tau_ref, bf16[2560,128]{1,0:T(8,128)(2,1)} %copy.8.q_ref, bf16[16384,2560]{1,0:T(8,128)(2,1)} %k_ref.5), custom_call_target="tpu_custom_call" | custom-call | flops 4026531840 | bytes 31457280 | tf_op jit(solution)/shard_map/scores/pallas_call | solution.py:68
  48.0 0.1 collective-permute-start.5
  48.1 8.2 %scores.3 = (f32[1024,128]{1,0:T(8,128)}, f32[512,128]{1,0:T(8,128)}, f32[512,128]{1,0:T(8,128)}) custom-call(f32[1]{0:T(128)} %bitcast.8.tau_ref, bf16[2560,128]{1,0:T(8,128)(2,1)} %copy.8.q_ref, bf16[16384,2560]{1,0:T(8,128)(2,1)} %k_ref.5), custom_call_target="tpu_custom_call" | custom-call | flops 1342177280 | bytes 10485760 | tf_op jit(solution)/shard_map/scores/pallas_call | solution.py:68
  56.3 2.0 collective-permute-start.4
  58.3 0.1 collective-permute-start
  58.3 0.6 pad_add_fusion.pos_ref
  58.9 37.3 %own_histogram.1 = (f32[3208,128]{1,0:T(8,128)}, f32[3208,128]{1,0:T(8,128)}, f32[3208,128]{1,0:T(8,128)}, f32[3208,128]{1,0:T(8,128)}, f32[3208,128]{1,0:T(8,12...) custom-call(s32[2]{0:T(128)} %pad_add_fusion.pos_ref, s32[128,128]{1,0:T(8,128)} %bitcast.15, ...), custom_call_target="tpu_custom_call" | custom-call | flops 1000000 | bytes 20000000 | tf_op jit(solution)/shard_map/own_histogram/pallas_call | solution.py:346
  96.2 0.0 collective-permute-done
  96.2 0.0 collective-permute-done.4.refs_0_
  96.2 0.0 collective-permute-done.5.refs_1_
  96.3 0.0 collective-permute-done.6.refs_2_
  96.3 0.6 copy-done.3
  96.9 0.3 copy-done.1
  97.2 29.3 %chunk_histogram.2 = (f32[3208,128]{1,0:T(8,128)}, f32[3208,128]{1,0:T(8,128)}, f32[3208,128]{1,0:T(8,128)}, f32[3208,128]{1,0:T(8,128)}) custom-call(s32[2]{0:T(128)} %pad_add_fusion.pos_ref, s32[128,128]{1,0:T(8,128)} %bitcast.13, f32[512,128]{1,0:T(8,128)} %collective-permute-done.4.refs_0_, f32[1536,128]{1,0:T(8,128)} %copy-done.1, ...), custom_call_target="tpu_custom_call" | custom-call | flops 1000000 | bytes 20000000 | tf_op jit(solution)/shard_map/chunk_histogram/pallas_call | solution.py:346
  126.5 0.6 collective-permute-start.7
  127.1 2.0 collective-permute-start.3
  129.1 0.0 collective-permute-start.2
  129.1 2.0 collective-permute-start.1
  131.1 0.0 collective-permute-done.7.b_ref
  131.1 3.4 %merge.2.refs_7_ = f32[3208,128]{1,0:T(8,128)} custom-call(f32[3208,128]{1,0:T(8,128)} %get-tuple-element.49.a_ref, f32[3208,128]{1,0:T(8,128)} %collective-permute-done.7.b_ref), custom_call_target="tpu_custom_call" | custom-call | flops 100000 | bytes 4927488 | tf_op jit(solution)/shard_map/merge/pallas_call | solution.py:382
  134.5 41.2 %collective-permute-done.1.refs_0_ = f32[512,128]{1,0:T(8,128)} collective-permute-done((f32[512,128]{1,0:T(8,128)}, f32[512,128]{1,0:T(8,128)}, u32[]{:S(2)}, u32[]{:S(2)}) %collective-permute-start.1) | collective-permute-done | bytes 262176 | tf_op jit(solution)/shard_map/ppermute | solution.py:490
  175.7 0.0 collective-permute-done.2.refs_1_
  175.7 0.0 collective-permute-done.3.refs_2_
  175.7 0.9 copy-done.2
  176.6 29.3 %chunk_histogram.3 = (f32[3208,128]{1,0:T(8,128)}, f32[3208,128]{1,0:T(8,128)}, f32[3208,128]{1,0:T(8,128)}, f32[3208,128]{1,0:T(8,128)}) custom-call(s32[2]{0:T(128)} %pad_add_fusion.pos_ref, s32[128,128]{1,0:T(8,128)} %bitcast.14, f32[512,128]{1,0:T(8,128)} %collective-permute-done.1.refs_0_, f32[1536,128]{1,0:T(8,128)} %copy-done.2, ...), custom_call_target="tpu_custom_call" | custom-call | flops 1000000 | bytes 20000000 | tf_op jit(solution)/shard_map/chunk_histogram/pallas_call | solution.py:346
  205.8 2.0 collective-permute-start.9
  207.8 0.0 collective-permute-start.13
  207.9 6.2 %collective-permute-start.14 = (f32[3208,128]{1,0:T(8,128)}, f32[3208,128]{1,0:T(8,128)}, u32[]{:S(2)}, u32[]{:S(2)}) collective-permute-start(f32[3208,128]{1,0:T(8,128)} %merge.2.refs_7_), channel_id=1, source_target_pairs={{0,2},{2,0},{1,3},{3,1},{4,6},{6,4},{5,7},{7,5}} | collective-permute-start | bytes 4927496 | tf_op jit(solution)/shard_map/ppermute | solution.py:496
  214.1 0.2 collective-permute-start.8
  214.3 0.0 collective-permute-done.9.b_ref
  214.3 3.4 %merge.3 = f32[3208,128]{1,0:T(8,128)} custom-call(f32[3208,128]{1,0:T(8,128)} %get-tuple-element.53.a_ref, f32[3208,128]{1,0:T(8,128)} %collective-permute-done.9.b_ref), custom_call_target="tpu_custom_call" | custom-call | flops 100000 | bytes 4927488 | tf_op jit(solution)/shard_map/merge/pallas_call | solution.py:382
  217.7 3.2 %collective-permute-start.10 = (f32[3208,128]{1,0:T(8,128)}, f32[3208,128]{1,0:T(8,128)}, u32[]{:S(2)}, u32[]{:S(2)}) collective-permute-start(f32[3208,128]{1,0:T(8,128)} %merge.3), channel_id=1, source_target_pairs={{0,2},{2,0},{1,3},{3,1},{4,6},{6,4},{5,7},{7,5}} | collective-permute-start | bytes 4927496 | tf_op jit(solution)/shard_map/ppermute | solution.py:496
  220.9 25.6 %head.1 = (f32[64,12800]{1,0:T(8,128)}, f32[2,64,128]{2,1,0:T(8,128)}) custom-call(bf16[64,2560]{1,0:T(8,128)(2,1)} %copy-done, bf16[2560,12800]{1,0:T(8,128)(2,1)} %w_ref.1, f32[3208,128]{1,0:T(8,128)} %get-tuple-element.51.after_ref.refs_0_.refs_3_), custom_call_target="tpu_custom_call" | custom-call | flops 4194304000 | bytes 65536000 | tf_op jit(solution)/shard_map/head/pallas_call | solution.py:415
  246.5 0.1 collective-permute-start.11
  246.6 1.4 collective-permute-done.11
  248.0 0.8 fusion.1
  248.8 0.0 collective-permute-start.12
  249.5 37.9 %collective-permute-done.12 = f32[2,64,128]{2,1,0:T(8,128)S(1)} collective-permute-done((f32[2,64,128]{2,1,0:T(8,128)S(1)}, f32[2,64,128]{2,1,0:T(8,128)S(1)}, u32[]{:S(2)}, u32[]{:S(2)}) %collective-permute-start.12) | collective-permute-done | bytes 65568 | tf_op jit(solution)/shard_map/ppermute | solution.py:496
  287.4 0.6 pad_maximum_fusion.1.refs_7_
  288.1 0.0 collective-permute-done.13.refs_1_.refs_4_
  288.1 0.0 collective-permute-done.14.refs_2_.refs_5_
  288.1 5.7 %mix.2.refs_8_ = f32[64,12800]{1,0:T(8,128)} custom-call(f32[1]{0:T(128)} %bitcast.11.mix_ref, f32[3208,128]{1,0:T(8,128)} %get-tuple-element.57.refs_0_.refs_3_, f32[3208,128]{1,0:T(8,128)} %collective-permute-done.13.refs_1_.refs_4_, f32[3208,128]{1,0:T(8,128)} %collective-permute-done.14.refs_2_.refs_5_, f32[3208,128]{1,0:T(8,128)} %get-tuple-element.57.refs_0_.refs_3_, ...), custom_call_target="tpu_custom_call" | custom-call | flops 100000 | bytes 8000000 | tf_op jit(solution)/shard_map/mix/pallas_call | solution.py:460
  293.7 0.0 collective-permute-done.8.refs_1_.refs_4_
  293.8 5.7 %mix.3 = f32[64,12800]{1,0:T(8,128)} custom-call(f32[1]{0:T(128)} %bitcast.12.mix_ref, f32[3208,128]{1,0:T(8,128)} %get-tuple-element.51.after_ref.refs_0_.refs_3_, f32[3208,128]{1,0:T(8,128)} %collective-permute-done.8.refs_1_.refs_4_, f32[3208,128]{1,0:T(8,128)} %collective-permute-done.10.refs_2_.refs_5_, ...), custom_call_target="tpu_custom_call", output_to_operand_aliasing={{}: (9, {})} | custom-call | flops 100000 | bytes 8000000 | tf_op jit(solution)/shard_map/mix/pallas_call | solution.py:460
  (11 shorter events, 0.1 us)
Async XLA Ops:
  1.1 25.2 %copy-start = (bf16[64,2560]{1,0:T(8,128)(2,1)}, bf16[64,2560]{1,0:T(8,128)(2,1)S(1)}, u32[]{:S(2)}) copy-start(bf16[64,2560]{1,0:T(8,128)(2,1)S(1)} %get-tuple-element.61.q_ref) | copy-start | bytes 983044
  26.3 69.9 %collective-permute-start.6 = (f32[2048,128]{1,0:T(8,128)}, f32[2048,128]{1,0:T(8,128)}, u32[]{:S(2)}, u32[]{:S(2)}) collective-permute-start(f32[2048,128]{1,0:T(8,128)} %get-tuple-element.44), channel_id=1, source_target_pairs={{0,4},{4,0},{1,5},{5,1},{2,6},{6,2},{3,7},{7,3}} | collective-permute-start | bytes 3145736 | tf_op jit(solution)/shard_map/ppermute | solution.py:490
  48.0 48.2 %collective-permute-start.5 = (f32[1536,128]{1,0:T(8,128)}, f32[1536,128]{1,0:T(8,128)S(1)}, u32[]{:S(2)}, u32[]{:S(2)}) collective-permute-start(f32[1536,128]{1,0:T(8,128)} %get-tuple-element.43), channel_id=1, source_target_pairs={{0,4},{4,0},{1,5},{5,1},{2,6},{6,2},{3,7},{7,3}} | collective-permute-start | bytes 2359304 | tf_op jit(solution)/shard_map/ppermute | solution.py:490
  48.1 10.2 %copy-start.4 = (s32[16384]{0:T(1024)S(1)}, s32[16384]{0:T(1024)}, u32[]{:S(2)}) copy-start(s32[16384]{0:T(1024)} %param.9) | copy-start | bytes 196612
  56.3 39.9 %collective-permute-start.4 = (f32[512,128]{1,0:T(8,128)}, f32[512,128]{1,0:T(8,128)}, u32[]{:S(2)}, u32[]{:S(2)}) collective-permute-start(f32[512,128]{1,0:T(8,128)} %get-tuple-element.42), channel_id=1, source_target_pairs={{0,4},{4,0},{1,5},{5,1},{2,6},{6,2},{3,7},{7,3}} | collective-permute-start | bytes 786440 | tf_op jit(solution)/shard_map/ppermute | solution.py:490
  58.3 37.9 %collective-permute-start = (s32[16384]{0:T(1024)S(1)}, s32[16384]{0:T(1024)S(1)}, u32[]{:S(2)}, u32[]{:S(2)}) collective-permute-start(s32[16384]{0:T(1024)S(1)} %copy-done.4), channel_id=1, source_target_pairs={{0,4},{4,0},{1,5},{5,1},{2,6},{6,2},{3,7},{7,3}} | collective-permute-start | bytes 196616 | tf_op jit(solution)/shard_map/ppermute | solution.py:490
  96.2 0.6 copy-start.3
  96.3 0.9 copy-start.1
  126.5 4.6 %collective-permute-start.7 = (f32[3208,128]{1,0:T(8,128)}, f32[3208,128]{1,0:T(8,128)}, u32[]{:S(2)}, u32[]{:S(2)}) collective-permute-start(f32[3208,128]{1,0:T(8,128)} %get-tuple-element.50), channel_id=1, source_target_pairs={{0,1},{1,0},{2,3},{3,2},{4,5},{5,4},{6,7},{7,6}} | collective-permute-start | bytes 4927496 | tf_op jit(solution)/shard_map/ppermute | solution.py:493
  127.1 48.6 %collective-permute-start.3 = (f32[2048,128]{1,0:T(8,128)}, f32[2048,128]{1,0:T(8,128)}, u32[]{:S(2)}, u32[]{:S(2)}) collective-permute-start(f32[2048,128]{1,0:T(8,128)} %get-tuple-element.34), channel_id=1, source_target_pairs={{0,4},{4,0},{1,5},{5,1},{2,6},{6,2},{3,7},{7,3}} | collective-permute-start | bytes 3145736 | tf_op jit(solution)/shard_map/ppermute | solution.py:490
  129.1 46.6 %collective-permute-start.2 = (f32[1536,128]{1,0:T(8,128)}, f32[1536,128]{1,0:T(8,128)S(1)}, u32[]{:S(2)}, u32[]{:S(2)}) collective-permute-start(f32[1536,128]{1,0:T(8,128)} %get-tuple-element.33), channel_id=1, source_target_pairs={{0,4},{4,0},{1,5},{5,1},{2,6},{6,2},{3,7},{7,3}} | collective-permute-start | bytes 2359304 | tf_op jit(solution)/shard_map/ppermute | solution.py:490
  129.1 46.5 %collective-permute-start.1 = (f32[512,128]{1,0:T(8,128)}, f32[512,128]{1,0:T(8,128)}, u32[]{:S(2)}, u32[]{:S(2)}) collective-permute-start(f32[512,128]{1,0:T(8,128)} %get-tuple-element.32), channel_id=1, source_target_pairs={{0,4},{4,0},{1,5},{5,1},{2,6},{6,2},{3,7},{7,3}} | collective-permute-start | bytes 786440 | tf_op jit(solution)/shard_map/ppermute | solution.py:490
  175.7 0.9 copy-start.2
  205.8 8.4 %collective-permute-start.9 = (f32[3208,128]{1,0:T(8,128)}, f32[3208,128]{1,0:T(8,128)}, u32[]{:S(2)}, u32[]{:S(2)}) collective-permute-start(f32[3208,128]{1,0:T(8,128)} %get-tuple-element.54), channel_id=1, source_target_pairs={{0,1},{1,0},{2,3},{3,2},{4,5},{5,4},{6,7},{7,6}} | collective-permute-start | bytes 4927496 | tf_op jit(solution)/shard_map/ppermute | solution.py:493
  207.8 80.2 %collective-permute-start.13 = (f32[3208,128]{1,0:T(8,128)}, f32[3208,128]{1,0:T(8,128)}, u32[]{:S(2)}, u32[]{:S(2)}) collective-permute-start(f32[3208,128]{1,0:T(8,128)} %get-tuple-element.58), channel_id=1, source_target_pairs={{0,1},{1,0},{2,3},{3,2},{4,5},{5,4},{6,7},{7,6}} | collective-permute-start | bytes 4927496 | tf_op jit(solution)/shard_map/ppermute | solution.py:493
  207.9 80.2 %collective-permute-start.14 = (f32[3208,128]{1,0:T(8,128)}, f32[3208,128]{1,0:T(8,128)}, u32[]{:S(2)}, u32[]{:S(2)}) collective-permute-start(f32[3208,128]{1,0:T(8,128)} %merge.2.refs_7_), channel_id=1, source_target_pairs={{0,2},{2,0},{1,3},{3,1},{4,6},{6,4},{5,7},{7,5}} | collective-permute-start | bytes 4927496 | tf_op jit(solution)/shard_map/ppermute | solution.py:496
  214.1 79.7 %collective-permute-start.8 = (f32[3208,128]{1,0:T(8,128)}, f32[3208,128]{1,0:T(8,128)}, u32[]{:S(2)}, u32[]{:S(2)}) collective-permute-start(f32[3208,128]{1,0:T(8,128)} %get-tuple-element.52), channel_id=1, source_target_pairs={{0,1},{1,0},{2,3},{3,2},{4,5},{5,4},{6,7},{7,6}} | collective-permute-start | bytes 4927496 | tf_op jit(solution)/shard_map/ppermute | solution.py:493
  217.7 76.1 %collective-permute-start.10 = (f32[3208,128]{1,0:T(8,128)}, f32[3208,128]{1,0:T(8,128)}, u32[]{:S(2)}, u32[]{:S(2)}) collective-permute-start(f32[3208,128]{1,0:T(8,128)} %merge.3), channel_id=1, source_target_pairs={{0,2},{2,0},{1,3},{3,1},{4,6},{6,4},{5,7},{7,5}} | collective-permute-start | bytes 4927496 | tf_op jit(solution)/shard_map/ppermute | solution.py:496
  246.5 1.5 collective-permute-start.11
  248.8 38.6 %collective-permute-start.12 = (f32[2,64,128]{2,1,0:T(8,128)S(1)}, f32[2,64,128]{2,1,0:T(8,128)S(1)}, u32[]{:S(2)}, u32[]{:S(2)}) collective-permute-start(f32[2,64,128]{2,1,0:T(8,128)S(1)} %pad_maximum_fusion), channel_id=1, source_target_pairs={{0,2},{2,0},{1,3},{3,1},{4,6},{6,4},{5,7},{7,5}} | collective-permute-start | bytes 196616 | tf_op jit(solution)/shard_map/ppermute | solution.py:496

commit v3 on v2

v3 whole, which is shorter than its diff:
```python
import functools

import jax
import jax.numpy as jnp
from jax import lax
from jax.experimental import pallas as pl
from jax.experimental.pallas import tpu as pltpu
from jax.sharding import PartitionSpec as P


F32 = jnp.float32
ANY = pl.ANY
VMEM = pltpu.VMEM
SMEM = pltpu.SMEM
KEY_BLOCK = 1024
VMEM_BYTES = 63 * 2**20
BATCH_KEYS = 8
FLAG_KEYS = 128
PACK = 4
TOK_BLOCK = 128
ORDERS = ((0, 2, 1, 3), (3, 0, 2, 1))
STAGE_BLOCKS = 5
HEAD = 8


def lane_group(width):
    return lax.broadcasted_iota(jnp.int32, (1, 128), 1) // width


def pick(group, parts):
    out = parts[-1]
    for index in range(len(parts) - 2, -1, -1):
        out = jnp.where(group == index, parts[index], out)
    return out


def roll(value, shift):
    return pltpu.roll(value, shift % 128, 1)


def score_kernel(tau_ref, rows_ref, k_ref, own_ref, *sent):
    *sent, q_ref = sent
    tau = tau_ref[0]
    first_ref, second_ref = (sent[0].at[0], sent[0].at[1]) if len(sent) == 1 else sent

    @pl.when(pl.program_id(0) == 0)
    def _():
        half = q_ref.shape[0] // 2
        y = lax.axis_index("store")
        q_ref[0:half, :] = rows_ref[pl.ds(pl.multiple_of(y * half, half), half), :]
        q_ref[half : 2 * half, :] = rows_ref[pl.ds(pl.multiple_of((1 - y) * half, half), half), :]

    dots = lax.dot_general(k_ref[...], q_ref[...], (((1,), (1,)), ((), ())), preferred_element_type=F32)
    step = 128
    norms = []
    for row in range(0, KEY_BLOCK, step):
        acc = jnp.zeros((step, 128), F32)
        for col in range(0, k_ref.shape[1], 128):
            part = k_ref[row : row + step, col : col + 128].astype(F32)
            acc += part * part
        norms.append(jnp.sum(acc, axis=1, keepdims=True))
    group = lane_group(32)
    scores = [(2.0 * dots[i * step : (i + 1) * step] - norms[i]) / tau for i in range(KEY_BLOCK // step)]
    for i in range(KEY_BLOCK // step // 2):
        own_ref[i * step : (i + 1) * step, :] = jnp.where(group < 2, scores[2 * i], roll(scores[2 * i + 1], 64))
    for i in range(KEY_BLOCK // step // 4):
        four = scores[4 * i : 4 * i + 4]
        rows = slice(i * step, (i + 1) * step)
        first_ref[rows, :] = pick(group, [roll(four[0], 64), roll(four[1], 96), four[2], roll(four[3], 32)])
        second_ref[rows, :] = pick(group, [roll(four[0], 32), roll(four[1], 64), roll(four[2], 96), four[3]])


def score_call(tau, queries, keys, start, count, joined):
    width = keys.shape[1]
    base = start // KEY_BLOCK
    half, quarter = KEY_BLOCK // 2, KEY_BLOCK // 4
    if joined:
        sent_shape = (jax.ShapeDtypeStruct((2, count // 4, 128), F32),)
        sent_spec = (pl.BlockSpec((2, quarter, 128), lambda i: (0, i, 0)),)
    else:
        sent_shape = (jax.ShapeDtypeStruct((count // 4, 128), F32),) * 2
        sent_spec = (pl.BlockSpec((quarter, 128), lambda i: (i, 0)),) * 2
    return pl.pallas_call(
        score_kernel,
        grid=(count // KEY_BLOCK,),
        out_shape=(jax.ShapeDtypeStruct((count // 2, 128), F32),) + sent_shape,
        in_specs=[
            pl.BlockSpec(memory_space=SMEM),
            pl.BlockSpec((128, width), lambda i: (0, 0)),
            pl.BlockSpec((KEY_BLOCK, width), lambda i: (i + base, 0)),
        ],
        out_specs=(pl.BlockSpec((half, 128), lambda i: (i, 0)),) + sent_spec,
        scratch_shapes=[VMEM((128, width), jnp.bfloat16)],
        compiler_params=pltpu.CompilerParams(vmem_limit_bytes=VMEM_BYTES),
        cost_estimate=pl.CostEstimate(flops=2 * count * width * 128, bytes_accessed=2 * count * width, transcendentals=0),
        name="scores",
    )(tau, queries, keys)


def place_ids(tok_ref, which, group_ref, ids_ref, line_ref, flag_ref, sem):
    assert PACK == 4 and TOK_BLOCK == 128
    tok = tok_ref[...]
    block, run, within = tok >> 9, (tok >> 7) & 3, tok & 127
    if which is None:
        line = block * 256 + (run >> 1) * 128 + within
        group = run & 1
    else:
        line = block * 128 + within
        group = sum(jnp.where(run == ORDERS[which][g], g, 0) for g in range(PACK))
    lane = lax.broadcasted_iota(jnp.int32, (1, 128), 1)
    meet = jnp.zeros(tok.shape, F32)
    for shift in range(1, BATCH_KEYS):
        same = (line == roll(line, shift)) & (lane % BATCH_KEYS >= shift)
        meet = jnp.where(same, 1.0, meet)
    rows = lax.broadcasted_iota(jnp.int32, (128, 128), 0) // FLAG_KEYS
    shared = (rows == lax.broadcasted_iota(jnp.int32, (128, 128), 1) // FLAG_KEYS).astype(F32)
    ids_ref[0] = line
    ids_ref[1] = jnp.dot(meet, shared, preferred_element_type=F32).astype(jnp.int32)
    group_ref[...] = group.astype(F32).T.astype(jnp.bfloat16)
    return [
        pltpu.make_async_copy(ids_ref.at[0], line_ref, sem.at[0]),
        pltpu.make_async_copy(ids_ref.at[1], flag_ref, sem.at[1]),
    ]


def load_parts(parts, which, scores, sem):
    copies = []
    start = 0
    for i, part in enumerate(parts):
        part = part.at[which] if len(part.shape) == 3 else part
        copies.append(pltpu.make_async_copy(part, scores.at[pl.ds(start, part.shape[0])], sem.at[i]))
        copies[-1].start()
        start += part.shape[0]
    return copies


def clear(hist):
    step = 512

    def body(i, carry):
        hist[pl.ds(pl.multiple_of(i * step, step), step), :] = jnp.zeros((step, 128), F32)
        return carry

    lax.fori_loop(0, hist.shape[0] // step, body, 0)


def across(value, width, combine):
    while width < 128:
        value = combine(value, roll(value, width))
        width *= 2
    return value


def top_of(scores, width):
    step = 512

    def body(i, best):
        block = scores[pl.ds(pl.multiple_of(i * step, step), step), :]
        return jnp.maximum(best, jnp.max(block.reshape(step // 8, 8, 128), axis=0))

    best = lax.fori_loop(0, scores.shape[0] // step, body, jnp.full((8, 128), -jnp.inf, F32))
    return across(jnp.max(best, axis=0, keepdims=True), width, jnp.maximum)


def spread_weights(scores, weights, group_ref, top, width):
    count = 128 // width
    group = lane_group(width)
    spread_lane = lax.broadcasted_iota(jnp.int32, (128, 128), 1) // width
    spread_row = lax.broadcasted_iota(jnp.int32, (128, 128), 0)
    together = 4

    def body(i, total):
        for u in range(together):
            block = i * together + u
            select = (spread_row == block * count + spread_lane).astype(F32).astype(jnp.bfloat16)
            target = jnp.dot(group_ref[...], select, preferred_element_type=F32).astype(jnp.int32)
            shift = (target - group) & (count - 1)
            value = jnp.exp(scores[pl.ds(pl.multiple_of(block * 128, 128), 128), :] - top)
            total = total + jnp.sum(value.reshape(16, 8, 128), axis=0)
            turned = [jnp.where(shift == d, value, 0.0) for d in range(count)]
            turned = [turned[0]] + [roll(turned[d], width * d) for d in range(1, count)]
            for source in range(count):
                line = pick(group, [turned[(g - source) % count] for g in range(count)])
                at = pl.multiple_of((block * count + source) * 128, 128)
                weights[pl.ds(at, 128), :] = line
        return total

    total = lax.fori_loop(0, scores.shape[0] // 128 // together, body, jnp.zeros((8, 128), F32))
    return across(jnp.sum(total, axis=0, keepdims=True), width, jnp.add)


def add_weights(line_ref, flag_ref, weights, hists):
    assert FLAG_KEYS == 128

    def add(hist, row, lane, key, count):
        at = [line_ref[row, lane + k] for k in range(count)]
        sums = [hist[pl.ds(at[k], 1), :] + weights[pl.ds(key + k, 1), :] for k in range(count)]
        for k in range(count):
            hist[pl.ds(at[k], 1), :] = sums[k]

    def body(i, carry):
        key = i * FLAG_KEYS

        def apart():
            for b in range(FLAG_KEYS // BATCH_KEYS):
                add(hists[b % 2], i, b * BATCH_KEYS, key + b * BATCH_KEYS, BATCH_KEYS)

        def one_by_one():
            def step(k, carry):
                for which in range(2):
                    add(hists[which], i, 2 * k + which, key + 2 * k + which, 1)
                return carry

            lax.fori_loop(0, FLAG_KEYS // 2, step, 0)

        lax.cond(flag_ref[i, 0] == 0, apart, one_by_one)
        return carry

    lax.fori_loop(0, weights.shape[0] // FLAG_KEYS, body, 0)


def piece_at(k, size):
    model = lax.axis_index("model")
    x, core = model // 2, model % 2
    x_of = x if k >= 2 else 1 - x
    core_of = core if k % 2 else 1 - core
    return (2 * x_of + core_of) * size


def head_block(top, total):
    row = lax.broadcasted_iota(jnp.int32, (HEAD, 128), 0)
    return jnp.where(row == 0, top, jnp.where(row == 1, total, 0.0))


def own_kernel(which, n_parts, tok_ref, *refs):
    parts, refs = refs[:n_parts], refs[n_parts:]
    outs, refs = refs[:8], refs[8:]
    group_ref, ids_ref, line_ref, flag_ref, id_sem, scores, weights, even, odd, heads, in_sem, out_sem, head_sem = refs
    lines = even.shape[0]
    piece = lines // 8
    copies = load_parts(parts, which, scores, in_sem)
    copies += place_ids(tok_ref, which, group_ref, ids_ref, line_ref, flag_ref, id_sem)
    for copy in copies[-2:]:
        copy.start()
    clear(even)
    clear(odd)
    for copy in copies:
        copy.wait()
    top = top_of(scores, 64)
    total = spread_weights(scores, weights, group_ref, top, 64)
    add_weights(line_ref, flag_ref, weights, (even, odd))

    quad = lane_group(32) % 2 == 0
    tops = [jnp.where(quad, top, roll(top, 32)), jnp.where(quad, roll(top, 32), top)]
    totals = [jnp.where(quad, total, roll(total, 32)), jnp.where(quad, roll(total, 32), total)]
    for c in range(2):
        heads[c] = head_block(tops[c], totals[c])
    together = 5

    sends = []
    for k in range(4):
        base = piece_at(k, 1)

        def split(i, carry, base=base):
            values = []
            for u in range(together):
                block = i * together + u
                near = pl.ds(pl.multiple_of(base * 2 * piece + block * 256, 128), 128)
                far = pl.ds(pl.multiple_of(base * 2 * piece + block * 256 + 128, 128), 128)
                low = even[near, :] + odd[near, :]
                high = roll(even[far, :] + odd[far, :], 32)
                values.append((block, low, high))
            for block, low, high in values:
                weights[pl.ds(pl.multiple_of(base * piece + block * 128, 128), 128), :] = jnp.where(quad, low, high)
                even[pl.ds(pl.multiple_of(base * 2 * piece + block * 128, 128), 128), :] = jnp.where(quad, high, low)
            return carry

        lax.fori_loop(0, piece // 128 // together, split, 0)
        firsts = weights.at[pl.ds(pl.multiple_of(base * piece, 128), piece)]
        seconds = even.at[pl.ds(pl.multiple_of(base * 2 * piece, 128), piece)]
        for c, source in enumerate((firsts, seconds)):
            out = outs[k * 2 + c]
            sends.append(pltpu.make_async_copy(source, out.at[pl.ds(0, piece)], out_sem.at[c, k]))
            sends.append(pltpu.make_async_copy(heads.at[c], out.at[pl.ds(piece, HEAD)], head_sem.at[c, k]))
        for send in sends[-4:]:
            send.start()
    for send in sends:
        send.wait()


def chunk_kernel(which, n_parts, tok_ref, *refs):
    parts, refs = refs[:n_parts], refs[n_parts:]
    prevs, refs = refs[:4], refs[5:]
    outs, refs = refs[:4], refs[4:]
    group_ref, ids_ref, line_ref, flag_ref, id_sem, scores, weights, even, odd, heads, in_sem, *refs = refs
    held, prev_sem, out_sem, head_sem = refs
    lines = even.shape[0]
    piece = lines // 4
    copies = load_parts(parts, which, scores, in_sem)
    fetches = [pltpu.make_async_copy(prevs[k], held.at[k], prev_sem.at[k]) for k in range(4)]
    for fetch in fetches:
        fetch.start()
    copies += place_ids(tok_ref, which, group_ref, ids_ref, line_ref, flag_ref, id_sem)
    for copy in copies[-2:]:
        copy.start()
    clear(even)
    clear(odd)
    for copy in copies:
        copy.wait()
    top = top_of(scores, 32)
    total = spread_weights(scores, weights, group_ref, top, 32)
    add_weights(line_ref, flag_ref, weights, (even, odd))

    for fetch in fetches:
        fetch.wait()
    old_top, old_total = held[0, piece : piece + 1, :], held[0, piece + 1 : piece + 2, :]
    new_top = jnp.maximum(top, old_top)
    scale, old_scale = jnp.exp(top - new_top), jnp.exp(old_top - new_top)
    heads[0] = head_block(new_top, total * scale + old_total * old_scale)
    step = 128
    sends = []
    for k in range(4):
        base = piece_at(k, piece)

        def join(i, carry, base=base, k=k):
            at = pl.ds(pl.multiple_of(base + i * step, step), step)
            old = held[k, pl.ds(pl.multiple_of(i * step, step), step), :]
            even[at, :] = (even[at, :] + odd[at, :]) * scale + old * old_scale
            return carry

        lax.fori_loop(0, piece // step, join, 0)
        source = even.at[pl.ds(pl.multiple_of(base, step), piece)]
        sends.append(pltpu.make_async_copy(source, outs[k].at[pl.ds(0, piece)], out_sem.at[k]))
        sends.append(pltpu.make_async_copy(heads.at[0], outs[k].at[pl.ds(piece, HEAD)], head_sem.at[k]))
        for send in sends[-2:]:
            send.start()
    for send in sends:
        send.wait()


def histogram_call(tok, which, parts, prevs, after, vocab):
    own = not prevs
    rows = sum(part.shape[-2] for part in parts)
    lines = vocab // (2 if own else PACK)
    out = jax.ShapeDtypeStruct((vocab // PACK // 4 + HEAD, 128), F32)
    keys = tok.shape[0]
    tok = tok.reshape(128, 128)
    assert keys == 128 * 128
    count = 8 if own else 4
    dma = pltpu.SemaphoreType.DMA
    extra = [] if own else [*prevs, after]
    return pl.pallas_call(
        functools.partial(own_kernel if own else chunk_kernel, which, len(parts)),
        out_shape=(out,) * count,
        in_specs=[pl.BlockSpec(memory_space=VMEM)]
        + [pl.BlockSpec(memory_space=ANY)] * (len(parts) + len(extra)),
        out_specs=(pl.BlockSpec(memory_space=ANY),) * count,
        scratch_shapes=[VMEM((128, 128), jnp.bfloat16), VMEM((2, 128, 128), jnp.int32)]
        + [SMEM((128, 128), jnp.int32), SMEM((128, 128), jnp.int32), dma((2,))]
        + [VMEM((rows, 128), F32), VMEM((keys, 128), F32), VMEM((lines, 128), F32), VMEM((lines, 128), F32)]
        + [VMEM((2, HEAD, 128), F32), dma((len(parts),))]
        + ([dma((2, 4)), dma((2, 4))] if own else [VMEM((4, lines // 4 + HEAD, 128), F32), dma((4,)), dma((4,)), dma((4,))]),
        compiler_params=pltpu.CompilerParams(vmem_limit_bytes=VMEM_BYTES),
        cost_estimate=pl.CostEstimate(flops=10**6, bytes_accessed=2 * 10**7, transcendentals=0),
        name="own_histogram" if own else "chunk_histogram",
    )(tok, *parts, *extra)


def merge_kernel(a_ref, b_ref, *refs):
    *outs, a_held, b_held, heads, in_sem, out_sem = refs
    lines = a_ref.shape[0] - HEAD
    block = STAGE_BLOCKS * TOK_BLOCK
    steps = lines // block

    def fetch(source, held, which, start, size, index):
        at = pl.ds(start, size)
        return pltpu.make_async_copy(source.at[at], held.at[at], in_sem.at[which, index])

    pairs = [(lines, HEAD)] + [(i * block, block) for i in range(steps)]
    fetches = [
        (fetch(a_ref, a_held, 0, start, size, i), fetch(b_ref, b_held, 1, start, size, i))
        for i, (start, size) in enumerate(pairs)
    ]
    for pair in fetches:
        for copy in pair:
            copy.start()
    sends = []
    for i, (start, size) in enumerate(pairs):
        for copy in fetches[i]:
            copy.wait()
        if i == 0:
            a_top, b_top = a_held[lines : lines + 1, :], b_held[lines : lines + 1, :]
            top = jnp.maximum(a_top, b_top)
            a_scale, b_scale = jnp.exp(a_top - top), jnp.exp(b_top - top)
            total = a_held[lines + 1 : lines + 2, :] * a_scale + b_held[lines + 1 : lines + 2, :] * b_scale
            heads[...] = head_block(top, total)
            source = heads
        else:
            at = slice(start, start + size)
            a_held[at, :] = a_held[at, :] * a_scale + b_held[at, :] * b_scale
            source = a_held.at[pl.ds(start, size)]
        if len(outs) == 1:
            target = outs[0].at[pl.ds(start, size)]
        else:
            first = outs[0].shape[0]
            target = outs[0].at[pl.ds(start, size)] if start < first else outs[1].at[pl.ds(start - first, size)]
        sends.append(pltpu.make_async_copy(source, target, out_sem.at[i]))
        sends[-1].start()
    for send in sends:
        send.wait()


def merge_call(a, b, parted):
    block = STAGE_BLOCKS * TOK_BLOCK
    steps = a.shape[0] // block
    sizes = (a.shape[0] - HEAD - block, block + HEAD) if parted else (a.shape[0],)
    dma = pltpu.SemaphoreType.DMA
    return pl.pallas_call(
        merge_kernel,
        out_shape=tuple(jax.ShapeDtypeStruct((size, 128), F32) for size in sizes),
        in_specs=[pl.BlockSpec(memory_space=ANY)] * 2,
        out_specs=tuple(pl.BlockSpec(memory_space=ANY) for _ in sizes),
        scratch_shapes=[VMEM(a.shape, F32), VMEM(a.shape, F32), VMEM((HEAD, 128), F32), dma((2, steps + 1)), dma((steps + 1,))],
        compiler_params=pltpu.CompilerParams(vmem_limit_bytes=VMEM_BYTES),
        cost_estimate=pl.CostEstimate(flops=10**5, bytes_accessed=3 * a.size * 4, transcendentals=0),
        name="merge",
    )(a, b)


def head_kernel(q_ref, w_ref, after_ref, logits_ref, stat_ref, top_ref, sum_ref):
    del after_ref
    i = pl.program_id(0)

    @pl.when(i == 0)
    def _():
        top_ref[...] = jnp.full(top_ref.shape, -jnp.inf, F32)
        sum_ref[...] = jnp.zeros(sum_ref.shape, F32)

    rows = logits_ref.shape[0]
    mine = q_ref[pl.ds(pl.multiple_of(lax.axis_index("store") * rows, rows), rows), :]
    logits = jnp.dot(mine, w_ref[...], preferred_element_type=F32)
    logits_ref[...] = logits
    old = top_ref[...]
    new = jnp.maximum(old, jnp.max(logits, axis=1, keepdims=True))
    part = jnp.sum(jnp.exp(logits - new[:, 0:1]), axis=1, keepdims=True)
    sum_ref[...] = sum_ref[...] * jnp.exp(old - new) + part
    top_ref[...] = new
    stat_ref[0] = top_ref[...]
    stat_ref[1] = sum_ref[...]


def head_call(queries, w_head, after):
    width = queries.shape[1]
    count = queries.shape[0] // 2
    cols = w_head.shape[1]
    block = cols // 10
    return pl.pallas_call(
        head_kernel,
        grid=(cols // block,),
        out_shape=(jax.ShapeDtypeStruct((count, cols), F32), jax.ShapeDtypeStruct((2, count, 128), F32)),
        in_specs=[
            pl.BlockSpec((2 * count, width), lambda i: (0, 0)),
            pl.BlockSpec((width, block), lambda i: (0, i)),
            pl.BlockSpec(memory_space=ANY),
        ],
        out_specs=(pl.BlockSpec((count, block), lambda i: (0, i)), pl.BlockSpec((2, count, 128), lambda i: (0, 0, 0))),
        scratch_shapes=[VMEM((count, 128), F32), VMEM((count, 128), F32)],
        compiler_params=pltpu.CompilerParams(vmem_limit_bytes=VMEM_BYTES),
        cost_estimate=pl.CostEstimate(flops=2 * count * width * cols, bytes_accessed=2 * width * cols, transcendentals=0),
        name="head",
    )(queries, w_head, after)


def mix_kernel(index, n_far, n_prev, mix_ref, stat_ref, logits_ref, *refs):
    pieces, refs = refs[: 2 + n_far], refs[2 + n_far + n_prev :]
    out_ref, held, heads, logits, result, in_sem, head_sem, logits_sem, out_sem = refs
    order = ORDERS[index]
    block = STAGE_BLOCKS * TOK_BLOCK
    steps = held.shape[1] // block
    wide = block * PACK
    rows = pl.ds(index * 32, 32)

    def sources(start, size):
        first = pieces[2].shape[0]
        far = pieces[2].at[pl.ds(start, size)] if start < first else pieces[3].at[pl.ds(start - first, size)]
        return [pieces[0].at[pl.ds(start, size)], pieces[1].at[pl.ds(start, size)], far]

    head_copies = [
        pltpu.make_async_copy(source, heads.at[p], head_sem.at[p])
        for p, source in enumerate(sources(steps * block, HEAD))
    ]
    for copy in head_copies:
        copy.start()
    copies = []
    for i in range(steps):
        at = pl.ds(i * block, block)
        cols = pl.ds(i * wide, wide)
        group = [
            pltpu.make_async_copy(source, held.at[p, at], in_sem.at[i, p])
            for p, source in enumerate(sources(i * block, block))
        ]
        group.append(pltpu.make_async_copy(logits_ref.at[rows, cols], logits.at[:, cols], logits_sem.at[i]))
        for copy in group:
            copy.start()
        copies.append(group)
    for copy in head_copies:
        copy.wait()
    mix = mix_ref[0]
    tops = [heads[p, 0:1, :] for p in range(3)]
    top = jnp.maximum(jnp.maximum(tops[0], tops[1]), tops[2])
    scales = [jnp.exp(value - top) for value in tops]
    total = sum(heads[p, 1:2, :] * scales[p] for p in range(3))
    scales = [scale * mix / total for scale in scales]
    lm_top = stat_ref[0, index * 32 : index * 32 + 32, :]
    lm_scale = (1.0 - mix) / stat_ref[1, index * 32 : index * 32 + 32, :]
    sends = []
    for i in range(steps):
        for copy in copies[i]:
            copy.wait()
        for b in range(i * STAGE_BLOCKS, (i + 1) * STAGE_BLOCKS):
            at = slice(b * TOK_BLOCK, (b + 1) * TOK_BLOCK)
            turned = sum(held[p, at, :] * scales[p] for p in range(3)).T
            for g in range(PACK):
                run = order[g]
                cols = slice((b * PACK + run) * TOK_BLOCK, (b * PACK + run + 1) * TOK_BLOCK)
                lm = jnp.exp(logits[:, cols] - lm_top) * lm_scale
                result[:, cols] = jnp.log(turned[g * 32 : (g + 1) * 32, :] + lm)
        cols = pl.ds(i * wide, wide)
        sends.append(pltpu.make_async_copy(result.at[:, cols], out_ref.at[rows, cols], out_sem.at[i]))
        sends[-1].start()
    for send in sends:
        send.wait()


def mix_call(mix, pieces, logits, stat, index, prev):
    lines = pieces[0].shape[0] - HEAD
    steps = lines // (STAGE_BLOCKS * TOK_BLOCK)
    count, cols = logits.shape
    n_prev = 0 if prev is None else 1
    dma = pltpu.SemaphoreType.DMA
    return pl.pallas_call(
        functools.partial(mix_kernel, index, len(pieces) - 2, n_prev),
        out_shape=jax.ShapeDtypeStruct((count, cols), F32),
        in_specs=[pl.BlockSpec(memory_space=SMEM), pl.BlockSpec(memory_space=VMEM)]
        + [pl.BlockSpec(memory_space=ANY)] * (1 + len(pieces) + n_prev),
        out_specs=pl.BlockSpec(memory_space=ANY),
        scratch_shapes=[VMEM((3, lines, 128), F32), VMEM((3, HEAD, 128), F32), VMEM((32, cols), F32), VMEM((32, cols), F32)]
        + [dma((steps, 3)), dma((3,)), dma((steps,)), dma((steps,))],
        input_output_aliases={3 + len(pieces): 0} if n_prev else {},
        compiler_params=pltpu.CompilerParams(vmem_limit_bytes=VMEM_BYTES),
        cost_estimate=pl.CostEstimate(flops=10**5, bytes_accessed=8 * 10**6, transcendentals=0),
        name="mix",
    )(mix, stat, logits, *pieces, *([prev] if n_prev else []))


CHUNKS = (5120, 11264)


def solution(mesh):
    store_devs = mesh.shape["store"]
    model_devs = mesh.shape["model"]
    assert store_devs == 2 and model_devs == 4
    group_axes = ("store", "model")
    across_y = [(0, 1), (1, 0)]
    across_core = [(0, 1), (1, 0), (2, 3), (3, 2)]
    across_x = [(0, 2), (2, 0), (1, 3), (3, 1)]

    def swap_y(value):
        return lax.ppermute(value, "store", across_y)

    def swap_core(value):
        return lax.ppermute(value, "model", across_core)

    def swap_x(value):
        return lax.ppermute(value, "model", across_x)

    def local_step(queries, w_head, store_keys, store_tok, temperature, mix_weight):
        vocab = w_head.shape[1] * model_devs
        tau = temperature.reshape(1)
        mix = mix_weight.reshape(1)

        their_tok = swap_y(store_tok)
        own, first, second = [], [], []
        start = 0
        for index, count in enumerate(CHUNKS):
            joined = index == 0
            kept, *sent = score_call(tau, queries, store_keys, start, count, joined)
            own.append(kept)
            first.append(swap_y(sent[0]))
            if joined:
                second.append(first[-1])
            else:
                second.append(swap_y(sent[1]))
            start += count

        kept = histogram_call(store_tok, None, own, [], None, vocab)
        nears, fars = [], []
        after = kept[0]
        for index, parts in enumerate((first, second)):
            out = histogram_call(their_tok, index, parts, kept[index::2], after, vocab)
            far = swap_core(out[0])
            near = swap_core(out[2])
            sums = merge_call(out[1], far, index == 1)
            if index == 0:
                after = sums[0]
                fars.append([swap_x(sums[0])])
            else:
                fars.append([swap_x(sums[0])])
            nears.append([out[3], near])
        logits, stat = head_call(queries, w_head, sums[0])
        for swap in (swap_core, swap_x):
            other = swap(stat)
            top = jnp.maximum(stat[0], other[0])
            stat = jnp.stack([top, stat[1] * jnp.exp(stat[0] - top) + other[1] * jnp.exp(other[0] - top)])
        fars[1].append(swap_x(sums[1]))
        result = None
        for index in range(2):
            result = mix_call(mix, nears[index] + fars[index], logits, stat, index, result)
        return result

    return jax.shard_map(
        local_step,
        mesh=mesh,
        in_specs=(P("data", None), P(None, "model"), P(group_axes, None), P(group_axes), P(), P()),
        out_specs=P(("data", "store"), "model"),
        check_vma=False,
    )
```

time: 301 us -> 279 us (0.927)
  Pallas kernels: 190 us -> 179 us
  waiting for transfers between devices: 80.5 us -> 72.9 us
    pallas_call x10 -> x9, Pallas kernels: 164 us -> 153 us  [the longest x3 90.2 us: histogram_call(): pl.pallas_call(functools.partial(own_kernel if own else chunk_kernel, whi...]
    ppermute x3 -> x4, waiting for transfers between devices: 37.9 us -> 33.2 us  [swap_x(): return lax.ppermute(value, 'model', across_x)]
    ppermute x7 -> x4, waiting for transfers between devices: 41.2 us -> 37.2 us  [swap_y(): return lax.ppermute(value, 'store', across_y)]
    ppermute x7 -> x4, starting transfers between devices: 9.44 us -> 7.76 us  [swap_y(): return lax.ppermute(value, 'store', across_y)]
    ppermute x3 -> x4, starting transfers between devices: 9.49 us -> 10.2 us  [swap_x(): return lax.ppermute(value, 'model', across_x)]
  transfers between devices with their start and end apart: 15 -> 13, of which waited for: 3 -> 6; matrix products, arithmetic and copies ran while one was open for 1% -> 1% of each run, Pallas kernels for 34% -> 31%
where the time goes in v3:
time: 279 us; the launch traced here: 278 us
  Pallas kernels  179 us (64%)
  waiting for transfers between devices  72.9 us (26%)
  starting transfers between devices  21.8 us (8%)
    pallas_call x3, Pallas kernels, histogram_call(): pl.pallas_call(functools.partial(own_kernel if own else chunk_kernel, whi...  90.2 us
    pallas_call x2, Pallas kernels, score_call(): pl.pallas_call(score_kernel, grid=(count // KEY_BLOCK,), out_shape=(jax.S...  47.1 us
    ppermute x4, waiting for transfers between devices, swap_y(): return lax.ppermute(value, 'store', across_y)  37.2 us
    ppermute x4, waiting for transfers between devices, swap_x(): return lax.ppermute(value, 'model', across_x)  33.2 us
    pallas_call x1, Pallas kernels, head_call(): pl.pallas_call(head_kernel, grid=(cols // block,), out_shape=(jax.ShapeDt...  25.7 us
    pallas_call x2, Pallas kernels, mix_call(): pl.pallas_call(functools.partial(mix_kernel, index, len(pieces) - 2, n_pr...  10.4 us
    ppermute x4, starting transfers between devices, swap_x(): return lax.ppermute(value, 'model', across_x)  10.2 us
    ppermute x4, starting transfers between devices, swap_y(): return lax.ppermute(value, 'store', across_y)  7.76 us
  transfers between devices with their start and end apart: 13, of which 6 were waited for; matrix products, arithmetic and copies ran while one was open for 1% of the time, Pallas kernels for 31%

profile of v3, /device:TPU:0, one launch (start us, length us, event | category | flops | bytes accessed | tf_op | source)
XLA Modules:
  0.0 277.9 jit_solution(5093923764144628697)
XLA Ops:
  0.7 31.1 %scores.3 = (f32[5632,128]{1,0:T(8,128)}, f32[2816,128]{1,0:T(8,128)}, f32[2816,128]{1,0:T(8,128)}) custom-call(f32[1]{0:T(128)} %bitcast.5.tau_ref, bf16[128,2560]{1,0:T(8,128)(2,1)} %q_ref.1, bf16[16384,2560]{1,0:T(8,128)(2,1)} %k_ref.3), custom_call_target="tpu_custom_call" | custom-call | flops 7381975040 | bytes 57671680 | tf_op jit(solution)/shard_map/scores/pallas_call | solution.py:83
  31.8 3.3 %collective-permute-start.3 = (f32[2816,128]{1,0:T(8,128)}, f32[2816,128]{1,0:T(8,128)}, u32[]{:S(2)}, u32[]{:S(2)}) collective-permute-start(f32[2816,128]{1,0:T(8,128)} %get-tuple-element.38), channel_id=1, source_target_pairs={{0,4},{4,0},{1,5},{5,1},{2,6},{6,2},{3,7},{7,3}} | collective-permute-start | bytes 4325384 | tf_op jit(solution)/shard_map/ppermute | solution.py:569
  35.1 0.0 copy-start.2
  35.1 16.0 %scores.2 = (f32[2560,128]{1,0:T(8,128)}, f32[2,1280,128]{2,1,0:T(8,128)}) custom-call(f32[1]{0:T(128)} %bitcast.4.tau_ref, bf16[128,2560]{1,0:T(8,128)(2,1)} %q_ref.1, bf16[16384,2560]{1,0:T(8,128)(2,1)} %k_ref.3), custom_call_target="tpu_custom_call" | custom-call | flops 3355443200 | bytes 26214400 | tf_op jit(solution)/shard_map/scores/pallas_call | solution.py:83
  51.1 0.0 collective-permute-start.1
  51.1 0.0 copy-done.2
  51.1 2.0 collective-permute-start
  53.1 34.7 %own_histogram.1 = (f32[3208,128]{1,0:T(8,128)}, f32[3208,128]{1,0:T(8,128)}, f32[3208,128]{1,0:T(8,128)}, f32[3208,128]{1,0:T(8,128)}, f32[3208,128]{1,0:T(8,12...) custom-call(s32[128,128]{1,0:T(8,128)} %bitcast.10, f32[2560,128]{1,0:T(8,128)} %get-tuple-element.32.refs_0_, ...), custom_call_target="tpu_custom_call" | custom-call | flops 1000000 | bytes 20000000 | tf_op jit(solution)/shard_map/own_histogram/pallas_call | solution.py:352
  87.8 8.6 %collective-permute-done = s32[16384]{0:T(1024)S(1)} collective-permute-done((s32[16384]{0:T(1024)S(1)}, s32[16384]{0:T(1024)S(1)}, u32[]{:S(2)}, u32[]{:S(2)}) %collective-permute-start) | collective-permute-done | bytes 65568 | tf_op jit(solution)/shard_map/ppermute | solution.py:569
  96.4 0.0 copy-start.1
  96.4 0.0 collective-permute-done.1.refs_0_
  96.4 0.0 collective-permute-done.3.refs_1_
  96.4 0.6 copy-done.1
  97.0 27.8 %chunk_histogram.2 = (f32[3208,128]{1,0:T(8,128)}, f32[3208,128]{1,0:T(8,128)}, f32[3208,128]{1,0:T(8,128)}, f32[3208,128]{1,0:T(8,128)}) custom-call(s32[128,128]{1,0:T(8,128)} %bitcast.8, f32[2,1280,128]{2,1,0:T(8,128)} %collective-permute-done.1.refs_0_, f32[2816,128]{1,0:T(8,128)} %collective-permute-done.3.refs_1_, ...), custom_call_target="tpu_custom_call" | custom-call | flops 1000000 | bytes 20000000 | tf_op jit(solution)/shard_map/chunk_histogram/pallas_call | solution.py:352
  124.8 1.5 collective-permute-start.4
  126.3 2.4 collective-permute-start.2
  128.7 1.1 collective-permute-done.4.b_ref
  129.8 2.8 %merge.2.refs_6_ = f32[3208,128]{1,0:T(8,128)} custom-call(f32[3208,128]{1,0:T(8,128)} %get-tuple-element.43.a_ref, f32[3208,128]{1,0:T(8,128)} %collective-permute-done.4.b_ref), custom_call_target="tpu_custom_call" | custom-call | flops 100000 | bytes 4927488 | tf_op jit(solution)/shard_map/merge/pallas_call | solution.py:418
  132.6 28.7 %collective-permute-done.2.refs_1_ = f32[2816,128]{1,0:T(8,128)} collective-permute-done((f32[2816,128]{1,0:T(8,128)}, f32[2816,128]{1,0:T(8,128)}, u32[]{:S(2)}, u32[]{:S(2)}) %collective-permute-start.2) | collective-permute-done | bytes 1441824 | tf_op jit(solution)/shard_map/ppermute | solution.py:569
  161.2 27.7 %chunk_histogram.3 = (f32[3208,128]{1,0:T(8,128)}, f32[3208,128]{1,0:T(8,128)}, f32[3208,128]{1,0:T(8,128)}, f32[3208,128]{1,0:T(8,128)}) custom-call(s32[128,128]{1,0:T(8,128)} %bitcast.9, f32[2,1280,128]{2,1,0:T(8,128)} %collective-permute-done.1.refs_0_, f32[2816,128]{1,0:T(8,128)} %collective-permute-done.2.refs_1_, ...), custom_call_target="tpu_custom_call" | custom-call | flops 1000000 | bytes 20000000 | tf_op jit(solution)/shard_map/chunk_histogram/pallas_call | solution.py:352
  188.9 2.0 collective-permute-start.5
  190.9 0.0 collective-permute-start.11
  191.0 5.1 %collective-permute-start.12 = (f32[3208,128]{1,0:T(8,128)}, f32[3208,128]{1,0:T(8,128)}, u32[]{:S(2)}, u32[]{:S(2)}) collective-permute-start(f32[3208,128]{1,0:T(8,128)} %merge.2.refs_6_), channel_id=1, source_target_pairs={{0,2},{2,0},{1,3},{3,1},{4,6},{6,4},{5,7},{7,5}} | collective-permute-start | bytes 4927496 | tf_op jit(solution)/shard_map/ppermute | solution.py:575
  196.1 0.2 collective-permute-start.8
  196.3 0.0 collective-permute-done.5.b_ref
  196.3 2.8 %merge.3 = (f32[2560,128]{1,0:T(8,128)}, f32[648,128]{1,0:T(8,128)}) custom-call(f32[3208,128]{1,0:T(8,128)} %get-tuple-element.45.a_ref, f32[3208,128]{1,0:T(8,128)} %collective-permute-done.5.b_ref), custom_call_target="tpu_custom_call" | custom-call | flops 100000 | bytes 4927488 | tf_op jit(solution)/shard_map/merge/pallas_call | solution.py:418
  199.1 0.0 copy-start.3
  199.1 3.3 %collective-permute-start.9 = (f32[2560,128]{1,0:T(8,128)}, f32[2560,128]{1,0:T(8,128)}, u32[]{:S(2)}, u32[]{:S(2)}) collective-permute-start(f32[2560,128]{1,0:T(8,128)} %get-tuple-element.47.after_ref), channel_id=1, source_target_pairs={{0,2},{2,0},{1,3},{3,1},{4,6},{6,4},{5,7},{7,5}} | collective-permute-start | bytes 3932168 | tf_op jit(solution)/shard_map/ppermute | solution.py:575
  202.4 25.7 %head.1 = (f32[64,12800]{1,0:T(8,128)}, f32[2,64,128]{2,1,0:T(8,128)}) custom-call(bf16[128,2560]{1,0:T(8,128)(2,1)} %q_ref.1, bf16[2560,12800]{1,0:T(8,128)(2,1)} %w_ref.1, f32[2560,128]{1,0:T(8,128)} %get-tuple-element.47.after_ref), custom_call_target="tpu_custom_call" | custom-call | flops 4194304000 | bytes 65536000 | tf_op jit(solution)/shard_map/head/pallas_call | solution.py:457
  228.1 0.1 collective-permute-start.6
  228.2 1.4 collective-permute-done.6
  229.5 0.8 fusion.1
  230.4 0.1 collective-permute-start.7
  231.1 31.2 %collective-permute-done.7 = f32[2,64,128]{2,1,0:T(8,128)S(1)} collective-permute-done((f32[2,64,128]{2,1,0:T(8,128)S(1)}, f32[2,64,128]{2,1,0:T(8,128)S(1)}, u32[]{:S(2)}, u32[]{:S(2)}) %collective-permute-start.7) | collective-permute-done | bytes 65568 | tf_op jit(solution)/shard_map/ppermute | solution.py:575
  262.3 0.0 copy-done.3
  262.3 1.7 collective-permute-start.10
  264.1 0.6 pad_maximum_fusion.1.stat_ref
  264.7 0.0 collective-permute-done.11.refs_1_
  264.7 0.0 collective-permute-done.12.refs_2_
  264.8 5.2 %mix.2.refs_4_ = f32[64,12800]{1,0:T(8,128)} custom-call(f32[1]{0:T(128)} %bitcast.6.mix_ref, f32[2,64,128]{2,1,0:T(8,128)} %pad_maximum_fusion.1.stat_ref, f32[64,12800]{1,0:T(8,128)} %get-tuple-element.49.logits_ref, f32[3208,128]{1,0:T(8,128)} %get-tuple-element.53.refs_0_, f32[3208,128]{1,0:T(8,128)} %collective-permute-done.11.refs_1_, ...), custom_call_target="tpu_custom_call" | custom-call | flops 100000 | bytes 8000000 | tf_op jit(solution)/shard_map/mix/pallas_call | solution.py:541
  270.0 0.0 collective-permute-done.8.refs_1_
  270.0 2.0 collective-permute-done.10.refs_3_
  271.9 0.0 copy-start
  271.9 0.0 collective-permute-done.9.refs_2_
  272.0 0.7 copy-done
  272.7 5.2 %mix.3 = f32[64,12800]{1,0:T(8,128)} custom-call(f32[1]{0:T(128)} %bitcast.7.mix_ref, f32[2,64,128]{2,1,0:T(8,128)} %pad_maximum_fusion.1.stat_ref, f32[64,12800]{1,0:T(8,128)} %get-tuple-element.49.logits_ref, f32[3208,128]{1,0:T(8,128)} %get-tuple-element.50.refs_0_, f32[3208,128]{1,0:T(8,128)} %collective-permute-done.8.refs_1_, ...), custom_call_target="tpu_custom_call", output_to_operand_aliasing={{}: (7, {})} | custom-call | flops 100000 | bytes 8000000 | tf_op jit(solution)/shard_map/mix/pallas_call | solution.py:541
  (2 shorter events, 0.0 us)
Async XLA Ops:
  31.8 64.6 %collective-permute-start.3 = (f32[2816,128]{1,0:T(8,128)}, f32[2816,128]{1,0:T(8,128)}, u32[]{:S(2)}, u32[]{:S(2)}) collective-permute-start(f32[2816,128]{1,0:T(8,128)} %get-tuple-element.38), channel_id=1, source_target_pairs={{0,4},{4,0},{1,5},{5,1},{2,6},{6,2},{3,7},{7,3}} | collective-permute-start | bytes 4325384 | tf_op jit(solution)/shard_map/ppermute | solution.py:569
  35.1 16.0 %copy-start.2 = (s32[16384]{0:T(1024)S(1)}, s32[16384]{0:T(1024)}, u32[]{:S(2)}) copy-start(s32[16384]{0:T(1024)} %param.9) | copy-start | bytes 196612
  51.1 45.3 %collective-permute-start.1 = (f32[2,1280,128]{2,1,0:T(8,128)}, f32[2,1280,128]{2,1,0:T(8,128)}, u32[]{:S(2)}, u32[]{:S(2)}) collective-permute-start(f32[2,1280,128]{2,1,0:T(8,128)} %get-tuple-element.30), channel_id=1, source_target_pairs={{0,4},{4,0},{1,5},{5,1},{2,6},{6,2},{3,7},{7,3}} | collective-permute-start | bytes 3932168 | tf_op jit(solution)/shard_map/ppermute | solution.py:569
  51.1 45.3 %collective-permute-start = (s32[16384]{0:T(1024)S(1)}, s32[16384]{0:T(1024)S(1)}, u32[]{:S(2)}, u32[]{:S(2)}) collective-permute-start(s32[16384]{0:T(1024)S(1)} %copy-done.2), channel_id=1, source_target_pairs={{0,4},{4,0},{1,5},{5,1},{2,6},{6,2},{3,7},{7,3}} | collective-permute-start | bytes 196616 | tf_op jit(solution)/shard_map/ppermute | solution.py:569
  96.4 0.6 copy-start.1
  124.8 5.0 %collective-permute-start.4 = (f32[3208,128]{1,0:T(8,128)}, f32[3208,128]{1,0:T(8,128)}, u32[]{:S(2)}, u32[]{:S(2)}) collective-permute-start(f32[3208,128]{1,0:T(8,128)} %get-tuple-element.44), channel_id=1, source_target_pairs={{0,1},{1,0},{2,3},{3,2},{4,5},{5,4},{6,7},{7,6}} | collective-permute-start | bytes 4927496 | tf_op jit(solution)/shard_map/ppermute | solution.py:572
  126.3 35.0 %collective-permute-start.2 = (f32[2816,128]{1,0:T(8,128)}, f32[2816,128]{1,0:T(8,128)}, u32[]{:S(2)}, u32[]{:S(2)}) collective-permute-start(f32[2816,128]{1,0:T(8,128)} %get-tuple-element.31), channel_id=1, source_target_pairs={{0,4},{4,0},{1,5},{5,1},{2,6},{6,2},{3,7},{7,3}} | collective-permute-start | bytes 4325384 | tf_op jit(solution)/shard_map/ppermute | solution.py:569
  188.9 7.4 %collective-permute-start.5 = (f32[3208,128]{1,0:T(8,128)}, f32[3208,128]{1,0:T(8,128)}, u32[]{:S(2)}, u32[]{:S(2)}) collective-permute-start(f32[3208,128]{1,0:T(8,128)} %get-tuple-element.46), channel_id=1, source_target_pairs={{0,1},{1,0},{2,3},{3,2},{4,5},{5,4},{6,7},{7,6}} | collective-permute-start | bytes 4927496 | tf_op jit(solution)/shard_map/ppermute | solution.py:572
  190.9 73.8 %collective-permute-start.11 = (f32[3208,128]{1,0:T(8,128)}, f32[3208,128]{1,0:T(8,128)}, u32[]{:S(2)}, u32[]{:S(2)}) collective-permute-start(f32[3208,128]{1,0:T(8,128)} %get-tuple-element.54), channel_id=1, source_target_pairs={{0,1},{1,0},{2,3},{3,2},{4,5},{5,4},{6,7},{7,6}} | collective-permute-start | bytes 4927496 | tf_op jit(solution)/shard_map/ppermute | solution.py:572
  191.0 73.8 %collective-permute-start.12 = (f32[3208,128]{1,0:T(8,128)}, f32[3208,128]{1,0:T(8,128)}, u32[]{:S(2)}, u32[]{:S(2)}) collective-permute-start(f32[3208,128]{1,0:T(8,128)} %merge.2.refs_6_), channel_id=1, source_target_pairs={{0,2},{2,0},{1,3},{3,1},{4,6},{6,4},{5,7},{7,5}} | collective-permute-start | bytes 4927496 | tf_op jit(solution)/shard_map/ppermute | solution.py:575
  196.1 73.9 %collective-permute-start.8 = (f32[3208,128]{1,0:T(8,128)}, f32[3208,128]{1,0:T(8,128)}, u32[]{:S(2)}, u32[]{:S(2)}) collective-permute-start(f32[3208,128]{1,0:T(8,128)} %get-tuple-element.51), channel_id=1, source_target_pairs={{0,1},{1,0},{2,3},{3,2},{4,5},{5,4},{6,7},{7,6}} | collective-permute-start | bytes 4927496 | tf_op jit(solution)/shard_map/ppermute | solution.py:572
  199.1 63.2 %copy-start.3 = (f32[648,128]{1,0:T(8,128)S(1)}, f32[648,128]{1,0:T(8,128)}, u32[]{:S(2)}) copy-start(f32[648,128]{1,0:T(8,128)} %get-tuple-element.52) | copy-start | bytes 995332
  199.1 72.8 %collective-permute-start.9 = (f32[2560,128]{1,0:T(8,128)}, f32[2560,128]{1,0:T(8,128)}, u32[]{:S(2)}, u32[]{:S(2)}) collective-permute-start(f32[2560,128]{1,0:T(8,128)} %get-tuple-element.47.after_ref), channel_id=1, source_target_pairs={{0,2},{2,0},{1,3},{3,1},{4,6},{6,4},{5,7},{7,5}} | collective-permute-start | bytes 3932168 | tf_op jit(solution)/shard_map/ppermute | solution.py:575
  228.1 1.5 collective-permute-start.6
  230.4 32.0 %collective-permute-start.7 = (f32[2,64,128]{2,1,0:T(8,128)S(1)}, f32[2,64,128]{2,1,0:T(8,128)S(1)}, u32[]{:S(2)}, u32[]{:S(2)}) collective-permute-start(f32[2,64,128]{2,1,0:T(8,128)S(1)} %pad_maximum_fusion), channel_id=1, source_target_pairs={{0,2},{2,0},{1,3},{3,1},{4,6},{6,4},{5,7},{7,5}} | collective-permute-start | bytes 196616 | tf_op jit(solution)/shard_map/ppermute | solution.py:575
  262.3 9.6 %collective-permute-start.10 = (f32[648,128]{1,0:T(8,128)S(1)}, f32[648,128]{1,0:T(8,128)S(1)}, u32[]{:S(2)}, u32[]{:S(2)}) collective-permute-start(f32[648,128]{1,0:T(8,128)S(1)} %copy-done.3), channel_id=1, source_target_pairs={{0,2},{2,0},{1,3},{3,1},{4,6},{6,4},{5,7},{7,5}} | collective-permute-start | bytes 995336 | tf_op jit(solution)/shard_map/ppermute | solution.py:575
  271.9 0.7 copy-start

commit v4 on v3

--- a/solution.py
+++ b/solution.py
@@ -13,9 +13,11 @@
 VMEM = pltpu.VMEM
 SMEM = pltpu.SMEM
 KEY_BLOCK = 1024
+LANES = 128
 VMEM_BYTES = 63 * 2**20
 BATCH_KEYS = 8
-FLAG_KEYS = 128
+FLAG_KEYS = 32
+STEP_ROWS = 2
 PACK = 4
 TOK_BLOCK = 128
 ORDERS = ((0, 2, 1, 3), (3, 0, 2, 1))
@@ -24,7 +26,7 @@
 
 
 def lane_group(width):
-    return lax.broadcasted_iota(jnp.int32, (1, 128), 1) // width
+    return lax.broadcasted_iota(jnp.int32, (1, LANES), 1) // width
 
 
 def pick(group, parts):
@@ -35,7 +37,7 @@
 
 
 def roll(value, shift):
-    return pltpu.roll(value, shift % 128, 1)
+    return pltpu.roll(value, shift % LANES, 1)
 
 
 def score_kernel(tau_ref, rows_ref, k_ref, own_ref, *sent):
@@ -51,12 +53,12 @@
         q_ref[half : 2 * half, :] = rows_ref[pl.ds(pl.multiple_of((1 - y) * half, half), half), :]
 
     dots = lax.dot_general(k_ref[...], q_ref[...], (((1,), (1,)), ((), ())), preferred_element_type=F32)
-    step = 128
+    step = LANES
     norms = []
     for row in range(0, KEY_BLOCK, step):
-        acc = jnp.zeros((step, 128), F32)
-        for col in range(0, k_ref.shape[1], 128):
-            part = k_ref[row : row + step, col : col + 128].astype(F32)
+        acc = jnp.zeros((step, LANES), F32)
+        for col in range(0, k_ref.shape[1], LANES):
+            part = k_ref[row : row + step, col : col + LANES].astype(F32)
             acc += part * part
         norms.append(jnp.sum(acc, axis=1, keepdims=True))
     group = lane_group(32)
@@ -75,45 +77,45 @@
     base = start // KEY_BLOCK
     half, quarter = KEY_BLOCK // 2, KEY_BLOCK // 4
     if joined:
-        sent_shape = (jax.ShapeDtypeStruct((2, count // 4, 128), F32),)
-        sent_spec = (pl.BlockSpec((2, quarter, 128), lambda i: (0, i, 0)),)
+        sent_shape = (jax.ShapeDtypeStruct((2, count // 4, LANES), F32),)
+        sent_spec = (pl.BlockSpec((2, quarter, LANES), lambda i: (0, i, 0)),)
     else:
-        sent_shape = (jax.ShapeDtypeStruct((count // 4, 128), F32),) * 2
-        sent_spec = (pl.BlockSpec((quarter, 128), lambda i: (i, 0)),) * 2
+        sent_shape = (jax.ShapeDtypeStruct((count // 4, LANES), F32),) * 2
+        sent_spec = (pl.BlockSpec((quarter, LANES), lambda i: (i, 0)),) * 2
     return pl.pallas_call(
         score_kernel,
         grid=(count // KEY_BLOCK,),
-        out_shape=(jax.ShapeDtypeStruct((count // 2, 128), F32),) + sent_shape,
+        out_shape=(jax.ShapeDtypeStruct((count // 2, LANES), F32),) + sent_shape,
         in_specs=[
             pl.BlockSpec(memory_space=SMEM),
-            pl.BlockSpec((128, width), lambda i: (0, 0)),
+            pl.BlockSpec((LANES, width), lambda i: (0, 0)),
             pl.BlockSpec((KEY_BLOCK, width), lambda i: (i + base, 0)),
         ],
-        out_specs=(pl.BlockSpec((half, 128), lambda i: (i, 0)),) + sent_spec,
-        scratch_shapes=[VMEM((128, width), jnp.bfloat16)],
+        out_specs=(pl.BlockSpec((half, LANES), lambda i: (i, 0)),) + sent_spec,
+        scratch_shapes=[VMEM((LANES, width), jnp.bfloat16)],
         compiler_params=pltpu.CompilerParams(vmem_limit_bytes=VMEM_BYTES),
-        cost_estimate=pl.CostEstimate(flops=2 * count * width * 128, bytes_accessed=2 * count * width, transcendentals=0),
+        cost_estimate=pl.CostEstimate(flops=2 * count * width * LANES, bytes_accessed=2 * count * width, transcendentals=0),
         name="scores",
     )(tau, queries, keys)
 
 
 def place_ids(tok_ref, which, group_ref, ids_ref, line_ref, flag_ref, sem):
-    assert PACK == 4 and TOK_BLOCK == 128
+    assert PACK == 4 and TOK_BLOCK == LANES
     tok = tok_ref[...]
     block, run, within = tok >> 9, (tok >> 7) & 3, tok & 127
     if which is None:
-        line = block * 256 + (run >> 1) * 128 + within
+        line = block * 256 + (run >> 1) * LANES + within
         group = run & 1
     else:
-        line = block * 128 + within
+        line = block * LANES + within
         group = sum(jnp.where(run == ORDERS[which][g], g, 0) for g in range(PACK))
-    lane = lax.broadcasted_iota(jnp.int32, (1, 128), 1)
+    lane = lax.broadcasted_iota(jnp.int32, (1, LANES), 1)
     meet = jnp.zeros(tok.shape, F32)
     for shift in range(1, BATCH_KEYS):
         same = (line == roll(line, shift)) & (lane % BATCH_KEYS >= shift)
         meet = jnp.where(same, 1.0, meet)
-    rows = lax.broadcasted_iota(jnp.int32, (128, 128), 0) // FLAG_KEYS
-    shared = (rows == lax.broadcasted_iota(jnp.int32, (128, 128), 1) // FLAG_KEYS).astype(F32)
+    rows = lax.broadcasted_iota(jnp.int32, (LANES, LANES), 0) // FLAG_KEYS
+    shared = (rows == lax.broadcasted_iota(jnp.int32, (LANES, LANES), 1) // FLAG_KEYS).astype(F32)
     ids_ref[0] = line
     ids_ref[1] = jnp.dot(meet, shared, preferred_element_type=F32).astype(jnp.int32)
     group_ref[...] = group.astype(F32).T.astype(jnp.bfloat16)
@@ -138,14 +140,14 @@
     step = 512
 
     def body(i, carry):
-        hist[pl.ds(pl.multiple_of(i * step, step), step), :] = jnp.zeros((step, 128), F32)
+        hist[pl.ds(pl.multiple_of(i * step, step), step), :] = jnp.zeros((step, LANES), F32)
         return carry
 
     lax.fori_loop(0, hist.shape[0] // step, body, 0)
 
 
 def across(value, width, combine):
-    while width < 128:
+    while width < LANES:
         value = combine(value, roll(value, width))
         width *= 2
     return value
@@ -156,17 +158,17 @@
 
     def body(i, best):
         block = scores[pl.ds(pl.multiple_of(i * step, step), step), :]
-        return jnp.maximum(best, jnp.max(block.reshape(step // 8, 8, 128), axis=0))
-
-    best = lax.fori_loop(0, scores.shape[0] // step, body, jnp.full((8, 128), -jnp.inf, F32))
+        return jnp.maximum(best, jnp.max(block.reshape(step // 8, 8, LANES), axis=0))
+
+    best = lax.fori_loop(0, scores.shape[0] // step, body, jnp.full((8, LANES), -jnp.inf, F32))
     return across(jnp.max(best, axis=0, keepdims=True), width, jnp.maximum)
 
 
 def spread_weights(scores, weights, group_ref, top, width):
-    count = 128 // width
+    count = LANES // width
     group = lane_group(width)
-    spread_lane = lax.broadcasted_iota(jnp.int32, (128, 128), 1) // width
-    spread_row = lax.broadcasted_iota(jnp.int32, (128, 128), 0)
+    spread_lane = lax.broadcasted_iota(jnp.int32, (LANES, LANES), 1) // width
+    spread_row = lax.broadcasted_iota(jnp.int32, (LANES, LANES), 0)
     together = 4
 
     def body(i, total):
@@ -175,23 +177,21 @@
             select = (spread_row == block * count + spread_lane).astype(F32).astype(jnp.bfloat16)
             target = jnp.dot(group_ref[...], select, preferred_element_type=F32).astype(jnp.int32)
             shift = (target - group) & (count - 1)
-            value = jnp.exp(scores[pl.ds(pl.multiple_of(block * 128, 128), 128), :] - top)
-            total = total + jnp.sum(value.reshape(16, 8, 128), axis=0)
+            value = jnp.exp(scores[pl.ds(pl.multiple_of(block * LANES, LANES), LANES), :] - top)
+            total = total + jnp.sum(value.reshape(16, 8, LANES), axis=0)
             turned = [jnp.where(shift == d, value, 0.0) for d in range(count)]
             turned = [turned[0]] + [roll(turned[d], width * d) for d in range(1, count)]
             for source in range(count):
                 line = pick(group, [turned[(g - source) % count] for g in range(count)])
-                at = pl.multiple_of((block * count + source) * 128, 128)
-                weights[pl.ds(at, 128), :] = line
+                at = pl.multiple_of((block * count + source) * LANES, LANES)
+                weights[pl.ds(at, LANES), :] = line
         return total
 
-    total = lax.fori_loop(0, scores.shape[0] // 128 // together, body, jnp.zeros((8, 128), F32))
+    total = lax.fori_loop(0, scores.shape[0] // LANES // together, body, jnp.zeros((8, LANES), F32))
     return across(jnp.sum(total, axis=0, keepdims=True), width, jnp.add)
 
 
 def add_weights(line_ref, flag_ref, weights, hists):
-    assert FLAG_KEYS == 128
-
     def add(hist, row, lane, key, count):
         at = [line_ref[row, lane + k] for k in range(count)]
         sums = [hist[pl.ds(at[k], 1), :] + weights[pl.ds(key + k, 1), :] for k in range(count)]
@@ -199,24 +199,36 @@
             hist[pl.ds(at[k], 1), :] = sums[k]
 
     def body(i, carry):
-        key = i * FLAG_KEYS
-
-        def apart():
-            for b in range(FLAG_KEYS // BATCH_KEYS):
-                add(hists[b % 2], i, b * BATCH_KEYS, key + b * BATCH_KEYS, BATCH_KEYS)
-
-        def one_by_one():
+        first = i * STEP_ROWS
+        groups = [(r, lane) for r in range(STEP_ROWS) for lane in range(0, LANES, FLAG_KEYS)]
+        flags = [flag_ref[first + r, lane] for r, lane in groups]
+
+        def apart(r, lane, count):
+            for b in range(count // BATCH_KEYS):
+                at = lane + b * BATCH_KEYS
+                add(hists[b % 2], first + r, at, (first + r) * LANES + at, BATCH_KEYS)
+
+        def one_by_one(r, lane):
             def step(k, carry):
                 for which in range(2):
-                    add(hists[which], i, 2 * k + which, key + 2 * k + which, 1)
+                    at = lane + 2 * k + which
+                    add(hists[which], first + r, at, (first + r) * LANES + at, 1)
                 return carry
 
             lax.fori_loop(0, FLAG_KEYS // 2, step, 0)
 
-        lax.cond(flag_ref[i, 0] == 0, apart, one_by_one)
+        def all_apart():
+            for r in range(STEP_ROWS):
+                apart(r, 0, LANES)
+
+        def some_apart():
+            for (r, lane), flag in zip(groups, flags):
+                lax.cond(flag == 0, lambda: apart(r, lane, FLAG_KEYS), lambda: one_by_one(r, lane))
+
+        lax.cond(sum(flags) == 0, all_apart, some_apart)
         return carry
 
-    lax.fori_loop(0, weights.shape[0] // FLAG_KEYS, body, 0)
+    lax.fori_loop(0, weights.shape[0] // LANES // STEP_ROWS, body, 0)
 
 
 def piece_at(k, size):
@@ -228,7 +240,7 @@
 
 
 def head_block(top, total):
-    row = lax.broadcasted_iota(jnp.int32, (HEAD, 128), 0)
+    row = lax.broadcasted_iota(jnp.int32, (HEAD, LANES), 0)
     return jnp.where(row == 0, top, jnp.where(row == 1, total, 0.0))
 
 
@@ -265,19 +277,19 @@
             values = []
             for u in range(together):
                 block = i * together + u
-                near = pl.ds(pl.multiple_of(base * 2 * piece + block * 256, 128), 128)
-                far = pl.ds(pl.multiple_of(base * 2 * piece + block * 256 + 128, 128), 128)
+                near = pl.ds(pl.multiple_of(base * 2 * piece + block * 256, LANES), LANES)
+                far = pl.ds(pl.multiple_of(base * 2 * piece + block * 256 + LANES, LANES), LANES)
                 low = even[near, :] + odd[near, :]
                 high = roll(even[far, :] + odd[far, :], 32)
                 values.append((block, low, high))
             for block, low, high in values:
-                weights[pl.ds(pl.multiple_of(base * piece + block * 128, 128), 128), :] = jnp.where(quad, low, high)
-                even[pl.ds(pl.multiple_of(base * 2 * piece + block * 128, 128), 128), :] = jnp.where(quad, high, low)
+                weights[pl.ds(pl.multiple_of(base * piece + block * LANES, LANES), LANES), :] = jnp.where(quad, low, high)
+                even[pl.ds(pl.multiple_of(base * 2 * piece + block * LANES, LANES), LANES), :] = jnp.where(quad, high, low)
             return carry
 
-        lax.fori_loop(0, piece // 128 // together, split, 0)
-        firsts = weights.at[pl.ds(pl.multiple_of(base * piece, 128), piece)]
-        seconds = even.at[pl.ds(pl.multiple_of(base * 2 * piece, 128), piece)]
+        lax.fori_loop(0, piece // LANES // together, split, 0)
+        firsts = weights.at[pl.ds(pl.multiple_of(base * piece, LANES), piece)]
+        seconds = even.at[pl.ds(pl.multiple_of(base * 2 * piece, LANES), piece)]
         for c, source in enumerate((firsts, seconds)):
             out = outs[k * 2 + c]
             sends.append(pltpu.make_async_copy(source, out.at[pl.ds(0, piece)], out_sem.at[c, k]))
@@ -317,7 +329,7 @@
     new_top = jnp.maximum(top, old_top)
     scale, old_scale = jnp.exp(top - new_top), jnp.exp(old_top - new_top)
     heads[0] = head_block(new_top, total * scale + old_total * old_scale)
-    step = 128
+    step = LANES
     sends = []
     for k in range(4):
         base = piece_at(k, piece)
@@ -342,10 +354,10 @@
     own = not prevs
     rows = sum(part.shape[-2] for part in parts)
     lines = vocab // (2 if own else PACK)
-    out = jax.ShapeDtypeStruct((vocab // PACK // 4 + HEAD, 128), F32)
+    out = jax.ShapeDtypeStruct((vocab // PACK // 4 + HEAD, LANES), F32)
     keys = tok.shape[0]
-    tok = tok.reshape(128, 128)
-    assert keys == 128 * 128
+    tok = tok.reshape(LANES, LANES)
+    assert keys == LANES * LANES
     count = 8 if own else 4
     dma = pltpu.SemaphoreType.DMA
     extra = [] if own else [*prevs, after]
@@ -355,11 +367,11 @@
         in_specs=[pl.BlockSpec(memory_space=VMEM)]
         + [pl.BlockSpec(memory_space=ANY)] * (len(parts) + len(extra)),
         out_specs=(pl.BlockSpec(memory_space=ANY),) * count,
-        scratch_shapes=[VMEM((128, 128), jnp.bfloat16), VMEM((2, 128, 128), jnp.int32)]
-        + [SMEM((128, 128), jnp.int32), SMEM((128, 128), jnp.int32), dma((2,))]
-        + [VMEM((rows, 128), F32), VMEM((keys, 128), F32), VMEM((lines, 128), F32), VMEM((lines, 128), F32)]
-        + [VMEM((2, HEAD, 128), F32), dma((len(parts),))]
-        + ([dma((2, 4)), dma((2, 4))] if own else [VMEM((4, lines // 4 + HEAD, 128), F32), dma((4,)), dma((4,)), dma((4,))]),
+        scratch_shapes=[VMEM((LANES, LANES), jnp.bfloat16), VMEM((2, LANES, LANES), jnp.int32)]
+        + [SMEM((LANES, LANES), jnp.int32), SMEM((LANES, LANES), jnp.int32), dma((2,))]
+        + [VMEM((rows, LANES), F32), VMEM((keys, LANES), F32), VMEM((lines, LANES), F32), VMEM((lines, LANES), F32)]
+        + [VMEM((2, HEAD, LANES), F32), dma((len(parts),))]
+        + ([dma((2, 4)), dma((2, 4))] if own else [VMEM((4, lines // 4 + HEAD, LANES), F32), dma((4,)), dma((4,)), dma((4,))]),
         compiler_params=pltpu.CompilerParams(vmem_limit_bytes=VMEM_BYTES),
         cost_estimate=pl.CostEstimate(flops=10**6, bytes_accessed=2 * 10**7, transcendentals=0),
         name="own_histogram" if own else "chunk_histogram",
@@ -417,10 +429,10 @@
     dma = pltpu.SemaphoreType.DMA
     return pl.pallas_call(
         merge_kernel,
-        out_shape=tuple(jax.ShapeDtypeStruct((size, 128), F32) for size in sizes),
+        out_shape=tuple(jax.ShapeDtypeStruct((size, LANES), F32) for size in sizes),
         in_specs=[pl.BlockSpec(memory_space=ANY)] * 2,
         out_specs=tuple(pl.BlockSpec(memory_space=ANY) for _ in sizes),
-        scratch_shapes=[VMEM(a.shape, F32), VMEM(a.shape, F32), VMEM((HEAD, 128), F32), dma((2, steps + 1)), dma((steps + 1,))],
+        scratch_shapes=[VMEM(a.shape, F32), VMEM(a.shape, F32), VMEM((HEAD, LANES), F32), dma((2, steps + 1)), dma((steps + 1,))],
         compiler_params=pltpu.CompilerParams(vmem_limit_bytes=VMEM_BYTES),
         cost_estimate=pl.CostEstimate(flops=10**5, bytes_accessed=3 * a.size * 4, transcendentals=0),
         name="merge",
@@ -457,14 +469,14 @@
     return pl.pallas_call(
         head_kernel,
         grid=(cols // block,),
-        out_shape=(jax.ShapeDtypeStruct((count, cols), F32), jax.ShapeDtypeStruct((2, count, 128), F32)),
+        out_shape=(jax.ShapeDtypeStruct((count, cols), F32), jax.ShapeDtypeStruct((2, count, LANES), F32)),
         in_specs=[
             pl.BlockSpec((2 * count, width), lambda i: (0, 0)),
             pl.BlockSpec((width, block), lambda i: (0, i)),
             pl.BlockSpec(memory_space=ANY),
         ],
-        out_specs=(pl.BlockSpec((count, block), lambda i: (0, i)), pl.BlockSpec((2, count, 128), lambda i: (0, 0, 0))),
-        scratch_shapes=[VMEM((count, 128), F32), VMEM((count, 128), F32)],
+        out_specs=(pl.BlockSpec((count, block), lambda i: (0, i)), pl.BlockSpec((2, count, LANES), lambda i: (0, 0, 0))),
+        scratch_shapes=[VMEM((count, LANES), F32), VMEM((count, LANES), F32)],
         compiler_params=pltpu.CompilerParams(vmem_limit_bytes=VMEM_BYTES),
         cost_estimate=pl.CostEstimate(flops=2 * count * width * cols, bytes_accessed=2 * width * cols, transcendentals=0),
         name="head",
@@ -544,7 +556,7 @@
         in_specs=[pl.BlockSpec(memory_space=SMEM), pl.BlockSpec(memory_space=VMEM)]
         + [pl.BlockSpec(memory_space=ANY)] * (1 + len(pieces) + n_prev),
         out_specs=pl.BlockSpec(memory_space=ANY),
-        scratch_shapes=[VMEM((3, lines, 128), F32), VMEM((3, HEAD, 128), F32), VMEM((32, cols), F32), VMEM((32, cols), F32)]
+        scratch_shapes=[VMEM((3, lines, LANES), F32), VMEM((3, HEAD, LANES), F32), VMEM((32, cols), F32), VMEM((32, cols), F32)]
         + [dma((steps, 3)), dma((3,)), dma((steps,)), dma((steps,))],
         input_output_aliases={3 + len(pieces): 0} if n_prev else {},
         compiler_params=pltpu.CompilerParams(vmem_limit_bytes=VMEM_BYTES),
@@ -553,7 +565,7 @@
     )(mix, stat, logits, *pieces, *([prev] if n_prev else []))
 
 
-CHUNKS = (5120, 11264)
+CHUNKS = (6144, 10240)
 
 
 def solution(mesh):

time: 279 us -> 263 us (0.943)
  waiting for transfers between devices: 72.9 us -> 62.8 us
  starting transfers between devices: 21.8 us -> 16.6 us
    ppermute x4, waiting for transfers between devices: 37.2 us -> 26.6 us  [swap_y(): return lax.ppermute(value, 'store', across_y)]
    ppermute x4, starting transfers between devices: 10.2 us -> 7.28 us  [swap_x(): return lax.ppermute(value, 'model', across_x)]
  transfers between devices with their start and end apart: 13 -> 13, of which waited for: 6 -> 7; matrix products, arithmetic and copies ran while one was open for 1% -> 1% of each run, Pallas kernels for 31% -> 37%
where the time goes in v4:
time: 263 us; the launch traced here: 262 us
  Pallas kernels  178 us (68%)
  waiting for transfers between devices  62.8 us (24%)
  starting transfers between devices  16.6 us (6%)
    pallas_call x3, Pallas kernels, histogram_call(): pl.pallas_call(functools.partial(own_kernel if own else chunk_kernel, whi...  89.7 us
    pallas_call x2, Pallas kernels, score_call(): pl.pallas_call(score_kernel, grid=(count // KEY_BLOCK,), out_shape=(jax.S...  47 us
    ppermute x4, waiting for transfers between devices, swap_x(): return lax.ppermute(value, 'model', across_x)  33.2 us
    ppermute x4, waiting for transfers between devices, swap_y(): return lax.ppermute(value, 'store', across_y)  26.6 us
    pallas_call x1, Pallas kernels, head_call(): pl.pallas_call(head_kernel, grid=(cols // block,), out_shape=(jax.ShapeDt...  25.7 us
    pallas_call x2, Pallas kernels, mix_call(): pl.pallas_call(functools.partial(mix_kernel, index, len(pieces) - 2, n_pr...  10.4 us
    ppermute x4, starting transfers between devices, swap_y(): return lax.ppermute(value, 'store', across_y)  7.88 us
    ppermute x4, starting transfers between devices, swap_x(): return lax.ppermute(value, 'model', across_x)  7.28 us
  transfers between devices with their start and end apart: 13, of which 7 were waited for; matrix products, arithmetic and copies ran while one was open for 1% of the time, Pallas kernels for 37%

profile of v4, /device:TPU:0, one launch (start us, length us, event | category | flops | bytes accessed | tf_op | source)
XLA Modules:
  0.0 262.0 jit_solution(15474971875963783128)
XLA Ops:
  0.7 18.4 %scores.2 = (f32[3072,128]{1,0:T(8,128)}, f32[2,1536,128]{2,1,0:T(8,128)}) custom-call(f32[1]{0:T(128)} %bitcast.4.tau_ref, bf16[128,2560]{1,0:T(8,128)(2,1)} %q_ref.1, bf16[16384,2560]{1,0:T(8,128)(2,1)} %k_ref.3), custom_call_target="tpu_custom_call" | custom-call | flops 4026531840 | bytes 31457280 | tf_op jit(solution)/shard_map/scores/pallas_call | solution.py:85
  19.1 3.3 %collective-permute-start.1 = (f32[2,1536,128]{2,1,0:T(8,128)}, f32[2,1536,128]{2,1,0:T(8,128)}, u32[]{:S(2)}, u32[]{:S(2)}) collective-permute-start(f32[2,1536,128]{2,1,0:T(8,128)} %get-tuple-element.30), channel_id=1, source_target_pairs={{0,4},{4,0},{1,5},{5,1},{2,6},{6,2},{3,7},{7,3}} | collective-permute-start | bytes 4718600 | tf_op jit(solution)/shard_map/ppermute | solution.py:581
  22.4 0.0 copy-start.2
  22.4 28.6 %scores.3 = (f32[5120,128]{1,0:T(8,128)}, f32[2560,128]{1,0:T(8,128)}, f32[2560,128]{1,0:T(8,128)}) custom-call(f32[1]{0:T(128)} %bitcast.5.tau_ref, bf16[128,2560]{1,0:T(8,128)(2,1)} %q_ref.1, bf16[16384,2560]{1,0:T(8,128)(2,1)} %k_ref.3), custom_call_target="tpu_custom_call" | custom-call | flops 6710886400 | bytes 52428800 | tf_op jit(solution)/shard_map/scores/pallas_call | solution.py:85
  51.0 0.0 collective-permute-start.3
  51.0 0.0 copy-done.2
  51.0 2.0 collective-permute-start
  53.0 32.7 %own_histogram.1 = (f32[3208,128]{1,0:T(8,128)}, f32[3208,128]{1,0:T(8,128)}, f32[3208,128]{1,0:T(8,128)}, f32[3208,128]{1,0:T(8,128)}, f32[3208,128]{1,0:T(8,12...) custom-call(s32[128,128]{1,0:T(8,128)} %bitcast.10, f32[3072,128]{1,0:T(8,128)} %get-tuple-element.32.refs_0_, ...), custom_call_target="tpu_custom_call" | custom-call | flops 1000000 | bytes 20000000 | tf_op jit(solution)/shard_map/own_histogram/pallas_call | solution.py:364
  85.8 0.7 collective-permute-done
  86.5 0.0 copy-start.1
  86.5 0.0 collective-permute-done.3.refs_1_
  86.5 0.0 collective-permute-done.1.refs_0_
  86.5 0.6 copy-done.1
  87.1 28.5 %chunk_histogram.2 = (f32[3208,128]{1,0:T(8,128)}, f32[3208,128]{1,0:T(8,128)}, f32[3208,128]{1,0:T(8,128)}, f32[3208,128]{1,0:T(8,128)}) custom-call(s32[128,128]{1,0:T(8,128)} %bitcast.8, f32[2,1536,128]{2,1,0:T(8,128)} %collective-permute-done.1.refs_0_, f32[2560,128]{1,0:T(8,128)} %collective-permute-done.3.refs_1_, ...), custom_call_target="tpu_custom_call" | custom-call | flops 1000000 | bytes 20000000 | tf_op jit(solution)/shard_map/chunk_histogram/pallas_call | solution.py:364
  115.7 0.3 collective-permute-start.4
  116.0 2.5 collective-permute-start.2
  118.5 1.1 collective-permute-done.4.b_ref
  119.6 2.8 %merge.2.refs_6_ = f32[3208,128]{1,0:T(8,128)} custom-call(f32[3208,128]{1,0:T(8,128)} %get-tuple-element.43.a_ref, f32[3208,128]{1,0:T(8,128)} %collective-permute-done.4.b_ref), custom_call_target="tpu_custom_call" | custom-call | flops 100000 | bytes 4927488 | tf_op jit(solution)/shard_map/merge/pallas_call | solution.py:430
  122.4 25.9 %collective-permute-done.2.refs_1_ = f32[2560,128]{1,0:T(8,128)} collective-permute-done((f32[2560,128]{1,0:T(8,128)}, f32[2560,128]{1,0:T(8,128)}, u32[]{:S(2)}, u32[]{:S(2)}) %collective-permute-start.2) | collective-permute-done | bytes 1310752 | tf_op jit(solution)/shard_map/ppermute | solution.py:581
  148.2 28.4 %chunk_histogram.3 = (f32[3208,128]{1,0:T(8,128)}, f32[3208,128]{1,0:T(8,128)}, f32[3208,128]{1,0:T(8,128)}, f32[3208,128]{1,0:T(8,128)}) custom-call(s32[128,128]{1,0:T(8,128)} %bitcast.9, f32[2,1536,128]{2,1,0:T(8,128)} %collective-permute-done.1.refs_0_, f32[2560,128]{1,0:T(8,128)} %collective-permute-done.2.refs_1_, ...), custom_call_target="tpu_custom_call" | custom-call | flops 1000000 | bytes 20000000 | tf_op jit(solution)/shard_map/chunk_histogram/pallas_call | solution.py:364
  176.7 0.8 collective-permute-start.5
  177.5 0.0 collective-permute-start.11
  177.6 2.7 %collective-permute-start.12 = (f32[3208,128]{1,0:T(8,128)}, f32[3208,128]{1,0:T(8,128)}, u32[]{:S(2)}, u32[]{:S(2)}) collective-permute-start(f32[3208,128]{1,0:T(8,128)} %merge.2.refs_6_), channel_id=1, source_target_pairs={{0,2},{2,0},{1,3},{3,1},{4,6},{6,4},{5,7},{7,5}} | collective-permute-start | bytes 4927496 | tf_op jit(solution)/shard_map/ppermute | solution.py:587
  180.3 0.2 collective-permute-start.8
  180.5 0.5 collective-permute-done.5.b_ref
  181.0 2.8 %merge.3 = (f32[2560,128]{1,0:T(8,128)}, f32[648,128]{1,0:T(8,128)}) custom-call(f32[3208,128]{1,0:T(8,128)} %get-tuple-element.45.a_ref, f32[3208,128]{1,0:T(8,128)} %collective-permute-done.5.b_ref), custom_call_target="tpu_custom_call" | custom-call | flops 100000 | bytes 4927488 | tf_op jit(solution)/shard_map/merge/pallas_call | solution.py:430
  183.8 0.0 copy-start.3
  183.8 2.7 %collective-permute-start.9 = (f32[2560,128]{1,0:T(8,128)}, f32[2560,128]{1,0:T(8,128)}, u32[]{:S(2)}, u32[]{:S(2)}) collective-permute-start(f32[2560,128]{1,0:T(8,128)} %get-tuple-element.47.after_ref), channel_id=1, source_target_pairs={{0,2},{2,0},{1,3},{3,1},{4,6},{6,4},{5,7},{7,5}} | collective-permute-start | bytes 3932168 | tf_op jit(solution)/shard_map/ppermute | solution.py:587
  186.6 25.7 %head.1 = (f32[64,12800]{1,0:T(8,128)}, f32[2,64,128]{2,1,0:T(8,128)}) custom-call(bf16[128,2560]{1,0:T(8,128)(2,1)} %q_ref.1, bf16[2560,12800]{1,0:T(8,128)(2,1)} %w_ref.1, f32[2560,128]{1,0:T(8,128)} %get-tuple-element.47.after_ref), custom_call_target="tpu_custom_call" | custom-call | flops 4194304000 | bytes 65536000 | tf_op jit(solution)/shard_map/head/pallas_call | solution.py:469
  212.2 0.1 collective-permute-start.6
  212.3 1.4 collective-permute-done.6
  213.7 0.8 fusion.1
  214.5 0.1 collective-permute-start.7
  215.3 31.2 %collective-permute-done.7 = f32[2,64,128]{2,1,0:T(8,128)S(1)} collective-permute-done((f32[2,64,128]{2,1,0:T(8,128)S(1)}, f32[2,64,128]{2,1,0:T(8,128)S(1)}, u32[]{:S(2)}, u32[]{:S(2)}) %collective-permute-start.7) | collective-permute-done | bytes 65568 | tf_op jit(solution)/shard_map/ppermute | solution.py:587
  246.5 0.0 copy-done.3
  246.5 1.7 collective-permute-start.10
  248.3 0.6 pad_maximum_fusion.1.stat_ref
  248.9 0.0 collective-permute-done.11.refs_1_
  248.9 0.0 collective-permute-done.12.refs_2_
  248.9 5.2 %mix.2.refs_4_ = f32[64,12800]{1,0:T(8,128)} custom-call(f32[1]{0:T(128)} %bitcast.6.mix_ref, f32[2,64,128]{2,1,0:T(8,128)} %pad_maximum_fusion.1.stat_ref, f32[64,12800]{1,0:T(8,128)} %get-tuple-element.49.logits_ref, f32[3208,128]{1,0:T(8,128)} %get-tuple-element.53.refs_0_, f32[3208,128]{1,0:T(8,128)} %collective-permute-done.11.refs_1_, ...), custom_call_target="tpu_custom_call" | custom-call | flops 100000 | bytes 8000000 | tf_op jit(solution)/shard_map/mix/pallas_call | solution.py:553
  254.1 0.0 collective-permute-done.8.refs_1_
  254.1 2.0 collective-permute-done.10.refs_3_
  256.1 0.0 copy-start
  256.1 0.0 collective-permute-done.9.refs_2_
  256.1 0.7 copy-done
  256.8 5.2 %mix.3 = f32[64,12800]{1,0:T(8,128)} custom-call(f32[1]{0:T(128)} %bitcast.7.mix_ref, f32[2,64,128]{2,1,0:T(8,128)} %pad_maximum_fusion.1.stat_ref, f32[64,12800]{1,0:T(8,128)} %get-tuple-element.49.logits_ref, f32[3208,128]{1,0:T(8,128)} %get-tuple-element.50.refs_0_, f32[3208,128]{1,0:T(8,128)} %collective-permute-done.8.refs_1_, ...), custom_call_target="tpu_custom_call", output_to_operand_aliasing={{}: (7, {})} | custom-call | flops 100000 | bytes 8000000 | tf_op jit(solution)/shard_map/mix/pallas_call | solution.py:553
  (2 shorter events, 0.0 us)
Async XLA Ops:
  19.1 67.4 %collective-permute-start.1 = (f32[2,1536,128]{2,1,0:T(8,128)}, f32[2,1536,128]{2,1,0:T(8,128)}, u32[]{:S(2)}, u32[]{:S(2)}) collective-permute-start(f32[2,1536,128]{2,1,0:T(8,128)} %get-tuple-element.30), channel_id=1, source_target_pairs={{0,4},{4,0},{1,5},{5,1},{2,6},{6,2},{3,7},{7,3}} | collective-permute-start | bytes 4718600 | tf_op jit(solution)/shard_map/ppermute | solution.py:581
  22.4 28.6 %copy-start.2 = (s32[16384]{0:T(1024)S(1)}, s32[16384]{0:T(1024)}, u32[]{:S(2)}) copy-start(s32[16384]{0:T(1024)} %param.9) | copy-start | bytes 196612
  51.0 35.5 %collective-permute-start.3 = (f32[2560,128]{1,0:T(8,128)}, f32[2560,128]{1,0:T(8,128)}, u32[]{:S(2)}, u32[]{:S(2)}) collective-permute-start(f32[2560,128]{1,0:T(8,128)} %get-tuple-element.38), channel_id=1, source_target_pairs={{0,4},{4,0},{1,5},{5,1},{2,6},{6,2},{3,7},{7,3}} | collective-permute-start | bytes 3932168 | tf_op jit(solution)/shard_map/ppermute | solution.py:581
  51.0 35.5 %collective-permute-start = (s32[16384]{0:T(1024)S(1)}, s32[16384]{0:T(1024)S(1)}, u32[]{:S(2)}, u32[]{:S(2)}) collective-permute-start(s32[16384]{0:T(1024)S(1)} %copy-done.2), channel_id=1, source_target_pairs={{0,4},{4,0},{1,5},{5,1},{2,6},{6,2},{3,7},{7,3}} | collective-permute-start | bytes 196616 | tf_op jit(solution)/shard_map/ppermute | solution.py:581
  86.5 0.6 copy-start.1
  115.7 3.9 %collective-permute-start.4 = (f32[3208,128]{1,0:T(8,128)}, f32[3208,128]{1,0:T(8,128)}, u32[]{:S(2)}, u32[]{:S(2)}) collective-permute-start(f32[3208,128]{1,0:T(8,128)} %get-tuple-element.44), channel_id=1, source_target_pairs={{0,1},{1,0},{2,3},{3,2},{4,5},{5,4},{6,7},{7,6}} | collective-permute-start | bytes 4927496 | tf_op jit(solution)/shard_map/ppermute | solution.py:584
  116.0 32.3 %collective-permute-start.2 = (f32[2560,128]{1,0:T(8,128)}, f32[2560,128]{1,0:T(8,128)}, u32[]{:S(2)}, u32[]{:S(2)}) collective-permute-start(f32[2560,128]{1,0:T(8,128)} %get-tuple-element.31), channel_id=1, source_target_pairs={{0,4},{4,0},{1,5},{5,1},{2,6},{6,2},{3,7},{7,3}} | collective-permute-start | bytes 3932168 | tf_op jit(solution)/shard_map/ppermute | solution.py:581
  176.7 4.3 %collective-permute-start.5 = (f32[3208,128]{1,0:T(8,128)}, f32[3208,128]{1,0:T(8,128)}, u32[]{:S(2)}, u32[]{:S(2)}) collective-permute-start(f32[3208,128]{1,0:T(8,128)} %get-tuple-element.46), channel_id=1, source_target_pairs={{0,1},{1,0},{2,3},{3,2},{4,5},{5,4},{6,7},{7,6}} | collective-permute-start | bytes 4927496 | tf_op jit(solution)/shard_map/ppermute | solution.py:584
  177.5 71.4 %collective-permute-start.11 = (f32[3208,128]{1,0:T(8,128)}, f32[3208,128]{1,0:T(8,128)}, u32[]{:S(2)}, u32[]{:S(2)}) collective-permute-start(f32[3208,128]{1,0:T(8,128)} %get-tuple-element.54), channel_id=1, source_target_pairs={{0,1},{1,0},{2,3},{3,2},{4,5},{5,4},{6,7},{7,6}} | collective-permute-start | bytes 4927496 | tf_op jit(solution)/shard_map/ppermute | solution.py:584
  177.6 71.4 %collective-permute-start.12 = (f32[3208,128]{1,0:T(8,128)}, f32[3208,128]{1,0:T(8,128)}, u32[]{:S(2)}, u32[]{:S(2)}) collective-permute-start(f32[3208,128]{1,0:T(8,128)} %merge.2.refs_6_), channel_id=1, source_target_pairs={{0,2},{2,0},{1,3},{3,1},{4,6},{6,4},{5,7},{7,5}} | collective-permute-start | bytes 4927496 | tf_op jit(solution)/shard_map/ppermute | solution.py:587
  180.3 73.9 %collective-permute-start.8 = (f32[3208,128]{1,0:T(8,128)}, f32[3208,128]{1,0:T(8,128)}, u32[]{:S(2)}, u32[]{:S(2)}) collective-permute-start(f32[3208,128]{1,0:T(8,128)} %get-tuple-element.51), channel_id=1, source_target_pairs={{0,1},{1,0},{2,3},{3,2},{4,5},{5,4},{6,7},{7,6}} | collective-permute-start | bytes 4927496 | tf_op jit(solution)/shard_map/ppermute | solution.py:584
  183.8 62.7 %copy-start.3 = (f32[648,128]{1,0:T(8,128)S(1)}, f32[648,128]{1,0:T(8,128)}, u32[]{:S(2)}) copy-start(f32[648,128]{1,0:T(8,128)} %get-tuple-element.52) | copy-start | bytes 995332
  183.8 72.3 %collective-permute-start.9 = (f32[2560,128]{1,0:T(8,128)}, f32[2560,128]{1,0:T(8,128)}, u32[]{:S(2)}, u32[]{:S(2)}) collective-permute-start(f32[2560,128]{1,0:T(8,128)} %get-tuple-element.47.after_ref), channel_id=1, source_target_pairs={{0,2},{2,0},{1,3},{3,1},{4,6},{6,4},{5,7},{7,5}} | collective-permute-start | bytes 3932168 | tf_op jit(solution)/shard_map/ppermute | solution.py:587
  212.2 1.5 collective-permute-start.6
  214.5 32.0 %collective-permute-start.7 = (f32[2,64,128]{2,1,0:T(8,128)S(1)}, f32[2,64,128]{2,1,0:T(8,128)S(1)}, u32[]{:S(2)}, u32[]{:S(2)}) collective-permute-start(f32[2,64,128]{2,1,0:T(8,128)S(1)} %pad_maximum_fusion), channel_id=1, source_target_pairs={{0,2},{2,0},{1,3},{3,1},{4,6},{6,4},{5,7},{7,5}} | collective-permute-start | bytes 196616 | tf_op jit(solution)/shard_map/ppermute | solution.py:587
  246.5 9.6 %collective-permute-start.10 = (f32[648,128]{1,0:T(8,128)S(1)}, f32[648,128]{1,0:T(8,128)S(1)}, u32[]{:S(2)}, u32[]{:S(2)}) collective-permute-start(f32[648,128]{1,0:T(8,128)S(1)} %copy-done.3), channel_id=1, source_target_pairs={{0,2},{2,0},{1,3},{3,1},{4,6},{6,4},{5,7},{7,5}} | collective-permute-start | bytes 995336 | tf_op jit(solution)/shard_map/ppermute | solution.py:587
  256.1 0.7 copy-start

commit v5 on v4

--- a/solution.py
+++ b/solution.py
@@ -14,10 +14,10 @@
 SMEM = pltpu.SMEM
 KEY_BLOCK = 1024
 LANES = 128
-VMEM_BYTES = 63 * 2**20
+VMEM_BYTES = 67043328
 BATCH_KEYS = 8
 FLAG_KEYS = 32
-STEP_ROWS = 2
+STEP_ROWS = 4
 PACK = 4
 TOK_BLOCK = 128
 ORDERS = ((0, 2, 1, 3), (3, 0, 2, 1))
@@ -565,7 +565,7 @@
     )(mix, stat, logits, *pieces, *([prev] if n_prev else []))
 
 
-CHUNKS = (6144, 10240)
+CHUNKS = (5120, 11264)
 
 
 def solution(mesh):

time: 263 us -> 275 us (1.046)
  waiting for transfers between devices: 62.8 us -> 75.7 us
    ppermute x4, waiting for transfers between devices: 26.6 us -> 39.8 us  [swap_y(): return lax.ppermute(value, 'store', across_y)]
  transfers between devices with their start and end apart: 13 -> 13, of which waited for: 7 -> 7; matrix products, arithmetic and copies ran while one was open for 1% -> 1% of each run, Pallas kernels for 37% -> 31%
where the time goes in v5:
time: 275 us; the launch traced here: 274 us
  Pallas kernels  177 us (64%)
  waiting for transfers between devices  75.7 us (28%)
  starting transfers between devices  18.4 us (7%)
    pallas_call x3, Pallas kernels, histogram_call(): pl.pallas_call(functools.partial(own_kernel if own else chunk_kernel, whi...  88.3 us
    pallas_call x2, Pallas kernels, score_call(): pl.pallas_call(score_kernel, grid=(count // KEY_BLOCK,), out_shape=(jax.S...  47.1 us
    ppermute x4, waiting for transfers between devices, swap_y(): return lax.ppermute(value, 'store', across_y)  39.8 us
    ppermute x4, waiting for transfers between devices, swap_x(): return lax.ppermute(value, 'model', across_x)  33.6 us
    pallas_call x1, Pallas kernels, head_call(): pl.pallas_call(head_kernel, grid=(cols // block,), out_shape=(jax.ShapeDt...  25.7 us
    pallas_call x2, Pallas kernels, mix_call(): pl.pallas_call(functools.partial(mix_kernel, index, len(pieces) - 2, n_pr...  10.4 us
    ppermute x4, starting transfers between devices, swap_x(): return lax.ppermute(value, 'model', across_x)  8.15 us
    ppermute x4, starting transfers between devices, swap_y(): return lax.ppermute(value, 'store', across_y)  8.01 us
  transfers between devices with their start and end apart: 13, of which 7 were waited for; matrix products, arithmetic and copies ran while one was open for 1% of the time, Pallas kernels for 31%

profile of v5, /device:TPU:0, one launch (start us, length us, event | category | flops | bytes accessed | tf_op | source)
XLA Modules:
  0.0 274.0 jit_solution(3081521060705303216)
XLA Ops:
  0.7 31.1 %scores.3 = (f32[5632,128]{1,0:T(8,128)}, f32[2816,128]{1,0:T(8,128)}, f32[2816,128]{1,0:T(8,128)}) custom-call(f32[1]{0:T(128)} %bitcast.5.tau_ref, bf16[128,2560]{1,0:T(8,128)(2,1)} %q_ref.1, bf16[16384,2560]{1,0:T(8,128)(2,1)} %k_ref.3), custom_call_target="tpu_custom_call" | custom-call | flops 7381975040 | bytes 57671680 | tf_op jit(solution)/shard_map/scores/pallas_call | solution.py:85
  31.8 3.3 %collective-permute-start.3 = (f32[2816,128]{1,0:T(8,128)}, f32[2816,128]{1,0:T(8,128)}, u32[]{:S(2)}, u32[]{:S(2)}) collective-permute-start(f32[2816,128]{1,0:T(8,128)} %get-tuple-element.38), channel_id=1, source_target_pairs={{0,4},{4,0},{1,5},{5,1},{2,6},{6,2},{3,7},{7,3}} | collective-permute-start | bytes 4325384 | tf_op jit(solution)/shard_map/ppermute | solution.py:581
  35.1 15.9 %scores.2 = (f32[2560,128]{1,0:T(8,128)}, f32[2,1280,128]{2,1,0:T(8,128)}) custom-call(f32[1]{0:T(128)} %bitcast.4.tau_ref, bf16[128,2560]{1,0:T(8,128)(2,1)} %q_ref.1, bf16[16384,2560]{1,0:T(8,128)(2,1)} %k_ref.3), custom_call_target="tpu_custom_call" | custom-call | flops 3355443200 | bytes 26214400 | tf_op jit(solution)/shard_map/scores/pallas_call | solution.py:85
  51.0 0.0 collective-permute-start.1
  51.1 2.0 collective-permute-start
  53.1 32.5 %own_histogram.1 = (f32[3208,128]{1,0:T(8,128)}, f32[3208,128]{1,0:T(8,128)}, f32[3208,128]{1,0:T(8,128)}, f32[3208,128]{1,0:T(8,128)}, f32[3208,128]{1,0:T(8,12...) custom-call(s32[128,128]{1,0:T(8,128)} %bitcast.8, f32[2560,128]{1,0:T(8,128)} %get-tuple-element.32.refs_0_, ...), custom_call_target="tpu_custom_call" | custom-call | flops 1000000 | bytes 20000000 | tf_op jit(solution)/shard_map/own_histogram/pallas_call | solution.py:364
  85.6 10.9 %collective-permute-done = s32[16384]{0:T(1024)} collective-permute-done((s32[16384]{0:T(1024)}, s32[16384]{0:T(1024)}, u32[]{:S(2)}, u32[]{:S(2)}) %collective-permute-start) | collective-permute-done | bytes 65568 | tf_op jit(solution)/shard_map/ppermute | solution.py:581
  96.5 0.0 collective-permute-done.1.refs_0_
  96.5 0.0 collective-permute-done.3.refs_1_
  96.5 28.0 %chunk_histogram.2 = (f32[3208,128]{1,0:T(8,128)}, f32[3208,128]{1,0:T(8,128)}, f32[3208,128]{1,0:T(8,128)}, f32[3208,128]{1,0:T(8,128)}) custom-call(s32[128,128]{1,0:T(8,128)} %bitcast.1.tok_ref, f32[2,1280,128]{2,1,0:T(8,128)} %collective-permute-done.1.refs_0_, f32[2816,128]{1,0:T(8,128)} %collective-permute-done.3.refs_1_, ...), custom_call_target="tpu_custom_call" | custom-call | flops 1000000 | bytes 20000000 | tf_op jit(solution)/shard_map/chunk_histogram/pallas_call | solution.py:364
  124.5 0.7 collective-permute-start.4
  125.1 2.7 collective-permute-start.2
  127.8 0.8 collective-permute-done.4.b_ref
  128.6 2.8 %merge.2.refs_6_ = f32[3208,128]{1,0:T(8,128)} custom-call(f32[3208,128]{1,0:T(8,128)} %get-tuple-element.43.a_ref, f32[3208,128]{1,0:T(8,128)} %collective-permute-done.4.b_ref), custom_call_target="tpu_custom_call" | custom-call | flops 100000 | bytes 4927488 | tf_op jit(solution)/shard_map/merge/pallas_call | solution.py:430
  131.4 28.9 %collective-permute-done.2.refs_1_ = f32[2816,128]{1,0:T(8,128)} collective-permute-done((f32[2816,128]{1,0:T(8,128)}, f32[2816,128]{1,0:T(8,128)}, u32[]{:S(2)}, u32[]{:S(2)}) %collective-permute-start.2) | collective-permute-done | bytes 1441824 | tf_op jit(solution)/shard_map/ppermute | solution.py:581
  160.3 27.8 %chunk_histogram.3 = (f32[3208,128]{1,0:T(8,128)}, f32[3208,128]{1,0:T(8,128)}, f32[3208,128]{1,0:T(8,128)}, f32[3208,128]{1,0:T(8,128)}) custom-call(s32[128,128]{1,0:T(8,128)} %bitcast.1.tok_ref, f32[2,1280,128]{2,1,0:T(8,128)} %collective-permute-done.1.refs_0_, f32[2816,128]{1,0:T(8,128)} %collective-permute-done.2.refs_1_, ...), custom_call_target="tpu_custom_call" | custom-call | flops 1000000 | bytes 20000000 | tf_op jit(solution)/shard_map/chunk_histogram/pallas_call | solution.py:364
  188.2 1.3 collective-permute-start.5
  189.5 0.0 collective-permute-start.11
  189.5 3.2 %collective-permute-start.12 = (f32[3208,128]{1,0:T(8,128)}, f32[3208,128]{1,0:T(8,128)}, u32[]{:S(2)}, u32[]{:S(2)}) collective-permute-start(f32[3208,128]{1,0:T(8,128)} %merge.2.refs_6_), channel_id=1, source_target_pairs={{0,2},{2,0},{1,3},{3,1},{4,6},{6,4},{5,7},{7,5}} | collective-permute-start | bytes 4927496 | tf_op jit(solution)/shard_map/ppermute | solution.py:587
  192.6 0.2 collective-permute-start.8
  192.8 0.1 collective-permute-done.5.b_ref
  192.9 2.8 %merge.3 = (f32[2560,128]{1,0:T(8,128)}, f32[648,128]{1,0:T(8,128)}) custom-call(f32[3208,128]{1,0:T(8,128)} %get-tuple-element.45.a_ref, f32[3208,128]{1,0:T(8,128)} %collective-permute-done.5.b_ref), custom_call_target="tpu_custom_call" | custom-call | flops 100000 | bytes 4927488 | tf_op jit(solution)/shard_map/merge/pallas_call | solution.py:430
  195.7 3.2 %collective-permute-start.9 = (f32[2560,128]{1,0:T(8,128)}, f32[2560,128]{1,0:T(8,128)}, u32[]{:S(2)}, u32[]{:S(2)}) collective-permute-start(f32[2560,128]{1,0:T(8,128)} %get-tuple-element.47.after_ref), channel_id=1, source_target_pairs={{0,2},{2,0},{1,3},{3,1},{4,6},{6,4},{5,7},{7,5}} | collective-permute-start | bytes 3932168 | tf_op jit(solution)/shard_map/ppermute | solution.py:587
  198.9 25.7 %head.1 = (f32[64,12800]{1,0:T(8,128)}, f32[2,64,128]{2,1,0:T(8,128)}) custom-call(bf16[128,2560]{1,0:T(8,128)(2,1)} %q_ref.1, bf16[2560,12800]{1,0:T(8,128)(2,1)} %w_ref.1, f32[2560,128]{1,0:T(8,128)} %get-tuple-element.47.after_ref), custom_call_target="tpu_custom_call" | custom-call | flops 4194304000 | bytes 65536000 | tf_op jit(solution)/shard_map/head/pallas_call | solution.py:469
  224.6 0.1 collective-permute-start.6
  224.7 1.4 collective-permute-done.6
  226.0 0.8 fusion.1
  226.9 0.1 collective-permute-start.7
  227.6 31.3 %collective-permute-done.7 = f32[2,64,128]{2,1,0:T(8,128)S(1)} collective-permute-done((f32[2,64,128]{2,1,0:T(8,128)S(1)}, f32[2,64,128]{2,1,0:T(8,128)S(1)}, u32[]{:S(2)}, u32[]{:S(2)}) %collective-permute-start.7) | collective-permute-done | bytes 65568 | tf_op jit(solution)/shard_map/ppermute | solution.py:587
  258.9 1.7 collective-permute-start.10
  260.6 0.6 pad_maximum_fusion.1.stat_ref
  261.3 0.0 collective-permute-done.11.refs_1_
  261.3 0.0 collective-permute-done.12.refs_2_
  261.3 5.2 %mix.2.refs_4_ = f32[64,12800]{1,0:T(8,128)} custom-call(f32[1]{0:T(128)} %bitcast.6.mix_ref, f32[2,64,128]{2,1,0:T(8,128)} %pad_maximum_fusion.1.stat_ref, f32[64,12800]{1,0:T(8,128)} %get-tuple-element.49.logits_ref, f32[3208,128]{1,0:T(8,128)} %get-tuple-element.53.refs_0_, f32[3208,128]{1,0:T(8,128)} %collective-permute-done.11.refs_1_, ...), custom_call_target="tpu_custom_call" | custom-call | flops 100000 | bytes 8000000 | tf_op jit(solution)/shard_map/mix/pallas_call | solution.py:553
  266.5 0.0 collective-permute-done.8.refs_1_
  266.5 2.3 collective-permute-done.10.refs_3_
  268.8 0.0 collective-permute-done.9.refs_2_
  268.8 5.2 %mix.3 = f32[64,12800]{1,0:T(8,128)} custom-call(f32[1]{0:T(128)} %bitcast.7.mix_ref, f32[2,64,128]{2,1,0:T(8,128)} %pad_maximum_fusion.1.stat_ref, f32[64,12800]{1,0:T(8,128)} %get-tuple-element.49.logits_ref, f32[3208,128]{1,0:T(8,128)} %get-tuple-element.50.refs_0_, f32[3208,128]{1,0:T(8,128)} %collective-permute-done.8.refs_1_, ...), custom_call_target="tpu_custom_call", output_to_operand_aliasing={{}: (7, {})} | custom-call | flops 100000 | bytes 8000000 | tf_op jit(solution)/shard_map/mix/pallas_call | solution.py:553
  (2 shorter events, 0.0 us)
Async XLA Ops:
  31.8 64.7 %collective-permute-start.3 = (f32[2816,128]{1,0:T(8,128)}, f32[2816,128]{1,0:T(8,128)}, u32[]{:S(2)}, u32[]{:S(2)}) collective-permute-start(f32[2816,128]{1,0:T(8,128)} %get-tuple-element.38), channel_id=1, source_target_pairs={{0,4},{4,0},{1,5},{5,1},{2,6},{6,2},{3,7},{7,3}} | collective-permute-start | bytes 4325384 | tf_op jit(solution)/shard_map/ppermute | solution.py:581
  51.0 45.5 %collective-permute-start.1 = (f32[2,1280,128]{2,1,0:T(8,128)}, f32[2,1280,128]{2,1,0:T(8,128)}, u32[]{:S(2)}, u32[]{:S(2)}) collective-permute-start(f32[2,1280,128]{2,1,0:T(8,128)} %get-tuple-element.30), channel_id=1, source_target_pairs={{0,4},{4,0},{1,5},{5,1},{2,6},{6,2},{3,7},{7,3}} | collective-permute-start | bytes 3932168 | tf_op jit(solution)/shard_map/ppermute | solution.py:581
  51.1 45.4 %collective-permute-start = (s32[16384]{0:T(1024)}, s32[16384]{0:T(1024)}, u32[]{:S(2)}, u32[]{:S(2)}) collective-permute-start(s32[16384]{0:T(1024)} %param.9), channel_id=1, source_target_pairs={{0,4},{4,0},{1,5},{5,1},{2,6},{6,2},{3,7},{7,3}} | collective-permute-start | bytes 196616 | tf_op jit(solution)/shard_map/ppermute | solution.py:581
  124.5 4.1 %collective-permute-start.4 = (f32[3208,128]{1,0:T(8,128)}, f32[3208,128]{1,0:T(8,128)}, u32[]{:S(2)}, u32[]{:S(2)}) collective-permute-start(f32[3208,128]{1,0:T(8,128)} %get-tuple-element.44), channel_id=1, source_target_pairs={{0,1},{1,0},{2,3},{3,2},{4,5},{5,4},{6,7},{7,6}} | collective-permute-start | bytes 4927496 | tf_op jit(solution)/shard_map/ppermute | solution.py:584
  125.1 35.2 %collective-permute-start.2 = (f32[2816,128]{1,0:T(8,128)}, f32[2816,128]{1,0:T(8,128)}, u32[]{:S(2)}, u32[]{:S(2)}) collective-permute-start(f32[2816,128]{1,0:T(8,128)} %get-tuple-element.31), channel_id=1, source_target_pairs={{0,4},{4,0},{1,5},{5,1},{2,6},{6,2},{3,7},{7,3}} | collective-permute-start | bytes 4325384 | tf_op jit(solution)/shard_map/ppermute | solution.py:581
  188.2 4.8 %collective-permute-start.5 = (f32[3208,128]{1,0:T(8,128)}, f32[3208,128]{1,0:T(8,128)}, u32[]{:S(2)}, u32[]{:S(2)}) collective-permute-start(f32[3208,128]{1,0:T(8,128)} %get-tuple-element.46), channel_id=1, source_target_pairs={{0,1},{1,0},{2,3},{3,2},{4,5},{5,4},{6,7},{7,6}} | collective-permute-start | bytes 4927496 | tf_op jit(solution)/shard_map/ppermute | solution.py:584
  189.5 71.8 %collective-permute-start.11 = (f32[3208,128]{1,0:T(8,128)}, f32[3208,128]{1,0:T(8,128)}, u32[]{:S(2)}, u32[]{:S(2)}) collective-permute-start(f32[3208,128]{1,0:T(8,128)} %get-tuple-element.54), channel_id=1, source_target_pairs={{0,1},{1,0},{2,3},{3,2},{4,5},{5,4},{6,7},{7,6}} | collective-permute-start | bytes 4927496 | tf_op jit(solution)/shard_map/ppermute | solution.py:584
  189.5 71.8 %collective-permute-start.12 = (f32[3208,128]{1,0:T(8,128)}, f32[3208,128]{1,0:T(8,128)}, u32[]{:S(2)}, u32[]{:S(2)}) collective-permute-start(f32[3208,128]{1,0:T(8,128)} %merge.2.refs_6_), channel_id=1, source_target_pairs={{0,2},{2,0},{1,3},{3,1},{4,6},{6,4},{5,7},{7,5}} | collective-permute-start | bytes 4927496 | tf_op jit(solution)/shard_map/ppermute | solution.py:587
  192.6 73.9 %collective-permute-start.8 = (f32[3208,128]{1,0:T(8,128)}, f32[3208,128]{1,0:T(8,128)}, u32[]{:S(2)}, u32[]{:S(2)}) collective-permute-start(f32[3208,128]{1,0:T(8,128)} %get-tuple-element.51), channel_id=1, source_target_pairs={{0,1},{1,0},{2,3},{3,2},{4,5},{5,4},{6,7},{7,6}} | collective-permute-start | bytes 4927496 | tf_op jit(solution)/shard_map/ppermute | solution.py:584
  195.7 73.1 %collective-permute-start.9 = (f32[2560,128]{1,0:T(8,128)}, f32[2560,128]{1,0:T(8,128)}, u32[]{:S(2)}, u32[]{:S(2)}) collective-permute-start(f32[2560,128]{1,0:T(8,128)} %get-tuple-element.47.after_ref), channel_id=1, source_target_pairs={{0,2},{2,0},{1,3},{3,1},{4,6},{6,4},{5,7},{7,5}} | collective-permute-start | bytes 3932168 | tf_op jit(solution)/shard_map/ppermute | solution.py:587
  224.6 1.5 collective-permute-start.6
  226.9 32.0 %collective-permute-start.7 = (f32[2,64,128]{2,1,0:T(8,128)S(1)}, f32[2,64,128]{2,1,0:T(8,128)S(1)}, u32[]{:S(2)}, u32[]{:S(2)}) collective-permute-start(f32[2,64,128]{2,1,0:T(8,128)S(1)} %pad_maximum_fusion), channel_id=1, source_target_pairs={{0,2},{2,0},{1,3},{3,1},{4,6},{6,4},{5,7},{7,5}} | collective-permute-start | bytes 196616 | tf_op jit(solution)/shard_map/ppermute | solution.py:587
  258.9 9.9 %collective-permute-start.10 = (f32[648,128]{1,0:T(8,128)}, f32[648,128]{1,0:T(8,128)}, u32[]{:S(2)}, u32[]{:S(2)}) collective-permute-start(f32[648,128]{1,0:T(8,128)} %get-tuple-element.52), channel_id=1, source_target_pairs={{0,2},{2,0},{1,3},{3,1},{4,6},{6,4},{5,7},{7,5}} | collective-permute-start | bytes 995336 | tf_op jit(solution)/shard_map/ppermute | solution.py:587
